TPU v7x, 256 devices: a whole 4x4x8 slice. The times are simulated.
256 devices in a mesh: cells: 128 (over y_lo, x, z, core), ens: 2 (over y_hi).
Axes of the slice: x: 4, y: 4 (y_hi: 2, y_lo: 2; y = y_hi * 2 + y_lo), z: 8, core: 2. Of those that a mesh axis runs over, the one named last changes fastest.
Arguments:
- later_adjoint: float32 [4, 4, 256, 8, 128], P('ens', None, 'cells'), may hold values from -6 to 6
- coupling: bfloat16 [4, 6, 4, 4, 256, 8, 128], P('ens', None, None, None, 'cells'), may hold values from -0.59765625 to 0.59765625
- diag_inverse: bfloat16 [4, 4, 4, 256, 8, 128], P('ens', None, None, 'cells'), may hold values from -0.7 to 1.6, as said below
- sensitivity: bfloat16 [4, 4, 256, 8, 128, 128], P('ens', None, 'cells'), may hold values from -0.0625 to 0.0625
- well_cells: int32 [256], replicated, may hold values from 0 to 262143
- well_misfit: float32 [4, 4, 256], P('ens'), may hold values from -6 to 6
- block_map: int32 [256, 8, 128], P('cells'), may hold values from 0 to 511, as said below
Outputs:
- adjoint: float32 [4, 4, 256, 8, 128], P('ens', None, 'cells')
- gradient: float32 [512, 128], P('cells')
Inputs may be any that keep to these rules, and one draw needn't show every extreme that they name: `block_map`: of the cells of each slab of 2 planes along the first dimension (x from i * 2 to i * 2 + 1), exactly 16 map to blocks whose number divided by 4 (rounded down) equals any given j. `diag_inverse`: each block is the inverse of a diagonal block; its diagonal entries lie in 0.4 to 1.6. `well_cells`: wells may share a cell.
All inputs are finite; a program needn't handle non-finite values.
Results may differ from a plain program's by a relative error of at most 0.0003.
Values sent between devices are 32-bit elements; how exact they have to be, the bound alone decides.
No kernel may reach another device: no remote copies, remote signals or barrier semaphores. Data moves between devices by JAX's collectives and lax.ppermute only.
A program may use at most 64 MiB of HBM per device.

v0:
```python
import jax
import jax.numpy as jnp
from jax import lax
from jax.sharding import PartitionSpec as P

ITERS = 4
BLK_DEV = 4


def from_behind(value, axis, by):
    devices = lax.axis_size(axis)
    pairs = [(i, i + by) for i in range(devices) if 0 <= i + by < devices]
    return lax.ppermute(value, axis, pairs)


def move_along(field, axis, forward):
    length = field.shape[axis]
    shape = list(field.shape)
    shape[axis] = 1
    zeros = jnp.zeros(shape, jnp.float32)
    if forward:
        return jnp.concatenate(
            [zeros, lax.slice_in_dim(field, 0, length - 1, axis=axis)], axis=axis
        )
    return jnp.concatenate([lax.slice_in_dim(field, 1, length, axis=axis), zeros], axis=axis)


def coupling_sum(adjoint, coupling):
    terms = jnp.sum(coupling.astype(jnp.float32) * adjoint[:, None, :, None], axis=2)
    upward = terms[:, 0]
    downward = terms[:, 1]
    planes = upward.shape[2]
    from_below = from_behind(upward[:, :, planes - 1 :], "cells", 1)
    from_above = from_behind(downward[:, :, :1], "cells", -1)
    total = jnp.concatenate([from_below, upward[:, :, : planes - 1]], axis=2)
    total = total + jnp.concatenate([downward[:, :, 1:], from_above], axis=2)
    total = total + move_along(terms[:, 2], 3, True) + move_along(terms[:, 3], 3, False)
    total = total + move_along(terms[:, 4], 4, True) + move_along(terms[:, 5], 4, False)
    return total


def apply_inverse(diag_inverse, source):
    return jnp.sum(diag_inverse.astype(jnp.float32) * source[:, :, None], axis=1)


def body(later_adjoint, coupling, diag_inverse, sensitivity, well_cells, well_misfit, block_map):
    members, unknowns, planes, columns, layers = later_adjoint.shape
    count = planes * columns * layers
    ranks = lax.axis_size("cells")
    first_cell = lax.axis_index("cells") * count
    cell_ids = first_cell + jnp.arange(count, dtype=jnp.int32)
    onehot = (well_cells[:, None] == cell_ids[None, :]).astype(jnp.float32)
    injected = jnp.dot(
        well_misfit.reshape(members * unknowns, -1),
        onehot,
        precision=lax.Precision.HIGHEST,
        preferred_element_type=jnp.float32,
    )
    source = later_adjoint + injected.reshape(later_adjoint.shape)
    adjoint = apply_inverse(diag_inverse, source)
    for sweep in range(ITERS):
        adjoint = apply_inverse(diag_inverse, source - coupling_sum(adjoint, coupling))
    params = sensitivity.shape[-1]
    adjoint_flat = adjoint.reshape(members, unknowns, count)
    sens_flat = sensitivity.reshape(members, unknowns, count, params)
    cell_grad = jnp.sum(adjoint_flat[..., None] * sens_flat.astype(jnp.float32), axis=(0, 1))
    flat_map = block_map.reshape(-1)
    owner = flat_map // BLK_DEV
    order = jnp.argsort(owner, stable=True)
    per_owner = count // ranks
    send_rows = cell_grad[order].reshape(ranks, per_owner, params)
    send_ids = (flat_map[order] % BLK_DEV).astype(jnp.float32).reshape(ranks, per_owner)
    got_rows, got_ids = (
        lax.all_to_all(send_rows, "cells", split_axis=0, concat_axis=0, tiled=True),
        lax.all_to_all(send_ids, "cells", split_axis=0, concat_axis=0, tiled=True),
    )
    owned = jax.ops.segment_sum(
        got_rows.reshape(-1, params), got_ids.reshape(-1).astype(jnp.int32), num_segments=BLK_DEV
    )
    gradient = lax.psum(owned, "ens")
    return (adjoint, gradient)


def solution(mesh):
    placed = (
        P("ens", None, "cells", None, None),
        P("ens", None, None, None, "cells", None, None),
        P("ens", None, None, "cells", None, None),
        P("ens", None, "cells", None, None, None),
        P(),
        P("ens", None, None),
        P("cells", None, None),
    )
    return jax.shard_map(
        body,
        mesh=mesh,
        in_specs=placed,
        out_specs=(P("ens", None, "cells", None, None), P("cells", None)),
        check_vma=False,
    )
```

profile of v0, /device:TPU:16, one launch (start us, length us, event | category | flops | bytes accessed | tf_op | source)
XLA Modules:
  0.0 148.1 jit_solution(6212600087634903519)
XLA Ops:
  0.7 0.8 reshape.110
  1.4 1.4 fusion.6
  2.9 0.9 add.130
  3.7 0.9 fusion.11
  4.7 0.2 fusion.2
  4.9 1.3 collective-permute-start.1
  6.3 3.0 %collective-permute-start = (f32[2,4,1,8,128]{4,3,2,1,0:T(8,128)S(1)}, f32[2,4,1,8,128]{4,3,2,1,0:T(8,128)S(1)}, u32[]{:S(2)}, u32[]{:S(2)}) collective-permute-start(f32[2,4,1,8,128]{4,3,2,1,0:T(8,128)S(1)} %get-tuple-element.42), channel_id=1, source_target_pairs={{0,2},{2,4},{4,6},{6,8},{8,10},{10,12},{12,14},{14,16},{16,18},{18... | collective-permute-start | bytes 98312 | tf_op jit(solution)/shard_map/ppermute | solution.py:13
  9.4 0.7 collective-permute-done
  10.1 0.1 fusion.20
  10.3 0.2 fusion.3
  10.5 1.3 collective-permute-start.3
  11.8 4.2 %collective-permute-start.2 = (f32[2,4,1,8,128]{4,3,2,1,0:T(8,128)S(1)}, f32[2,4,1,8,128]{4,3,2,1,0:T(8,128)S(1)}, u32[]{:S(2)}, u32[]{:S(2)}) collective-permute-start(f32[2,4,1,8,128]{4,3,2,1,0:T(8,128)S(1)} %get-tuple-element.38), channel_id=1, source_target_pairs={{0,2},{2,4},{4,6},{6,8},{8,10},{10,12},{12,14},{14,16},{16,18},{18... | collective-permute-start | bytes 98312 | tf_op jit(solution)/shard_map/ppermute | solution.py:13
  16.1 5.0 %sort.17 = (s32[2048]{0:T(1024)}, s32[2048]{0:T(1024)S(1)}) sort(s32[2048]{0:T(1024)S(1)} %add_select_fusion.1, s32[2048]{0:T(1024)S(1)} %iota.10), dimensions={0}, to_apply=%region_9.0 | sort | flops 22528 | bytes 32768 | tf_op jit(solution)/shard_map/jit(argsort)/sort | solution.py:69
  21.2 0.1 fusion.25
  21.4 0.2 fusion.4
  21.6 1.3 collective-permute-start.5
  22.9 4.9 %collective-permute-start.4 = (f32[2,4,1,8,128]{4,3,2,1,0:T(8,128)S(1)}, f32[2,4,1,8,128]{4,3,2,1,0:T(8,128)S(1)}, u32[]{:S(2)}, u32[]{:S(2)}) collective-permute-start(f32[2,4,1,8,128]{4,3,2,1,0:T(8,128)S(1)} %get-tuple-element.34), channel_id=1, source_target_pairs={{0,2},{2,4},{4,6},{6,8},{8,10},{10,12},{12,14},{14,16},{16,18},{18... | collective-permute-start | bytes 98312 | tf_op jit(solution)/shard_map/ppermute | solution.py:13
  27.8 11.8 %gather_fusion = s32[2048]{0:T(1024)S(1)} fusion(s32[2048]{0:T(1024)S(1)} %bitcast.113, s32[2048]{0:T(1024)S(1)} %fusion.39), kind=kCustom, calls=%fused_computation | custom fusion | bytes 24576 | tf_op jit(solution)/shard_map/gather | solution.py:72
  39.8 0.1 fusion.30
  40.0 0.2 fusion.5
  40.2 1.3 collective-permute-start.7
  41.5 4.3 %collective-permute-start.6 = (f32[2,4,1,8,128]{4,3,2,1,0:T(8,128)S(1)}, f32[2,4,1,8,128]{4,3,2,1,0:T(8,128)S(1)}, u32[]{:S(2)}, u32[]{:S(2)}) collective-permute-start(f32[2,4,1,8,128]{4,3,2,1,0:T(8,128)S(1)} %get-tuple-element.30), channel_id=1, source_target_pairs={{0,2},{2,4},{4,6},{6,8},{8,10},{10,12},{12,14},{14,16},{16,18},{18... | collective-permute-start | bytes 98312 | tf_op jit(solution)/shard_map/ppermute | solution.py:13
  45.8 0.7 copy.59
  46.5 29.3 %all-to-all-start = ((f32[128,1,16]{2,1,0:T(1,128)}), f32[128,1,16]{2,1,0:T(1,128)S(1)}, u32[]{:S(2)}, u32[]{:S(2)}) async-start(f32[128,1,16]{2,1,0:T(1,128)} %copy.59), calls=%async_computation | async-start | bytes 131072 | tf_op jit(solution)/shard_map/all_to_all | solution.py:75
  76.0 0.1 fusion.35
  76.1 4.5 %multiply_reduce_fusion = f32[2,8,128,128]{3,2,1,0:T(8,128)S(1)} fusion(bf16[2,4,2,8,128,128]{5,4,3,2,1,0:T(8,128)(2,1)} %param.10, f32[2,4,2,8,128]{4,3,2,1,0:T(8,128)S(1)} %fusion.15), kind=kLoop, calls=%fused_computation.3 | loop fusion | flops 6029312 | bytes 5308416 | tf_op jit(solution)/shard_map/reduce_sum | solution.py:66
  80.6 7.6 %gather_fusion.1 = f32[2048,128]{1,0:T(8,128)} fusion(f32[2048,128]{1,0:T(8,128)S(1)} %bitcast.114, s32[2048]{0:T(1024)S(1)} %fusion.39), kind=kCustom, calls=%fused_computation.1 | custom fusion | bytes 2105344 | tf_op jit(solution)/shard_map/gather | solution.py:71
  88.2 12.4 %all-to-all-start.1 = ((f32[128,16,128]{2,1,0:T(8,128)}), f32[128,16,128]{2,1,0:T(8,128)S(1)}, u32[]{:S(2)}, u32[]{:S(2)}) async-start(f32[128,16,128]{2,1,0:T(8,128)} %bitcast.27), calls=%async_computation.1 | async-start | bytes 2097152 | tf_op jit(solution)/shard_map/all_to_all | solution.py:74
  100.6 0.2 convert_reduce_fusion
  100.9 28.8 %all-to-all-done.1 = f32[128,16,128]{2,1,0:T(8,128)S(1)} async-done(((f32[128,16,128]{2,1,0:T(8,128)}), f32[128,16,128]{2,1,0:T(8,128)S(1)}, u32[]{:S(2)}, u32[]{:S(2)}) %all-to-all-start.1) | async-done | bytes 1048608 | tf_op jit(solution)/shard_map/all_to_all | solution.py:74
  129.7 11.4 %scatter_custom_fusion = f32[4,128]{1,0:T(4,128)S(1)} fusion(s32[2048]{0:T(1024)S(1)} %reshape.133, f32[2048,128]{1,0:T(8,128)S(1)} %bitcast.115, f32[]{:T(128)} %constant.36.clone.1), kind=kCustom, calls=%fused_computation.91 | custom fusion | flops 262144 | bytes 2052 | tf_op jit(solution)/shard_map/scatter-add | solution.py:77
  141.1 7.0 %psum.7 = f32[4,128]{1,0:T(4,128)} all-reduce(f32[4,128]{1,0:T(4,128)S(1)} %scatter_custom_fusion), channel_id=1, replica_groups=mesh['cells'=128,'ens'=2] {'ens'}, use_global_device_ids=true, to_apply=%region_12.13 | all-reduce | flops 512 | bytes 4096 | tf_op jit(solution)/shard_map/psum | solution.py:80
  (49 shorter events, 0.9 us)
Async XLA Ops:
  0.6 4.1 %copy-start.1 = (bf16[2,6,4,4,2,8,128]{6,5,4,3,2,1,0:T(8,128)(2,1)S(1)}, bf16[2,6,4,4,2,8,128]{6,5,4,3,2,1,0:T(8,128)(2,1)}, u32[]{:S(2)}) copy-start(bf16[2,6,4,4,2,8,128]{6,5,4,3,2,1,0:T(8,128)(2,1)} %param.8) | copy-start | bytes 2359300
  4.7 5.5 %copy-start.2 = (bf16[2,4,4,2,8,128]{5,4,3,2,1,0:T(8,128)(2,1)S(1)}, bf16[2,4,4,2,8,128]{5,4,3,2,1,0:T(8,128)(2,1)}, u32[]{:S(2)}) copy-start(bf16[2,4,4,2,8,128]{5,4,3,2,1,0:T(8,128)(2,1)} %param.9) | copy-start | bytes 393220
  4.9 4.5 %collective-permute-start.1 = (f32[2,4,1,8,128]{4,3,2,1,0:T(8,128)S(1)}, f32[2,4,1,8,128]{4,3,2,1,0:T(8,128)S(1)}, u32[]{:S(2)}, u32[]{:S(2)}) collective-permute-start(f32[2,4,1,8,128]{4,3,2,1,0:T(8,128)S(1)} %get-tuple-element.41), channel_id=1, source_target_pairs={{2,0},{4,2},{6,4},{8,6},{10,8},{12,10},{14,12},{16,14},{18,16},{20... | collective-permute-start | bytes 98312 | tf_op jit(solution)/shard_map/ppermute | solution.py:13
  6.3 3.9 %collective-permute-start = (f32[2,4,1,8,128]{4,3,2,1,0:T(8,128)S(1)}, f32[2,4,1,8,128]{4,3,2,1,0:T(8,128)S(1)}, u32[]{:S(2)}, u32[]{:S(2)}) collective-permute-start(f32[2,4,1,8,128]{4,3,2,1,0:T(8,128)S(1)} %get-tuple-element.42), channel_id=1, source_target_pairs={{0,2},{2,4},{4,6},{6,8},{8,10},{10,12},{12,14},{14,16},{16,18},{18... | collective-permute-start | bytes 98312 | tf_op jit(solution)/shard_map/ppermute | solution.py:13
  9.4 6.7 %copy-start = (s32[2,8,128]{2,1,0:T(8,128)S(1)}, s32[2,8,128]{2,1,0:T(8,128)}, u32[]{:S(2)}) copy-start(s32[2,8,128]{2,1,0:T(8,128)} %param.13) | copy-start | bytes 24580
  10.5 10.7 %collective-permute-start.3 = (f32[2,4,1,8,128]{4,3,2,1,0:T(8,128)S(1)}, f32[2,4,1,8,128]{4,3,2,1,0:T(8,128)S(1)}, u32[]{:S(2)}, u32[]{:S(2)}) collective-permute-start(f32[2,4,1,8,128]{4,3,2,1,0:T(8,128)S(1)} %get-tuple-element.37), channel_id=1, source_target_pairs={{2,0},{4,2},{6,4},{8,6},{10,8},{12,10},{14,12},{16,14},{18,16},{20... | collective-permute-start | bytes 98312 | tf_op jit(solution)/shard_map/ppermute | solution.py:13
  11.8 9.4 %collective-permute-start.2 = (f32[2,4,1,8,128]{4,3,2,1,0:T(8,128)S(1)}, f32[2,4,1,8,128]{4,3,2,1,0:T(8,128)S(1)}, u32[]{:S(2)}, u32[]{:S(2)}) collective-permute-start(f32[2,4,1,8,128]{4,3,2,1,0:T(8,128)S(1)} %get-tuple-element.38), channel_id=1, source_target_pairs={{0,2},{2,4},{4,6},{6,8},{8,10},{10,12},{12,14},{14,16},{16,18},{18... | collective-permute-start | bytes 98312 | tf_op jit(solution)/shard_map/ppermute | solution.py:13
  21.6 18.2 %collective-permute-start.5 = (f32[2,4,1,8,128]{4,3,2,1,0:T(8,128)S(1)}, f32[2,4,1,8,128]{4,3,2,1,0:T(8,128)S(1)}, u32[]{:S(2)}, u32[]{:S(2)}) collective-permute-start(f32[2,4,1,8,128]{4,3,2,1,0:T(8,128)S(1)} %get-tuple-element.33), channel_id=1, source_target_pairs={{2,0},{4,2},{6,4},{8,6},{10,8},{12,10},{14,12},{16,14},{18,16},{20... | collective-permute-start | bytes 98312 | tf_op jit(solution)/shard_map/ppermute | solution.py:13
  22.9 16.9 %collective-permute-start.4 = (f32[2,4,1,8,128]{4,3,2,1,0:T(8,128)S(1)}, f32[2,4,1,8,128]{4,3,2,1,0:T(8,128)S(1)}, u32[]{:S(2)}, u32[]{:S(2)}) collective-permute-start(f32[2,4,1,8,128]{4,3,2,1,0:T(8,128)S(1)} %get-tuple-element.34), channel_id=1, source_target_pairs={{0,2},{2,4},{4,6},{6,8},{8,10},{10,12},{12,14},{14,16},{16,18},{18... | collective-permute-start | bytes 98312 | tf_op jit(solution)/shard_map/ppermute | solution.py:13
  40.2 35.7 %collective-permute-start.7 = (f32[2,4,1,8,128]{4,3,2,1,0:T(8,128)S(1)}, f32[2,4,1,8,128]{4,3,2,1,0:T(8,128)S(1)}, u32[]{:S(2)}, u32[]{:S(2)}) collective-permute-start(f32[2,4,1,8,128]{4,3,2,1,0:T(8,128)S(1)} %get-tuple-element.29), channel_id=1, source_target_pairs={{2,0},{4,2},{6,4},{8,6},{10,8},{12,10},{14,12},{16,14},{18,16},{20... | collective-permute-start | bytes 98312 | tf_op jit(solution)/shard_map/ppermute | solution.py:13
  41.5 34.4 %collective-permute-start.6 = (f32[2,4,1,8,128]{4,3,2,1,0:T(8,128)S(1)}, f32[2,4,1,8,128]{4,3,2,1,0:T(8,128)S(1)}, u32[]{:S(2)}, u32[]{:S(2)}) collective-permute-start(f32[2,4,1,8,128]{4,3,2,1,0:T(8,128)S(1)} %get-tuple-element.30), channel_id=1, source_target_pairs={{0,2},{2,4},{4,6},{6,8},{8,10},{10,12},{12,14},{14,16},{16,18},{18... | collective-permute-start | bytes 98312 | tf_op jit(solution)/shard_map/ppermute | solution.py:13
  46.5 41.7 %all-to-all-start = ((f32[128,1,16]{2,1,0:T(1,128)}), f32[128,1,16]{2,1,0:T(1,128)S(1)}, u32[]{:S(2)}, u32[]{:S(2)}) async-start(f32[128,1,16]{2,1,0:T(1,128)} %copy.59), calls=%async_computation | async-start | bytes 131072 | tf_op jit(solution)/shard_map/all_to_all | solution.py:75
  76.1 4.5 %copy-start.3 = (f32[2,4,2,8,128]{4,3,2,1,0:T(8,128)}, f32[2,4,2,8,128]{4,3,2,1,0:T(8,128)S(1)}, u32[]{:S(2)}) copy-start(f32[2,4,2,8,128]{4,3,2,1,0:T(8,128)S(1)} %fusion.15) | copy-start | bytes 196612
  88.2 41.5 %all-to-all-start.1 = ((f32[128,16,128]{2,1,0:T(8,128)}), f32[128,16,128]{2,1,0:T(8,128)S(1)}, u32[]{:S(2)}, u32[]{:S(2)}) async-start(f32[128,16,128]{2,1,0:T(8,128)} %bitcast.27), calls=%async_computation.1 | async-start | bytes 2097152 | tf_op jit(solution)/shard_map/all_to_all | solution.py:74
where the time goes:
time: 149 us; the launch traced here: 148 us
  starting transfers between devices  63.3 us (42%)
  waiting for transfers between devices  29.5 us (20%)
  other arithmetic  24.1 us (16%)
  local copies, waits for them, and re-layouts  21.6 us (14%)
  blocking collectives  7.02 us (5%)
    all_to_all x1, starting transfers between devices, body(): lax.all_to_all(send_ids, 'cells', split_axis=0, concat_axis=0, tiled=True)  29.3 us
    all_to_all x1, waiting for transfers between devices, body(): lax.all_to_all(send_rows, 'cells', split_axis=0, concat_axis=0, tiled=True)  28.8 us
    ppermute x8, starting transfers between devices, from_behind(): return lax.ppermute(value, axis, pairs)  21.6 us
    all_to_all x1, starting transfers between devices, body(): lax.all_to_all(send_rows, 'cells', split_axis=0, concat_axis=0, tiled=True)  12.4 us
    gather x3, local copies, waits for them, and re-layouts, body(): flat_map[order] % BLK_DEV  11.9 us
    scatter-add x1, other arithmetic, body(): jax.ops.segment_sum(got_rows.reshape(-1, params), got_ids.reshape(-1).ast...  11.4 us
    gather x1, local copies, waits for them, and re-layouts, body(): send_rows = cell_grad[order].reshape(ranks, per_owner, params)  7.58 us
    psum x1, blocking collectives, body(): gradient = lax.psum(owned, 'ens')  7.02 us
  transfers between devices with their start and end apart: 10, of which 2 were waited for; matrix products, arithmetic and copies ran while one was open for 21% of the time, Pallas kernels for 0%

commit v1 on v0

v1 whole, which is shorter than its diff:
```python
import jax
import jax.numpy as jnp
from jax import lax
from jax.experimental import pallas as pl
from jax.experimental.pallas import tpu as pltpu
from jax.sharding import PartitionSpec as P

BLK_DEV = 4
F32 = jnp.float32
BF16 = jnp.bfloat16


def shift_lanes(x, by):
    size = x.shape[2]
    lane = lax.broadcasted_iota(jnp.int32, x.shape, 2)
    keep = lane >= 1 if by == 1 else lane < size - 1
    return jnp.where(keep, pltpu.roll(x, by % size, 2), 0.0)


def shift_rows(x, by):
    size = x.shape[1]
    row = lax.broadcasted_iota(jnp.int32, x.shape, 1)
    keep = row >= 1 if by == 1 else row < size - 1
    return jnp.where(keep, pltpu.roll(x, by % size, 1), 0.0)


def products(cpl, m, k, a):
    unk = len(a)
    out = []
    for v in range(unk):
        total = cpl[m, k, 0, v].astype(F32) * a[0]
        for u in range(1, unk):
            total = total + cpl[m, k, u, v].astype(F32) * a[u]
        out.append(total)
    return out


def local_coupling(cpl, m, a):
    unk = len(a)
    terms = [products(cpl, m, k, a) for k in range(6)]
    inner, up, down = [], [], []
    for v in range(unk):
        t = [terms[k][v] for k in range(6)]
        planes = t[0].shape[0]
        zero = jnp.zeros_like(t[0][:1])
        total = jnp.concatenate([zero, t[0][: planes - 1]], axis=0)
        total = total + jnp.concatenate([t[1][1:], zero], axis=0)
        total = total + shift_rows(t[2], 1) + shift_rows(t[3], -1)
        total = total + shift_lanes(t[4], 1) + shift_lanes(t[5], -1)
        inner.append(total)
        up.append(t[0][planes - 1])
        down.append(t[1][0])
    return inner, up, down


def apply_inverse(inv, m, r):
    unk = len(r)
    out = []
    for v in range(unk):
        total = inv[m, 0, v].astype(F32) * r[0]
        for w in range(1, unk):
            total = total + inv[m, w, v].astype(F32) * r[w]
        out.append(total)
    return out


def plane_products(cpl, m, k, plane, a):
    unk = len(a)
    out = []
    for v in range(unk):
        total = cpl[m, k, 0, v, plane].astype(F32) * a[0]
        for u in range(1, unk):
            total = total + cpl[m, k, u, v, plane].astype(F32) * a[u]
        out.append(total)
    return out


def two_sweep_payload(cpl, inv, m, src, a):
    planes = a[0].shape[0]
    inner, up0, down0 = local_coupling(cpl, m, a)
    nxt = apply_inverse(inv, m, [s - b for s, b in zip(src, inner)])
    up1 = plane_products(cpl, m, 0, planes - 1, [x[planes - 1] for x in nxt])
    down1 = plane_products(cpl, m, 1, 0, [x[0] for x in nxt])
    return nxt, up0 + up1, down0 + down1


def transfer_blocks(cpl, inv, m, k, plane, unk):
    out = []
    for w in range(unk):
        for v in range(unk):
            total = inv[m, w, 0, plane].astype(F32) * cpl[m, k, 0, v, plane].astype(F32)
            for u in range(1, unk):
                total = total + inv[m, w, u, plane].astype(F32) * cpl[m, k, u, v, plane].astype(F32)
            out.append(total)
    return out


def split3(x):
    hi = x.astype(BF16)
    rest = x - hi.astype(F32)
    mid = rest.astype(BF16)
    lo = (rest - mid.astype(F32)).astype(BF16)
    return hi, mid, lo


def injected(wells, misfit, first, shape):
    members, unk, planes, rows, lanes = shape
    count = planes * rows * lanes
    nwell = wells.shape[1]
    place = wells[...] - first
    inside = (place >= 0) & (place < count)
    line = jnp.where(inside, place // lanes, -1)
    lane = jnp.where(inside, place % lanes, -1)
    lines = lax.broadcasted_iota(jnp.int32, (planes * rows, nwell), 0) == line
    onlane = (lax.broadcasted_iota(jnp.int32, (lanes, nwell), 0) == lane).astype(F32).astype(BF16)
    left = []
    for m in range(members):
        for u in range(unk):
            left.append(jnp.where(lines, misfit[m, u : u + 1, :], 0.0))
    stacked = jnp.concatenate(split3(jnp.concatenate(left, axis=0)), axis=0)
    full = lax.dot_general(stacked, onlane, (((1,), (1,)), ((), ())), preferred_element_type=F32)
    n = members * unk * planes * rows
    total = full[:n] + full[n : 2 * n] + full[2 * n :]
    return total.reshape(shape)


def start_kernel(pos, wells, misfit, later, cpl, inv, src_out, nxt_out, intra_out, cross_out):
    shape = later.shape
    members, unk, planes = shape[:3]
    even = pos[0] % 2 == 0
    count = planes * shape[3] * shape[4]
    src_out[...] = later[...] + injected(wells, misfit, pos[0] * count, shape)
    for m in range(members):
        src = [src_out[m, u] for u in range(unk)]
        a = apply_inverse(inv, m, src)
        nxt, up, down = two_sweep_payload(cpl, inv, m, src, a)
        up = up + transfer_blocks(cpl, inv, m, 0, planes - 1, unk)
        down = down + transfer_blocks(cpl, inv, m, 1, 0, unk)
        for u in range(unk):
            nxt_out[m, u] = nxt[u]
        for j in range(len(up)):
            intra_out[m, j] = jnp.where(even, up[j], down[j])
            cross_out[m, j] = jnp.where(even, down[j], up[j])


def incoming(pos, last, m, unk, blocks, sent_intra, sent_cross, got_intra, got_cross):
    even = pos[0] % 2 == 0
    has_cross = (pos[0] != 0) & (pos[0] != last)
    out = []
    sides = []
    for sent, got, block in ((sent_intra, got_intra, blocks[0]), (sent_cross, got_cross, blocks[1])):
        first = [got[m, v] for v in range(unk)]
        second = []
        for v in range(unk):
            total = got[m, unk + v]
            for w in range(unk):
                total = total - block[m, 2 * unk + w * unk + v] * sent[m, w]
            second.append(total)
        sides.append((first, second))
    for n in range(2):
        low, high = [], []
        for v in range(unk):
            near = sides[0][n][v]
            far = jnp.where(has_cross, sides[1][n][v], 0.0)
            low.append(jnp.where(even, far, near))
            high.append(jnp.where(even, near, far))
        out.append([jnp.stack([lo, hi], axis=0) for lo, hi in zip(low, high)])
    return out


def finish_two(cpl, inv, m, src, nxt, arrived):
    a1 = [x - d for x, d in zip(nxt, apply_inverse(inv, m, arrived[0]))]
    inner, _, _ = local_coupling(cpl, m, a1)
    return apply_inverse(inv, m, [s - b - p for s, b, p in zip(src, inner, arrived[1])])


def make_middle(last):
    def middle_kernel(pos, src, nxt, sent_intra, sent_cross, got_intra, got_cross, cpl, inv, nxt_out, intra_out, cross_out):
        members, unk = src.shape[:2]
        even = pos[0] % 2 == 0
        for m in range(members):
            arrived = incoming(
                pos, last, m, unk, (got_intra, got_cross), sent_intra, sent_cross, got_intra, got_cross
            )
            s = [src[m, u] for u in range(unk)]
            a = finish_two(cpl, inv, m, s, [nxt[m, u] for u in range(unk)], arrived)
            ahead, up, down = two_sweep_payload(cpl, inv, m, s, a)
            for u in range(unk):
                nxt_out[m, u] = ahead[u]
            for j in range(len(up)):
                intra_out[m, j] = jnp.where(even, up[j], down[j])
                cross_out[m, j] = jnp.where(even, down[j], up[j])

    return middle_kernel


def make_end(last, nblk):
    def end_kernel(
        pos, src, nxt, block_intra, block_cross, sent_intra, sent_cross, got_intra, got_cross, cpl, inv, bmap, sens,
        adj_out, mine_out, other_out, sens_buf, onehot, grads, sems,
    ):
        members, unk, planes, rows, lanes = src.shape
        params = sens.shape[-1]
        groups = planes * rows
        copies = []
        for x in range(planes):
            for half in range(2):
                n = rows // 2
                part = (slice(None), slice(None), x, slice(half * n, half * n + n))
                copies.append(pltpu.make_async_copy(sens.at[part], sens_buf.at[part], sems.at[x * 2 + half]))
        for c in copies:
            c.start()
        core = pos[0] % 2
        slot = lax.broadcasted_iota(jnp.int32, (nblk, lanes), 0)
        half_rows = nblk // 2
        parity = jnp.where(slot < half_rows, core, 1 - core)
        within = jnp.where(slot < half_rows, slot, slot - half_rows)
        block = (within // BLK_DEV * 2 + parity) * BLK_DEV + within % BLK_DEV
        for g in range(groups):
            row = bmap[g // rows, g % rows : g % rows + 1, :]
            onehot[:, g * lanes : (g + 1) * lanes] = (block == row).astype(F32).astype(BF16)
        for m in range(members):
            arrived = incoming(
                pos, last, m, unk, (block_intra, block_cross), sent_intra, sent_cross, got_intra, got_cross
            )
            a = finish_two(
                cpl, inv, m, [src[m, u] for u in range(unk)], [nxt[m, u] for u in range(unk)], arrived
            )
            for u in range(unk):
                adj_out[m, u] = a[u]
        turned = adj_out[...].reshape(members * unk * groups, lanes).T
        per = groups // len(copies)
        for i, c in enumerate(copies):
            c.wait()
            for g in range(i * per, i * per + per):
                x, y = g // rows, g % rows
                total = None
                for m in range(members):
                    for u in range(unk):
                        col = (m * unk + u) * groups + g
                        term = turned[:, col : col + 1] * sens_buf[m, u, x, y].astype(F32)
                        total = term if total is None else total + term
                hi = total.astype(BF16)
                lo = (total - hi.astype(F32)).astype(BF16)
                grads[g * lanes : (g + 1) * lanes, :params] = hi
                grads[g * lanes : (g + 1) * lanes, params:] = lo
        both = jnp.dot(onehot[...], grads[...], preferred_element_type=F32)
        out = both[:, :params] + both[:, params:]
        mine_out[...] = out[:half_rows]
        other_out[...] = out[half_rows:]

    return end_kernel


VM = pl.BlockSpec(memory_space=pltpu.VMEM)
SM = pl.BlockSpec(memory_space=pltpu.SMEM)
HB = pl.BlockSpec(memory_space=pl.ANY)


def shaped(*shape):
    return jax.ShapeDtypeStruct(shape, F32)


def body(later_adjoint, coupling, diag_inverse, sensitivity, well_cells, well_misfit, block_map):
    members, unk, planes, rows, lanes = later_adjoint.shape
    count = planes * rows * lanes
    params = sensitivity.shape[-1]
    ranks = lax.axis_size("cells")
    nblk = ranks * BLK_DEV
    pos = lax.axis_index("cells").astype(jnp.int32).reshape(1)
    intra_pairs = [(i, i ^ 1) for i in range(ranks)]
    cross_pairs = [(i, i + 1 if i % 2 else i - 1) for i in range(1, ranks - 1)] + [(0, 0), (ranks - 1, ranks - 1)]

    def exchange(intra, cross):
        return lax.ppermute(intra, "cells", intra_pairs), lax.ppermute(cross, "cells", cross_pairs)

    field = shaped(members, unk, planes, rows, lanes)
    first_size = 2 * unk + unk * unk
    with jax.named_scope("start"):
        src, nxt, intra, cross = pl.pallas_call(
            start_kernel,
            out_shape=(field, field, shaped(members, first_size, rows, lanes), shaped(members, first_size, rows, lanes)),
            in_specs=[SM, VM, VM, VM, VM, VM],
            out_specs=(VM, VM, VM, VM),
        )(pos, well_cells.reshape(1, -1), well_misfit, later_adjoint, coupling, diag_inverse)
    got_intra, got_cross = exchange(intra, cross)
    with jax.named_scope("middle"):
        nxt2, intra2, cross2 = pl.pallas_call(
            make_middle(ranks - 1),
            out_shape=(field, shaped(members, 2 * unk, rows, lanes), shaped(members, 2 * unk, rows, lanes)),
            in_specs=[SM] + [VM] * 8,
            out_specs=(VM, VM, VM),
        )(pos, src, nxt, intra, cross, got_intra, got_cross, coupling, diag_inverse)
    got_intra2, got_cross2 = exchange(intra2, cross2)
    with jax.named_scope("end"):
        adjoint, mine, other = pl.pallas_call(
            make_end(ranks - 1, nblk),
            out_shape=(field, shaped(nblk // 2, params), shaped(nblk // 2, params)),
            in_specs=[SM] + [VM] * 11 + [HB],
            out_specs=(VM, VM, VM),
            scratch_shapes=[
                pltpu.VMEM(sensitivity.shape, BF16),
                pltpu.VMEM((nblk, count), BF16),
                pltpu.VMEM((count, 2 * params), BF16),
                pltpu.SemaphoreType.DMA((2 * planes,)),
            ],
        )(
            pos, src, nxt2, got_intra, got_cross, intra2, cross2, got_intra2, got_cross2,
            coupling, diag_inverse, block_map, sensitivity,
        )
    chips = ranks // 2
    half = mine + lax.ppermute(other, "cells", intra_pairs)
    same_core = [[core + 2 * chip for chip in range(chips)] for core in range(2)]
    parts = lax.all_to_all(
        half.reshape(chips, BLK_DEV, params), "cells", 0, 0, tiled=True, axis_index_groups=same_core
    )
    owned = jnp.sum(parts, axis=0)
    gradient = owned + lax.ppermute(owned, "ens", [(0, 1), (1, 0)])
    return (adjoint, gradient)


def solution(mesh):
    placed = (
        P("ens", None, "cells", None, None),
        P("ens", None, None, None, "cells", None, None),
        P("ens", None, None, "cells", None, None),
        P("ens", None, "cells", None, None, None),
        P(),
        P("ens", None, None),
        P("cells", None, None),
    )
    return jax.shard_map(
        body,
        mesh=mesh,
        in_specs=placed,
        out_specs=(P("ens", None, "cells", None, None), P("cells", None)),
        check_vma=False,
    )
```

time: 149 us -> 65.6 us (0.44)
  starting transfers between devices: 63.3 us -> 14.1 us
  waiting for transfers between devices: 29.5 us -> 6.04 us
  blocking collectives: 7.02 us -> 29.9 us
  other arithmetic: 24.1 us -> 1.58 us
  local copies, waits for them, and re-layouts: 21.6 us -> 1.37 us
  Pallas kernels: 0 us -> 11.6 us
    all_to_all x2 -> x0, starting transfers between devices: 41.8 us -> none  [the longest x1 29.3 us: body(): lax.all_to_all(send_ids, 'cells', split_axis=0, concat_axis=0, tiled=True)]
    all_to_all x0 -> x1, blocking collectives: none -> 29.9 us  [body(): lax.all_to_all(half.reshape(chips, BLK_DEV, params), 'cells', 0, 0, tiled...]
    all_to_all x2 -> x0, waiting for transfers between devices: 28.8 us -> none  [the longest x1 28.8 us: body(): lax.all_to_all(send_rows, 'cells', split_axis=0, concat_axis=0, tiled=True)]
    gather x4 -> x0, local copies, waits for them, and re-layouts: 19.5 us -> none  [the longest x3 11.9 us: body(): flat_map[order] % BLK_DEV]
    pallas_call x0 -> x3, Pallas kernels: none -> 11.6 us  [the longest x1 6.54 us: body(): pl.pallas_call(make_end(ranks - 1, nblk), out_shape=(field, shaped(nblk /...]
    scatter-add x1 -> x0, other arithmetic: 11.4 us -> none  [body(): jax.ops.segment_sum(got_rows.reshape(-1, params), got_ids.reshape(-1).ast...]
    ppermute x8 -> x6, starting transfers between devices: 21.6 us -> 14.1 us  [the longest x2 5.97 us: exchange(): lax.ppermute(intra, 'cells', intra_pairs)]
    psum x1 -> x0, blocking collectives: 7.02 us -> none  [body(): gradient = lax.psum(owned, 'ens')]
  transfers between devices with their start and end apart: 10 -> 6, of which waited for: 2 -> 3; matrix products, arithmetic and copies ran while one was open for 21% -> 0% of each run, Pallas kernels for 0% -> 0%
where the time goes in v1:
time: 65.6 us; the launch traced here: 65.3 us
  blocking collectives  29.9 us (46%)
  starting transfers between devices  14.1 us (21%)
  Pallas kernels  11.6 us (18%)
  waiting for transfers between devices  6.04 us (9%)
  other arithmetic  1.58 us (2%)
  local copies, waits for them, and re-layouts  1.37 us (2%)
  between operations  0.67 us (1%)
    all_to_all x1, blocking collectives, body(): lax.all_to_all(half.reshape(chips, BLK_DEV, params), 'cells', 0, 0, tiled...  29.9 us
    pallas_call x1, Pallas kernels, body(): pl.pallas_call(make_end(ranks - 1, nblk), out_shape=(field, shaped(nblk /...  6.54 us
    ppermute x2, starting transfers between devices, exchange(): lax.ppermute(intra, 'cells', intra_pairs)  5.97 us
    ppermute x1, waiting for transfers between devices, body(): gradient = owned + lax.ppermute(owned, 'ens', [(0, 1), (1, 0)])  4.76 us
    ppermute x1, starting transfers between devices, body(): half = mine + lax.ppermute(other, 'cells', intra_pairs)  4.66 us
    ppermute x2, starting transfers between devices, exchange(): lax.ppermute(cross, 'cells', cross_pairs)  3.06 us
    pallas_call x1, Pallas kernels, body(): pl.pallas_call(make_middle(ranks - 1), out_shape=(field, shaped(members,...  2.6 us
    pallas_call x1, Pallas kernels, body(): pl.pallas_call(start_kernel, out_shape=(field, field, shaped(members, fir...  2.47 us
  transfers between devices with their start and end apart: 6, of which 3 were waited for; matrix products, arithmetic and copies ran while one was open for 0% of the time, Pallas kernels for 0%

profile of v1, /device:TPU:16, one launch (start us, length us, event | category | flops | bytes accessed | tf_op | source)
XLA Modules:
  0.0 65.3 jit_solution(8856265649709697566)
XLA Ops:
  0.6 2.5 %start.1 = (f32[2,4,2,8,128]{4,3,2,1,0:T(8,128)}, f32[2,4,2,8,128]{4,3,2,1,0:T(8,128)}, f32[2,24,8,128]{3,2,1,0:T(8,128)}, f32[2,24,8,128]{3,2,1,0:T(8,128)}) custom-call(s32[1]{0:T(128)} %bitcast.pos, s32[1,256]{1,0:T(1,128)} %bitcast.4, f32[2,4,256]{2,1,0:T(4,128)} %misfit.1, f32[2,4,2,8,128]{4,3,2,1,0:T(8,128)} %later.1, ...), custom_call_target="tpu_custom_call" | custom-call | tf_op jit(solution)/shard_map/start/pallas_call | solution.py:280
  3.1 0.0 collective-permute-start
  3.1 1.6 %collective-permute-start.1 = (f32[2,24,8,128]{3,2,1,0:T(8,128)}, f32[2,24,8,128]{3,2,1,0:T(8,128)S(1)}, u32[]{:S(2)}, u32[]{:S(2)}) collective-permute-start(f32[2,24,8,128]{3,2,1,0:T(8,128)} %get-tuple-element.15.sent_cross), channel_id=1, source_target_pairs={{2,4},{4,2},{6,8},{8,6},{10,12},{12,10},{14,16},{16,14},{18,20},{2... | collective-permute-start | bytes 589832 | tf_op jit(solution)/shard_map/ppermute | solution.py:275
  4.7 0.1 collective-permute-done.got_intra.block_intra
  4.8 0.0 copy-start
  4.8 0.0 collective-permute-done.1.got_cross.block_cross
  4.8 0.0 copy-start.1
  4.8 0.7 %copy-done = f32[2,24,8,128]{3,2,1,0:T(8,128)} copy-done((f32[2,24,8,128]{3,2,1,0:T(8,128)}, f32[2,24,8,128]{3,2,1,0:T(8,128)S(1)}, u32[]{:S(2)}) %copy-start) | copy-done | bytes 196632
  5.4 0.1 copy-done.1
  5.5 2.6 %middle.1 = (f32[2,4,2,8,128]{4,3,2,1,0:T(8,128)}, f32[2,8,8,128]{3,2,1,0:T(8,128)}, f32[2,8,8,128]{3,2,1,0:T(8,128)}) custom-call(s32[1]{0:T(128)} %bitcast.pos, f32[2,4,2,8,128]{4,3,2,1,0:T(8,128)} %get-tuple-element.12.src, f32[2,4,2,8,128]{4,3,2,1,0:T(8,128)} %get-tuple-element.13.nxt, f32[2,24,8,128]{3,2,1,0:T(8,128)} %get-tuple-element.14.sent_intra, ...), custom_call_target="tpu_custom_call" | custom-call | tf_op jit(solution)/shard_map/middle/pallas_call | solution.py:288
  8.1 6.0 %collective-permute-start.2 = (f32[2,8,8,128]{3,2,1,0:T(8,128)}, f32[2,8,8,128]{3,2,1,0:T(8,128)S(1)}, u32[]{:S(2)}, u32[]{:S(2)}) collective-permute-start(f32[2,8,8,128]{3,2,1,0:T(8,128)} %get-tuple-element.17.sent_intra), channel_id=1, source_target_pairs={{0,2},{2,0},{4,6},{6,4},{8,10},{10,8},{12,14},{14,12},{16,18},{18,... | collective-permute-start | bytes 196616 | tf_op jit(solution)/shard_map/ppermute | solution.py:275
  14.1 1.5 %collective-permute-start.3 = (f32[2,8,8,128]{3,2,1,0:T(8,128)}, f32[2,8,8,128]{3,2,1,0:T(8,128)S(1)}, u32[]{:S(2)}, u32[]{:S(2)}) collective-permute-start(f32[2,8,8,128]{3,2,1,0:T(8,128)} %get-tuple-element.18.sent_cross), channel_id=1, source_target_pairs={{2,4},{4,2},{6,8},{8,6},{10,12},{12,10},{14,16},{16,14},{18,20},{2... | collective-permute-start | bytes 196616 | tf_op jit(solution)/shard_map/ppermute | solution.py:275
  15.6 0.0 collective-permute-done.2.got_intra
  15.6 0.0 copy-start.2
  15.6 0.0 collective-permute-done.3.got_cross
  15.6 0.0 copy-start.3
  15.6 0.6 copy-done.2
  16.2 0.0 copy-done.3
  16.2 6.5 %end.1 = (f32[2,4,2,8,128]{4,3,2,1,0:T(8,128)}, f32[256,128]{1,0:T(8,128)}, f32[256,128]{1,0:T(8,128)}) custom-call(s32[1]{0:T(128)} %bitcast.pos, f32[2,4,2,8,128]{4,3,2,1,0:T(8,128)} %get-tuple-element.12.src, f32[2,4,2,8,128]{4,3,2,1,0:T(8,128)} %get-tuple-element.16.nxt, f32[2,24,8,128]{3,2,1,0:T(8,128)} %copy-done, f32[2,24,8,128]{3,2,1,0:T(8,128)} %copy-done.1, ...), custom_call_target="tpu_custom_call" | custom-call | tf_op jit(solution)/shard_map/end/pallas_call | solution.py:296
  22.8 4.7 %collective-permute-start.4 = (f32[256,128]{1,0:T(8,128)}, f32[256,128]{1,0:T(8,128)S(1)}, u32[]{:S(2)}, u32[]{:S(2)}) collective-permute-start(f32[256,128]{1,0:T(8,128)} %get-tuple-element.21), channel_id=1, source_target_pairs={{0,2},{2,0},{4,6},{6,4},{8,10},{10,8},{12,14},{14,12},{16,18},{18,... | collective-permute-start | bytes 393224 | tf_op jit(solution)/shard_map/ppermute | solution.py:312
  27.4 1.2 %collective-permute-done.4 = f32[256,128]{1,0:T(8,128)S(1)} collective-permute-done((f32[256,128]{1,0:T(8,128)}, f32[256,128]{1,0:T(8,128)S(1)}, u32[]{:S(2)}, u32[]{:S(2)}) %collective-permute-start.4) | collective-permute-done | bytes 131104 | tf_op jit(solution)/shard_map/ppermute | solution.py:312
  28.6 0.9 %add.6 = f32[256,128]{1,0:T(8,128)S(1)} add(f32[256,128]{1,0:T(8,128)} %get-tuple-element.20, f32[256,128]{1,0:T(8,128)S(1)} %collective-permute-done.4) | non-fusion elementwise | flops 32768 | bytes 393216 | tf_op jit(solution)/shard_map/add | solution.py:312
  29.5 29.9 %all_to_all.5 = f32[64,4,128]{2,1,0:T(4,128)S(1)} all-to-all(f32[64,4,128]{2,1,0:T(4,128)S(1)} %bitcast.3), channel_id=1, replica_groups={{0,4,8,12,16,20,24,28,32,36,40,44,48,52,56,60,64,68,72,76,80,84,88,92,9..., dimensions={0} | all-to-all | bytes 262144 | tf_op jit(solution)/shard_map/all_to_all | solution.py:314
  59.5 0.1 reduce_sum.9
  59.5 0.4 collective-permute-start.5
  59.9 4.8 %collective-permute-done.5 = f32[4,128]{1,0:T(4,128)S(1)} collective-permute-done((f32[4,128]{1,0:T(4,128)S(1)}, f32[4,128]{1,0:T(4,128)S(1)}, u32[]{:S(2)}, u32[]{:S(2)}) %collective-permute-start.5) | collective-permute-done | bytes 2080 | tf_op jit(solution)/shard_map/ppermute | solution.py:318
  64.7 0.6 add.7
Async XLA Ops:
  3.1 1.7 %collective-permute-start = (f32[2,24,8,128]{3,2,1,0:T(8,128)}, f32[2,24,8,128]{3,2,1,0:T(8,128)S(1)}, u32[]{:S(2)}, u32[]{:S(2)}) collective-permute-start(f32[2,24,8,128]{3,2,1,0:T(8,128)} %get-tuple-element.14.sent_intra), channel_id=1, source_target_pairs={{0,2},{2,0},{4,6},{6,4},{8,10},{10,8},{12,14},{14,12},{16,18},{18,... | collective-permute-start | bytes 589832 | tf_op jit(solution)/shard_map/ppermute | solution.py:275
  3.1 1.7 %collective-permute-start.1 = (f32[2,24,8,128]{3,2,1,0:T(8,128)}, f32[2,24,8,128]{3,2,1,0:T(8,128)S(1)}, u32[]{:S(2)}, u32[]{:S(2)}) collective-permute-start(f32[2,24,8,128]{3,2,1,0:T(8,128)} %get-tuple-element.15.sent_cross), channel_id=1, source_target_pairs={{2,4},{4,2},{6,8},{8,6},{10,12},{12,10},{14,16},{16,14},{18,20},{2... | collective-permute-start | bytes 589832 | tf_op jit(solution)/shard_map/ppermute | solution.py:275
  4.8 0.7 %copy-start = (f32[2,24,8,128]{3,2,1,0:T(8,128)}, f32[2,24,8,128]{3,2,1,0:T(8,128)S(1)}, u32[]{:S(2)}) copy-start(f32[2,24,8,128]{3,2,1,0:T(8,128)S(1)} %collective-permute-done.got_intra.block_intra) | copy-start | bytes 589828
  4.8 0.7 %copy-start.1 = (f32[2,24,8,128]{3,2,1,0:T(8,128)}, f32[2,24,8,128]{3,2,1,0:T(8,128)S(1)}, u32[]{:S(2)}) copy-start(f32[2,24,8,128]{3,2,1,0:T(8,128)S(1)} %collective-permute-done.1.got_cross.block_cross) | copy-start | bytes 589828
  8.1 7.5 %collective-permute-start.2 = (f32[2,8,8,128]{3,2,1,0:T(8,128)}, f32[2,8,8,128]{3,2,1,0:T(8,128)S(1)}, u32[]{:S(2)}, u32[]{:S(2)}) collective-permute-start(f32[2,8,8,128]{3,2,1,0:T(8,128)} %get-tuple-element.17.sent_intra), channel_id=1, source_target_pairs={{0,2},{2,0},{4,6},{6,4},{8,10},{10,8},{12,14},{14,12},{16,18},{18,... | collective-permute-start | bytes 196616 | tf_op jit(solution)/shard_map/ppermute | solution.py:275
  14.1 1.5 %collective-permute-start.3 = (f32[2,8,8,128]{3,2,1,0:T(8,128)}, f32[2,8,8,128]{3,2,1,0:T(8,128)S(1)}, u32[]{:S(2)}, u32[]{:S(2)}) collective-permute-start(f32[2,8,8,128]{3,2,1,0:T(8,128)} %get-tuple-element.18.sent_cross), channel_id=1, source_target_pairs={{2,4},{4,2},{6,8},{8,6},{10,12},{12,10},{14,16},{16,14},{18,20},{2... | collective-permute-start | bytes 196616 | tf_op jit(solution)/shard_map/ppermute | solution.py:275
  15.6 0.6 copy-start.2
  15.6 0.6 copy-start.3
  22.8 5.9 %collective-permute-start.4 = (f32[256,128]{1,0:T(8,128)}, f32[256,128]{1,0:T(8,128)S(1)}, u32[]{:S(2)}, u32[]{:S(2)}) collective-permute-start(f32[256,128]{1,0:T(8,128)} %get-tuple-element.21), channel_id=1, source_target_pairs={{0,2},{2,0},{4,6},{6,4},{8,10},{10,8},{12,14},{14,12},{16,18},{18,... | collective-permute-start | bytes 393224 | tf_op jit(solution)/shard_map/ppermute | solution.py:312
  59.5 5.2 %collective-permute-start.5 = (f32[4,128]{1,0:T(4,128)S(1)}, f32[4,128]{1,0:T(4,128)S(1)}, u32[]{:S(2)}, u32[]{:S(2)}) collective-permute-start(f32[4,128]{1,0:T(4,128)S(1)} %reduce_sum.9), channel_id=1, source_target_pairs={{0,1},{1,0},{2,3},{3,2},{4,5},{5,4},{6,7},{7,6},{8,9},{9,8},{10,11... | collective-permute-start | bytes 6152 | tf_op jit(solution)/shard_map/ppermute | solution.py:318

commit v2 on v1

--- a/solution.py
+++ b/solution.py
@@ -124,16 +124,28 @@
     return total.reshape(shape)
 
 
-def start_kernel(pos, wells, misfit, later, cpl, inv, src_out, nxt_out, intra_out, cross_out):
-    shape = later.shape
+def start_kernel(
+    pos, wells_in, misfit_in, later_in, cpl_in, inv_in, src, nxt_out, intra_out, cross_out, cpl, inv, wells, misfit, sems
+):
+    shape = src.shape
     members, unk, planes = shape[:3]
+    moves = ((wells_in, wells), (misfit_in, misfit), (later_in, src), (inv_in, inv), (cpl_in, cpl))
+    copies = [pltpu.make_async_copy(a, b, sems.at[i]) for i, (a, b) in enumerate(moves)]
+    for c in copies:
+        c.start()
     even = pos[0] % 2 == 0
     count = planes * shape[3] * shape[4]
-    src_out[...] = later[...] + injected(wells, misfit, pos[0] * count, shape)
+    copies[0].wait()
+    copies[1].wait()
+    extra = injected(wells, misfit, pos[0] * count, shape)
+    copies[2].wait()
+    src[...] = src[...] + extra
+    copies[3].wait()
+    copies[4].wait()
     for m in range(members):
-        src = [src_out[m, u] for u in range(unk)]
-        a = apply_inverse(inv, m, src)
-        nxt, up, down = two_sweep_payload(cpl, inv, m, src, a)
+        s = [src[m, u] for u in range(unk)]
+        a = apply_inverse(inv, m, s)
+        nxt, up, down = two_sweep_payload(cpl, inv, m, s, a)
         up = up + transfer_blocks(cpl, inv, m, 0, planes - 1, unk)
         down = down + transfer_blocks(cpl, inv, m, 1, 0, unk)
         for u in range(unk):
@@ -194,31 +206,35 @@
     return middle_kernel
 
 
+def select_kernel(pos, bmap_in, sens_in, onehot, sens, bmap, sems):
+    fetch = pltpu.make_async_copy(sens_in, sens, sems.at[0])
+    small = pltpu.make_async_copy(bmap_in, bmap, sems.at[1])
+    small.start()
+    fetch.start()
+    rows, lanes = bmap.shape[1:]
+    nblk = onehot.shape[0]
+    core = pos[0] % 2
+    slot = lax.broadcasted_iota(jnp.int32, (nblk, lanes), 0)
+    half_rows = nblk // 2
+    parity = jnp.where(slot < half_rows, core, 1 - core)
+    within = jnp.where(slot < half_rows, slot, slot - half_rows)
+    block = (within // BLK_DEV * 2 + parity) * BLK_DEV + within % BLK_DEV
+    small.wait()
+    for g in range(bmap.shape[0] * rows):
+        row = bmap[g // rows, g % rows : g % rows + 1, :]
+        onehot[:, g * lanes : (g + 1) * lanes] = (block == row).astype(F32).astype(BF16)
+    fetch.wait()
+
+
 def make_end(last, nblk):
     def end_kernel(
-        pos, src, nxt, block_intra, block_cross, sent_intra, sent_cross, got_intra, got_cross, cpl, inv, bmap, sens,
-        adj_out, mine_out, other_out, sens_buf, onehot, grads, sems,
+        pos, src, nxt, block_intra, block_cross, sent_intra, sent_cross, got_intra, got_cross, cpl, inv, onehot, sens,
+        adj_out, mine_out, other_out, adj, grads, sems,
     ):
         members, unk, planes, rows, lanes = src.shape
         params = sens.shape[-1]
         groups = planes * rows
-        copies = []
-        for x in range(planes):
-            for half in range(2):
-                n = rows // 2
-                part = (slice(None), slice(None), x, slice(half * n, half * n + n))
-                copies.append(pltpu.make_async_copy(sens.at[part], sens_buf.at[part], sems.at[x * 2 + half]))
-        for c in copies:
-            c.start()
-        core = pos[0] % 2
-        slot = lax.broadcasted_iota(jnp.int32, (nblk, lanes), 0)
         half_rows = nblk // 2
-        parity = jnp.where(slot < half_rows, core, 1 - core)
-        within = jnp.where(slot < half_rows, slot, slot - half_rows)
-        block = (within // BLK_DEV * 2 + parity) * BLK_DEV + within % BLK_DEV
-        for g in range(groups):
-            row = bmap[g // rows, g % rows : g % rows + 1, :]
-            onehot[:, g * lanes : (g + 1) * lanes] = (block == row).astype(F32).astype(BF16)
         for m in range(members):
             arrived = incoming(
                 pos, last, m, unk, (block_intra, block_cross), sent_intra, sent_cross, got_intra, got_cross
@@ -227,34 +243,39 @@
                 cpl, inv, m, [src[m, u] for u in range(unk)], [nxt[m, u] for u in range(unk)], arrived
             )
             for u in range(unk):
-                adj_out[m, u] = a[u]
-        turned = adj_out[...].reshape(members * unk * groups, lanes).T
-        per = groups // len(copies)
-        for i, c in enumerate(copies):
-            c.wait()
-            for g in range(i * per, i * per + per):
-                x, y = g // rows, g % rows
-                total = None
-                for m in range(members):
-                    for u in range(unk):
-                        col = (m * unk + u) * groups + g
-                        term = turned[:, col : col + 1] * sens_buf[m, u, x, y].astype(F32)
-                        total = term if total is None else total + term
-                hi = total.astype(BF16)
-                lo = (total - hi.astype(F32)).astype(BF16)
-                grads[g * lanes : (g + 1) * lanes, :params] = hi
-                grads[g * lanes : (g + 1) * lanes, params:] = lo
+                adj[m, u] = a[u]
+        store = pltpu.make_async_copy(adj, adj_out, sems.at[0])
+        store.start()
+        turned = adj[...].reshape(members * unk * groups, lanes).T
+        for g in range(groups):
+            x, y = g // rows, g % rows
+            total = None
+            for m in range(members):
+                for u in range(unk):
+                    col = (m * unk + u) * groups + g
+                    term = turned[:, col : col + 1] * sens[m, u, x, y].astype(F32)
+                    total = term if total is None else total + term
+            hi = total.astype(BF16)
+            lo = (total - hi.astype(F32)).astype(BF16)
+            grads[g * lanes : (g + 1) * lanes, :params] = hi
+            grads[g * lanes : (g + 1) * lanes, params:] = lo
         both = jnp.dot(onehot[...], grads[...], preferred_element_type=F32)
         out = both[:, :params] + both[:, params:]
         mine_out[...] = out[:half_rows]
         other_out[...] = out[half_rows:]
+        store.wait()
 
     return end_kernel
 
 
 VM = pl.BlockSpec(memory_space=pltpu.VMEM)
 SM = pl.BlockSpec(memory_space=pltpu.SMEM)
-HB = pl.BlockSpec(memory_space=pl.ANY)
+HB = pl.BlockSpec(memory_space=pltpu.HBM)
+MIB = 1 << 20
+
+
+def room(mib):
+    return pltpu.CompilerParams(vmem_limit_bytes=mib * MIB)
 
 
 def shaped(*shape):
@@ -276,37 +297,53 @@
 
     field = shaped(members, unk, planes, rows, lanes)
     first_size = 2 * unk + unk * unk
+    wells = well_cells.reshape(1, -1)
+    dma = pltpu.SemaphoreType.DMA
     with jax.named_scope("start"):
-        src, nxt, intra, cross = pl.pallas_call(
+        src, nxt, intra, cross, cpl, inv = pl.pallas_call(
             start_kernel,
-            out_shape=(field, field, shaped(members, first_size, rows, lanes), shaped(members, first_size, rows, lanes)),
-            in_specs=[SM, VM, VM, VM, VM, VM],
-            out_specs=(VM, VM, VM, VM),
-        )(pos, well_cells.reshape(1, -1), well_misfit, later_adjoint, coupling, diag_inverse)
+            out_shape=(
+                field,
+                field,
+                shaped(members, first_size, rows, lanes),
+                shaped(members, first_size, rows, lanes),
+                jax.ShapeDtypeStruct(coupling.shape, BF16),
+                jax.ShapeDtypeStruct(diag_inverse.shape, BF16),
+            ),
+            in_specs=[SM] + [HB] * 5,
+            out_specs=(VM,) * 6,
+            scratch_shapes=[pltpu.VMEM(wells.shape, jnp.int32), pltpu.VMEM(well_misfit.shape, F32), dma((5,))],
+            compiler_params=room(6),
+        )(pos, wells, well_misfit, later_adjoint, coupling, diag_inverse)
     got_intra, got_cross = exchange(intra, cross)
+    with jax.named_scope("select"):
+        onehot, sens = pl.pallas_call(
+            select_kernel,
+            out_shape=(jax.ShapeDtypeStruct((nblk, count), BF16), jax.ShapeDtypeStruct(sensitivity.shape, BF16)),
+            in_specs=[SM, HB, HB],
+            out_specs=(VM, VM),
+            scratch_shapes=[pltpu.VMEM(block_map.shape, jnp.int32), dma((2,))],
+            compiler_params=room(10),
+        )(pos, block_map, sensitivity)
     with jax.named_scope("middle"):
         nxt2, intra2, cross2 = pl.pallas_call(
             make_middle(ranks - 1),
             out_shape=(field, shaped(members, 2 * unk, rows, lanes), shaped(members, 2 * unk, rows, lanes)),
             in_specs=[SM] + [VM] * 8,
             out_specs=(VM, VM, VM),
-        )(pos, src, nxt, intra, cross, got_intra, got_cross, coupling, diag_inverse)
+            compiler_params=room(6),
+        )(pos, src, nxt, intra, cross, got_intra, got_cross, cpl, inv)
     got_intra2, got_cross2 = exchange(intra2, cross2)
     with jax.named_scope("end"):
         adjoint, mine, other = pl.pallas_call(
             make_end(ranks - 1, nblk),
             out_shape=(field, shaped(nblk // 2, params), shaped(nblk // 2, params)),
-            in_specs=[SM] + [VM] * 11 + [HB],
-            out_specs=(VM, VM, VM),
-            scratch_shapes=[
-                pltpu.VMEM(sensitivity.shape, BF16),
-                pltpu.VMEM((nblk, count), BF16),
-                pltpu.VMEM((count, 2 * params), BF16),
-                pltpu.SemaphoreType.DMA((2 * planes,)),
-            ],
+            in_specs=[SM] + [VM] * 12,
+            out_specs=(HB, VM, VM),
+            scratch_shapes=[pltpu.VMEM(field.shape, F32), pltpu.VMEM((count, 2 * params), BF16), dma((1,))],
+            compiler_params=room(16),
         )(
-            pos, src, nxt2, got_intra, got_cross, intra2, cross2, got_intra2, got_cross2,
-            coupling, diag_inverse, block_map, sensitivity,
+            pos, src, nxt2, got_intra, got_cross, intra2, cross2, got_intra2, got_cross2, cpl, inv, onehot, sens,
         )
     chips = ranks // 2
     half = mine + lax.ppermute(other, "cells", intra_pairs)

time: 65.6 us -> 60.6 us (0.924)
  Pallas kernels: 11.6 us -> 5.82 us
  local copies, waits for them, and re-layouts: 1.37 us -> 7.12 us
  starting transfers between devices: 14.1 us -> 11.3 us
  blocking collectives: 29.9 us -> 28 us
  other arithmetic: 1.58 us -> 0.67 us
    unnamed x8 -> x14, local copies, waits for them, and re-layouts: 1.37 us -> 7.12 us
    pallas_call x1, Pallas kernels: 6.54 us -> 3.55 us  [body(): pl.pallas_call(make_end(ranks - 1, nblk), out_shape=(field, shaped(nblk /...]
    pallas_call x1, Pallas kernels: 2.6 us -> 0.45 us  [body(): pl.pallas_call(make_middle(ranks - 1), out_shape=(field, shaped(members,...]
    all_to_all x1, blocking collectives: 29.9 us -> 28 us  [body(): lax.all_to_all(half.reshape(chips, BLK_DEV, params), 'cells', 0, 0, tiled...]
    ppermute x2, starting transfers between devices: 3.06 us -> 1.33 us  [exchange(): lax.ppermute(cross, 'cells', cross_pairs)]
    pallas_call x1, Pallas kernels: 2.47 us -> 0.91 us  [body(): pl.pallas_call(start_kernel, out_shape=(field, field, shaped(members, fir...]
    ppermute x1, starting transfers between devices: 4.66 us -> 3.36 us  [body(): half = mine + lax.ppermute(other, 'cells', intra_pairs)]
    pallas_call x0 -> x1, Pallas kernels: none -> 0.92 us  [body(): pl.pallas_call(select_kernel, out_shape=(jax.ShapeDtypeStruct((nblk, coun...]
  transfers between devices with their start and end apart: 6 -> 6, of which waited for: 3 -> 3; matrix products, arithmetic and copies ran while one was open for 0% -> 0% of each run, Pallas kernels for 0% -> 2%
where the time goes in v2:
time: 60.6 us; the launch traced here: 60.2 us
  blocking collectives  28 us (46%)
  starting transfers between devices  11.3 us (19%)
  local copies, waits for them, and re-layouts  7.12 us (12%)
  waiting for transfers between devices  6.5 us (11%)
  Pallas kernels  5.82 us (10%)
  between operations  0.73 us (1%)
  other arithmetic  0.67 us (1%)
    all_to_all x1, blocking collectives, body(): lax.all_to_all(half.reshape(chips, BLK_DEV, params), 'cells', 0, 0, tiled...  28 us
    unnamed x14, local copies, waits for them, and re-layouts  7.12 us
    ppermute x2, starting transfers between devices, exchange(): lax.ppermute(intra, 'cells', intra_pairs)  6.22 us
    ppermute x1, waiting for transfers between devices, body(): gradient = owned + lax.ppermute(owned, 'ens', [(0, 1), (1, 0)])  4.75 us
    pallas_call x1, Pallas kernels, body(): pl.pallas_call(make_end(ranks - 1, nblk), out_shape=(field, shaped(nblk /...  3.55 us
    ppermute x1, starting transfers between devices, body(): half = mine + lax.ppermute(other, 'cells', intra_pairs)  3.36 us
    ppermute x2, starting transfers between devices, exchange(): lax.ppermute(cross, 'cells', cross_pairs)  1.33 us
  transfers between devices with their start and end apart: 6, of which 3 were waited for; matrix products, arithmetic and copies ran while one was open for 0% of the time, Pallas kernels for 2%

profile of v2, /device:TPU:16, one launch (start us, length us, event | category | flops | bytes accessed | tf_op | source)
XLA Modules:
  0.0 60.2 jit_solution(15191331403400745952)
XLA Ops:
  0.6 0.0 copy-start.1
  0.6 1.1 %copy-done.1 = bf16[2,6,4,4,2,8,128]{6,5,4,3,2,1,0:T(8,128)(2,1)S(1)} copy-done((bf16[2,6,4,4,2,8,128]{6,5,4,3,2,1,0:T(8,128)(2,1)S(1)}, bf16[2,6,4,4,2,8,128]{6,5,4,3,2,1,0:T(8,128)(2,1)}, u32[]{:S(2)}) %copy-start.1) | copy-done | bytes 786456
  1.8 0.0 copy-start.2
  1.8 0.9 %copy-done.2 = bf16[2,4,4,2,8,128]{5,4,3,2,1,0:T(8,128)(2,1)S(1)} copy-done((bf16[2,4,4,2,8,128]{5,4,3,2,1,0:T(8,128)(2,1)S(1)}, bf16[2,4,4,2,8,128]{5,4,3,2,1,0:T(8,128)(2,1)}, u32[]{:S(2)}) %copy-start.2) | copy-done | bytes 131096
  2.7 0.0 copy-start.3
  2.7 0.8 %copy-done.3 = f32[2,4,2,8,128]{4,3,2,1,0:T(8,128)S(1)} copy-done((f32[2,4,2,8,128]{4,3,2,1,0:T(8,128)S(1)}, f32[2,4,2,8,128]{4,3,2,1,0:T(8,128)}, u32[]{:S(2)}) %copy-start.3) | copy-done | bytes 65560
  3.5 0.7 %copy-done.4 = f32[2,4,256]{2,1,0:T(4,128)S(1)} copy-done((f32[2,4,256]{2,1,0:T(4,128)S(1)}, f32[2,4,256]{2,1,0:T(4,128)}, u32[]{:S(2)}) %copy-start.4) | copy-done | bytes 8216
  4.2 0.0 copy-start.6
  4.2 0.7 %copy-done.6 = s32[256]{0:T(256)S(1)} copy-done((s32[256]{0:T(256)S(1)}, s32[256]{0:T(256)}, u32[]{:S(2)}) %copy-start.6) | copy-done | bytes 1048
  4.9 0.9 %start.1 = (f32[2,4,2,8,128]{4,3,2,1,0:T(8,128)S(1)}, f32[2,4,2,8,128]{4,3,2,1,0:T(8,128)S(1)}, f32[2,24,8,128]{3,2,1,0:T(8,128)S(1)}, f32[2,24,8,128]{3,2,1,0:T...) custom-call(s32[1]{0:T(128)} %bitcast.pos, s32[1,256]{1,0:T(1,128)S(1)} %bitcast.3, ...), custom_call_target="tpu_custom_call" | custom-call | tf_op jit(solution)/shard_map/start/pallas_call | solution.py:303
  5.8 0.1 collective-permute-start
  5.9 0.7 %collective-permute-start.1 = (f32[2,24,8,128]{3,2,1,0:T(8,128)S(1)}, f32[2,24,8,128]{3,2,1,0:T(8,128)S(1)}, u32[]{:S(2)}, u32[]{:S(2)}) collective-permute-start(f32[2,24,8,128]{3,2,1,0:T(8,128)S(1)} %get-tuple-element.19.sent_cross), channel_id=1, source_target_pairs={{2,4},{4,2},{6,8},{8,6},{10,12},{12,10},{14,16},{16,14},{18,20},{2... | collective-permute-start | bytes 589832 | tf_op jit(solution)/shard_map/ppermute | solution.py:296
  6.6 0.7 %collective-permute-done.got_intra.block_intra = f32[2,24,8,128]{3,2,1,0:T(8,128)S(1)} collective-permute-done((f32[2,24,8,128]{3,2,1,0:T(8,128)S(1)}, f32[2,24,8,128]{3,2,1,0:T(8,128)S(1)}, u32[]{:S(2)}, u32[]{:S(2)}) %collective-permute-start) | collective-permute-done | bytes 196640 | tf_op jit(solution)/shard_map/ppermute | solution.py:296
  7.3 0.0 collective-permute-done.1.got_cross.block_cross
  7.3 0.4 middle.1
  7.8 6.1 %collective-permute-start.2 = (f32[2,8,8,128]{3,2,1,0:T(8,128)S(1)}, f32[2,8,8,128]{3,2,1,0:T(8,128)S(1)}, u32[]{:S(2)}, u32[]{:S(2)}) collective-permute-start(f32[2,8,8,128]{3,2,1,0:T(8,128)S(1)} %get-tuple-element.23.sent_intra), channel_id=1, source_target_pairs={{0,2},{2,0},{4,6},{6,4},{8,10},{10,8},{12,14},{14,12},{16,18},{18,... | collective-permute-start | bytes 196616 | tf_op jit(solution)/shard_map/ppermute | solution.py:296
  13.9 0.7 %collective-permute-start.3 = (f32[2,8,8,128]{3,2,1,0:T(8,128)S(1)}, f32[2,8,8,128]{3,2,1,0:T(8,128)S(1)}, u32[]{:S(2)}, u32[]{:S(2)}) collective-permute-start(f32[2,8,8,128]{3,2,1,0:T(8,128)S(1)} %get-tuple-element.24.sent_cross), channel_id=1, source_target_pairs={{2,4},{4,2},{6,8},{8,6},{10,12},{12,10},{14,16},{16,14},{18,20},{2... | collective-permute-start | bytes 196616 | tf_op jit(solution)/shard_map/ppermute | solution.py:296
  14.6 0.0 copy-start
  14.6 2.2 %copy-done = bf16[2,4,2,8,128,128]{5,4,3,2,1,0:T(8,128)(2,1)S(1)} copy-done((bf16[2,4,2,8,128,128]{5,4,3,2,1,0:T(8,128)(2,1)S(1)}, bf16[2,4,2,8,128,128]{5,4,3,2,1,0:T(8,128)(2,1)}, u32[]{:S(2)}) %copy-start) | copy-done | bytes 4194328
  16.8 0.0 copy-start.5
  16.8 0.7 %copy-done.5 = s32[2,8,128]{2,1,0:T(8,128)S(1)} copy-done((s32[2,8,128]{2,1,0:T(8,128)S(1)}, s32[2,8,128]{2,1,0:T(8,128)}, u32[]{:S(2)}) %copy-start.5) | copy-done | bytes 8216
  17.5 0.9 %select.1 = (bf16[512,2048]{1,0:T(8,128)(2,1)S(1)}, bf16[2,4,2,8,128,128]{5,4,3,2,1,0:T(8,128)(2,1)S(1)}) custom-call(s32[1]{0:T(128)} %bitcast.pos, s32[2,8,128]{2,1,0:T(8,128)S(1)} %copy-done.5, bf16[2,4,2,8,128,128]{5,4,3,2,1,0:T(8,128)(2,1)S(1)} %copy-done), custom_call_target="tpu_custom_call" | custom-call | tf_op jit(solution)/shard_map/select/pallas_call | solution.py:320
  18.4 0.0 collective-permute-done.2.got_intra
  18.4 0.0 collective-permute-done.3.got_cross
  18.4 3.5 %end.1 = (f32[2,4,2,8,128]{4,3,2,1,0:T(8,128)}, f32[256,128]{1,0:T(8,128)S(1)}, f32[256,128]{1,0:T(8,128)S(1)}) custom-call(s32[1]{0:T(128)} %bitcast.pos, f32[2,4,2,8,128]{4,3,2,1,0:T(8,128)S(1)} %get-tuple-element.16.src, f32[2,4,2,8,128]{4,3,2,1,0:T(8,128)S(1)} %get-tuple-element.22.nxt, f32[2,24,8,128]{3,2,1,0:T(8,128)S(1)} %collective-permute-done.got_intra.block_intra, ...), custom_call_target="tpu_custom_call" | custom-call | tf_op jit(solution)/shard_map/end/pallas_call | solution.py:338
  22.0 3.4 %collective-permute-start.4 = (f32[256,128]{1,0:T(8,128)S(1)}, f32[256,128]{1,0:T(8,128)S(1)}, u32[]{:S(2)}, u32[]{:S(2)}) collective-permute-start(f32[256,128]{1,0:T(8,128)S(1)} %get-tuple-element.29), channel_id=1, source_target_pairs={{0,2},{2,0},{4,6},{6,4},{8,10},{10,8},{12,14},{14,12},{16,18},{18,... | collective-permute-start | bytes 393224 | tf_op jit(solution)/shard_map/ppermute | solution.py:349
  25.3 1.0 %collective-permute-done.4 = f32[256,128]{1,0:T(8,128)S(1)} collective-permute-done((f32[256,128]{1,0:T(8,128)S(1)}, f32[256,128]{1,0:T(8,128)S(1)}, u32[]{:S(2)}, u32[]{:S(2)}) %collective-permute-start.4) | collective-permute-done | bytes 131104 | tf_op jit(solution)/shard_map/ppermute | solution.py:349
  26.3 28.0 %all_to_all.5 = f32[64,4,128]{2,1,0:T(4,128)S(1)} all-to-all(f32[64,4,128]{2,1,0:T(4,128)S(1)} %bitcast.4), channel_id=1, replica_groups={{0,4,8,12,16,20,24,28,32,36,40,44,48,52,56,60,64,68,72,76,80,84,88,92,9..., dimensions={0} | all-to-all | bytes 262144 | tf_op jit(solution)/shard_map/all_to_all | solution.py:351
  54.4 0.1 reduce_sum.9
  54.4 0.4 collective-permute-start.5
  54.9 4.8 %collective-permute-done.5 = f32[4,128]{1,0:T(4,128)S(1)} collective-permute-done((f32[4,128]{1,0:T(4,128)S(1)}, f32[4,128]{1,0:T(4,128)S(1)}, u32[]{:S(2)}, u32[]{:S(2)}) %collective-permute-start.5) | collective-permute-done | bytes 2080 | tf_op jit(solution)/shard_map/ppermute | solution.py:355
  59.6 0.6 add.7
  (2 shorter events, 0.0 us)
Async XLA Ops:
  0.6 1.1 %copy-start.1 = (bf16[2,6,4,4,2,8,128]{6,5,4,3,2,1,0:T(8,128)(2,1)S(1)}, bf16[2,6,4,4,2,8,128]{6,5,4,3,2,1,0:T(8,128)(2,1)}, u32[]{:S(2)}) copy-start(bf16[2,6,4,4,2,8,128]{6,5,4,3,2,1,0:T(8,128)(2,1)} %cpl_in.1) | copy-start | bytes 2359300
  1.8 0.9 %copy-start.2 = (bf16[2,4,4,2,8,128]{5,4,3,2,1,0:T(8,128)(2,1)S(1)}, bf16[2,4,4,2,8,128]{5,4,3,2,1,0:T(8,128)(2,1)}, u32[]{:S(2)}) copy-start(bf16[2,4,4,2,8,128]{5,4,3,2,1,0:T(8,128)(2,1)} %inv_in.1) | copy-start | bytes 393220
  2.7 0.8 %copy-start.3 = (f32[2,4,2,8,128]{4,3,2,1,0:T(8,128)S(1)}, f32[2,4,2,8,128]{4,3,2,1,0:T(8,128)}, u32[]{:S(2)}) copy-start(f32[2,4,2,8,128]{4,3,2,1,0:T(8,128)} %later_in.1) | copy-start | bytes 196612
  3.5 0.7 %copy-start.4 = (f32[2,4,256]{2,1,0:T(4,128)S(1)}, f32[2,4,256]{2,1,0:T(4,128)}, u32[]{:S(2)}) copy-start(f32[2,4,256]{2,1,0:T(4,128)} %misfit_in.1) | copy-start | bytes 24580
  4.2 0.7 %copy-start.6 = (s32[256]{0:T(256)S(1)}, s32[256]{0:T(256)}, u32[]{:S(2)}) copy-start(s32[256]{0:T(256)} %param.11) | copy-start | bytes 3076
  5.8 1.5 %collective-permute-start = (f32[2,24,8,128]{3,2,1,0:T(8,128)S(1)}, f32[2,24,8,128]{3,2,1,0:T(8,128)S(1)}, u32[]{:S(2)}, u32[]{:S(2)}) collective-permute-start(f32[2,24,8,128]{3,2,1,0:T(8,128)S(1)} %get-tuple-element.18.sent_intra), channel_id=1, source_target_pairs={{0,2},{2,0},{4,6},{6,4},{8,10},{10,8},{12,14},{14,12},{16,18},{18,... | collective-permute-start | bytes 589832 | tf_op jit(solution)/shard_map/ppermute | solution.py:296
  5.9 1.4 %collective-permute-start.1 = (f32[2,24,8,128]{3,2,1,0:T(8,128)S(1)}, f32[2,24,8,128]{3,2,1,0:T(8,128)S(1)}, u32[]{:S(2)}, u32[]{:S(2)}) collective-permute-start(f32[2,24,8,128]{3,2,1,0:T(8,128)S(1)} %get-tuple-element.19.sent_cross), channel_id=1, source_target_pairs={{2,4},{4,2},{6,8},{8,6},{10,12},{12,10},{14,16},{16,14},{18,20},{2... | collective-permute-start | bytes 589832 | tf_op jit(solution)/shard_map/ppermute | solution.py:296
  7.8 10.6 %collective-permute-start.2 = (f32[2,8,8,128]{3,2,1,0:T(8,128)S(1)}, f32[2,8,8,128]{3,2,1,0:T(8,128)S(1)}, u32[]{:S(2)}, u32[]{:S(2)}) collective-permute-start(f32[2,8,8,128]{3,2,1,0:T(8,128)S(1)} %get-tuple-element.23.sent_intra), channel_id=1, source_target_pairs={{0,2},{2,0},{4,6},{6,4},{8,10},{10,8},{12,14},{14,12},{16,18},{18,... | collective-permute-start | bytes 196616 | tf_op jit(solution)/shard_map/ppermute | solution.py:296
  13.9 4.5 %collective-permute-start.3 = (f32[2,8,8,128]{3,2,1,0:T(8,128)S(1)}, f32[2,8,8,128]{3,2,1,0:T(8,128)S(1)}, u32[]{:S(2)}, u32[]{:S(2)}) collective-permute-start(f32[2,8,8,128]{3,2,1,0:T(8,128)S(1)} %get-tuple-element.24.sent_cross), channel_id=1, source_target_pairs={{2,4},{4,2},{6,8},{8,6},{10,12},{12,10},{14,16},{16,14},{18,20},{2... | collective-permute-start | bytes 196616 | tf_op jit(solution)/shard_map/ppermute | solution.py:296
  14.6 2.2 %copy-start = (bf16[2,4,2,8,128,128]{5,4,3,2,1,0:T(8,128)(2,1)S(1)}, bf16[2,4,2,8,128,128]{5,4,3,2,1,0:T(8,128)(2,1)}, u32[]{:S(2)}) copy-start(bf16[2,4,2,8,128,128]{5,4,3,2,1,0:T(8,128)(2,1)} %sens_in.1) | copy-start | bytes 12582916
  16.8 0.7 %copy-start.5 = (s32[2,8,128]{2,1,0:T(8,128)S(1)}, s32[2,8,128]{2,1,0:T(8,128)}, u32[]{:S(2)}) copy-start(s32[2,8,128]{2,1,0:T(8,128)} %bmap_in.1) | copy-start | bytes 24580
  22.0 4.3 %collective-permute-start.4 = (f32[256,128]{1,0:T(8,128)S(1)}, f32[256,128]{1,0:T(8,128)S(1)}, u32[]{:S(2)}, u32[]{:S(2)}) collective-permute-start(f32[256,128]{1,0:T(8,128)S(1)} %get-tuple-element.29), channel_id=1, source_target_pairs={{0,2},{2,0},{4,6},{6,4},{8,10},{10,8},{12,14},{14,12},{16,18},{18,... | collective-permute-start | bytes 393224 | tf_op jit(solution)/shard_map/ppermute | solution.py:349
  54.4 5.2 %collective-permute-start.5 = (f32[4,128]{1,0:T(4,128)S(1)}, f32[4,128]{1,0:T(4,128)S(1)}, u32[]{:S(2)}, u32[]{:S(2)}) collective-permute-start(f32[4,128]{1,0:T(4,128)S(1)} %reduce_sum.9), channel_id=1, source_target_pairs={{0,1},{1,0},{2,3},{3,2},{4,5},{5,4},{6,7},{7,6},{8,9},{9,8},{10,11... | collective-permute-start | bytes 6152 | tf_op jit(solution)/shard_map/ppermute | solution.py:355

commit v3 on v2

--- a/solution.py
+++ b/solution.py
@@ -124,24 +124,18 @@
     return total.reshape(shape)
 
 
-def start_kernel(
-    pos, wells_in, misfit_in, later_in, cpl_in, inv_in, src, nxt_out, intra_out, cross_out, cpl, inv, wells, misfit, sems
-):
+def place_kernel(pos, out):
+    out[0] = pos[0]
+
+
+def start_kernel(pos, wells, misfit, later, cpl_in, inv_in, src, nxt_out, intra_out, cross_out, cpl, inv):
     shape = src.shape
     members, unk, planes = shape[:3]
-    moves = ((wells_in, wells), (misfit_in, misfit), (later_in, src), (inv_in, inv), (cpl_in, cpl))
-    copies = [pltpu.make_async_copy(a, b, sems.at[i]) for i, (a, b) in enumerate(moves)]
-    for c in copies:
-        c.start()
+    cpl[...] = cpl_in[...]
+    inv[...] = inv_in[...]
     even = pos[0] % 2 == 0
     count = planes * shape[3] * shape[4]
-    copies[0].wait()
-    copies[1].wait()
-    extra = injected(wells, misfit, pos[0] * count, shape)
-    copies[2].wait()
-    src[...] = src[...] + extra
-    copies[3].wait()
-    copies[4].wait()
+    src[...] = later[...] + injected(wells, misfit, pos[0] * count, shape)
     for m in range(members):
         s = [src[m, u] for u in range(unk)]
         a = apply_inverse(inv, m, s)
@@ -206,11 +200,7 @@
     return middle_kernel
 
 
-def select_kernel(pos, bmap_in, sens_in, onehot, sens, bmap, sems):
-    fetch = pltpu.make_async_copy(sens_in, sens, sems.at[0])
-    small = pltpu.make_async_copy(bmap_in, bmap, sems.at[1])
-    small.start()
-    fetch.start()
+def select_kernel(pos, bmap, onehot):
     rows, lanes = bmap.shape[1:]
     nblk = onehot.shape[0]
     core = pos[0] % 2
@@ -219,11 +209,9 @@
     parity = jnp.where(slot < half_rows, core, 1 - core)
     within = jnp.where(slot < half_rows, slot, slot - half_rows)
     block = (within // BLK_DEV * 2 + parity) * BLK_DEV + within % BLK_DEV
-    small.wait()
     for g in range(bmap.shape[0] * rows):
         row = bmap[g // rows, g % rows : g % rows + 1, :]
         onehot[:, g * lanes : (g + 1) * lanes] = (block == row).astype(F32).astype(BF16)
-    fetch.wait()
 
 
 def make_end(last, nblk):
@@ -278,6 +266,10 @@
     return pltpu.CompilerParams(vmem_limit_bytes=mib * MIB)
 
 
+def busy(flops):
+    return pl.CostEstimate(flops=flops, bytes_accessed=0, transcendentals=0)
+
+
 def shaped(*shape):
     return jax.ShapeDtypeStruct(shape, F32)
 
@@ -298,6 +290,15 @@
     field = shaped(members, unk, planes, rows, lanes)
     first_size = 2 * unk + unk * unk
     wells = well_cells.reshape(1, -1)
+    with jax.named_scope("place"):
+        pos = pl.pallas_call(
+            place_kernel,
+            out_shape=jax.ShapeDtypeStruct((1,), jnp.int32),
+            in_specs=[SM],
+            out_specs=SM,
+            compiler_params=room(1),
+            cost_estimate=busy(1 << 31),
+        )(pos)
     dma = pltpu.SemaphoreType.DMA
     with jax.named_scope("start"):
         src, nxt, intra, cross, cpl, inv = pl.pallas_call(
@@ -310,21 +311,20 @@
                 jax.ShapeDtypeStruct(coupling.shape, BF16),
                 jax.ShapeDtypeStruct(diag_inverse.shape, BF16),
             ),
-            in_specs=[SM] + [HB] * 5,
+            in_specs=[SM] + [VM] * 5,
             out_specs=(VM,) * 6,
-            scratch_shapes=[pltpu.VMEM(wells.shape, jnp.int32), pltpu.VMEM(well_misfit.shape, F32), dma((5,))],
             compiler_params=room(6),
         )(pos, wells, well_misfit, later_adjoint, coupling, diag_inverse)
     got_intra, got_cross = exchange(intra, cross)
     with jax.named_scope("select"):
-        onehot, sens = pl.pallas_call(
+        onehot = pl.pallas_call(
             select_kernel,
-            out_shape=(jax.ShapeDtypeStruct((nblk, count), BF16), jax.ShapeDtypeStruct(sensitivity.shape, BF16)),
-            in_specs=[SM, HB, HB],
-            out_specs=(VM, VM),
-            scratch_shapes=[pltpu.VMEM(block_map.shape, jnp.int32), dma((2,))],
-            compiler_params=room(10),
-        )(pos, block_map, sensitivity)
+            out_shape=jax.ShapeDtypeStruct((nblk, count), BF16),
+            in_specs=[SM, VM],
+            out_specs=VM,
+            compiler_params=room(6),
+            cost_estimate=busy(1 << 24),
+        )(pos, block_map)
     with jax.named_scope("middle"):
         nxt2, intra2, cross2 = pl.pallas_call(
             make_middle(ranks - 1),
@@ -343,7 +343,7 @@
             scratch_shapes=[pltpu.VMEM(field.shape, F32), pltpu.VMEM((count, 2 * params), BF16), dma((1,))],
             compiler_params=room(16),
         )(
-            pos, src, nxt2, got_intra, got_cross, intra2, cross2, got_intra2, got_cross2, cpl, inv, onehot, sens,
+            pos, src, nxt2, got_intra, got_cross, intra2, cross2, got_intra2, got_cross2, cpl, inv, onehot, sensitivity,
         )
     chips = ranks // 2
     half = mine + lax.ppermute(other, "cells", intra_pairs)

time: 60.6 us -> 59.1 us (0.975)
  local copies, waits for them, and re-layouts: 7.12 us -> 0.66 us
  Pallas kernels: 5.82 us -> 8.25 us
  blocking collectives: 28 us -> 29.9 us
  starting transfers between devices: 11.3 us -> 12 us
    unnamed x14, local copies, waits for them, and re-layouts: 7.12 us -> 0.66 us
    all_to_all x1, blocking collectives: 28 us -> 29.9 us  [body(): lax.all_to_all(half.reshape(chips, BLK_DEV, params), 'cells', 0, 0, tiled...]
    pallas_call x1 -> x2, Pallas kernels: 0.92 us -> 1.72 us  [the longest x1 1.21 us: body(): pl.pallas_call(select_kernel, out_shape=jax.ShapeDtypeStruct((nblk, count...]
    ppermute x1, starting transfers between devices: 3.36 us -> 4.05 us  [body(): half = mine + lax.ppermute(other, 'cells', intra_pairs)]
where the time goes in v3:
time: 59.1 us; the launch traced here: 58.8 us
  blocking collectives  29.9 us (51%)
  starting transfers between devices  12 us (20%)
  Pallas kernels  8.25 us (14%)
  waiting for transfers between devices  6.49 us (11%)
  between operations  0.79 us (1%)
  other arithmetic  0.67 us (1%)
  local copies, waits for them, and re-layouts  0.66 us (1%)
    all_to_all x1, blocking collectives, body(): lax.all_to_all(half.reshape(chips, BLK_DEV, params), 'cells', 0, 0, tiled...  29.9 us
    ppermute x2, starting transfers between devices, exchange(): lax.ppermute(intra, 'cells', intra_pairs)  6.22 us
    ppermute x1, waiting for transfers between devices, body(): gradient = owned + lax.ppermute(owned, 'ens', [(0, 1), (1, 0)])  4.75 us
    pallas_call x1, Pallas kernels, body(): pl.pallas_call(make_end(ranks - 1, nblk), out_shape=(field, shaped(nblk /...  4.1 us
    ppermute x1, starting transfers between devices, body(): half = mine + lax.ppermute(other, 'cells', intra_pairs)  4.05 us
    pallas_call x1, Pallas kernels, body(): pl.pallas_call(start_kernel, out_shape=(field, field, shaped(members, fir...  1.42 us
    ppermute x2, starting transfers between devices, exchange(): lax.ppermute(cross, 'cells', cross_pairs)  1.33 us
    pallas_call x1, Pallas kernels, body(): pl.pallas_call(select_kernel, out_shape=jax.ShapeDtypeStruct((nblk, count...  1.21 us
  transfers between devices with their start and end apart: 6, of which 3 were waited for; matrix products, arithmetic and copies ran while one was open for 0% of the time, Pallas kernels for 2%

profile of v3, /device:TPU:16, one launch (start us, length us, event | category | flops | bytes accessed | tf_op | source)
XLA Modules:
  0.0 58.8 jit_solution(9096516019104487620)
XLA Ops:
  0.6 0.0 copy-start.4
  0.6 0.0 copy-start.6
  0.7 0.0 copy-start.2
  0.7 0.0 copy-start.1
  0.7 0.0 copy-start.3
  0.7 0.0 copy-start.5
  0.7 0.5 place.1.pos
  1.2 0.0 copy-start
  1.2 0.1 copy-done.4
  1.3 0.0 copy-done.6
  1.3 0.2 copy-done.2
  1.6 0.3 copy-done.1
  1.9 0.0 copy-done.3
  1.9 1.4 %start.1 = (f32[2,4,2,8,128]{4,3,2,1,0:T(8,128)S(1)}, f32[2,4,2,8,128]{4,3,2,1,0:T(8,128)S(1)}, f32[2,24,8,128]{3,2,1,0:T(8,128)S(1)}, f32[2,24,8,128]{3,2,1,0:T...) custom-call(s32[1]{0:T(128)} %place.1.pos, s32[1,256]{1,0:T(1,128)S(1)} %bitcast.3, ...), custom_call_target="tpu_custom_call" | custom-call | tf_op jit(solution)/shard_map/start/pallas_call | solution.py:304
  3.3 0.1 collective-permute-start
  3.4 0.7 %collective-permute-start.1 = (f32[2,24,8,128]{3,2,1,0:T(8,128)S(1)}, f32[2,24,8,128]{3,2,1,0:T(8,128)S(1)}, u32[]{:S(2)}, u32[]{:S(2)}) collective-permute-start(f32[2,24,8,128]{3,2,1,0:T(8,128)S(1)} %get-tuple-element.17.sent_cross), channel_id=1, source_target_pairs={{2,4},{4,2},{6,8},{8,6},{10,12},{12,10},{14,16},{16,14},{18,20},{2... | collective-permute-start | bytes 589832 | tf_op jit(solution)/shard_map/ppermute | solution.py:288
  4.1 0.7 %collective-permute-done.got_intra.block_intra = f32[2,24,8,128]{3,2,1,0:T(8,128)S(1)} collective-permute-done((f32[2,24,8,128]{3,2,1,0:T(8,128)S(1)}, f32[2,24,8,128]{3,2,1,0:T(8,128)S(1)}, u32[]{:S(2)}, u32[]{:S(2)}) %collective-permute-start) | collective-permute-done | bytes 196640 | tf_op jit(solution)/shard_map/ppermute | solution.py:288
  4.8 0.0 collective-permute-done.1.got_cross.block_cross
  4.8 1.0 %middle.1 = (f32[2,4,2,8,128]{4,3,2,1,0:T(8,128)S(1)}, f32[2,8,8,128]{3,2,1,0:T(8,128)S(1)}, f32[2,8,8,128]{3,2,1,0:T(8,128)S(1)}) custom-call(s32[1]{0:T(128)} %place.1.pos, f32[2,4,2,8,128]{4,3,2,1,0:T(8,128)S(1)} %get-tuple-element.14.src, f32[2,4,2,8,128]{4,3,2,1,0:T(8,128)S(1)} %get-tuple-element.15.nxt, ...), custom_call_target="tpu_custom_call" | custom-call | tf_op jit(solution)/shard_map/middle/pallas_call | solution.py:329
  5.8 6.1 %collective-permute-start.2 = (f32[2,8,8,128]{3,2,1,0:T(8,128)S(1)}, f32[2,8,8,128]{3,2,1,0:T(8,128)S(1)}, u32[]{:S(2)}, u32[]{:S(2)}) collective-permute-start(f32[2,8,8,128]{3,2,1,0:T(8,128)S(1)} %get-tuple-element.21.sent_intra), channel_id=1, source_target_pairs={{0,2},{2,0},{4,6},{6,4},{8,10},{10,8},{12,14},{14,12},{16,18},{18,... | collective-permute-start | bytes 196616 | tf_op jit(solution)/shard_map/ppermute | solution.py:288
  12.0 0.7 %collective-permute-start.3 = (f32[2,8,8,128]{3,2,1,0:T(8,128)S(1)}, f32[2,8,8,128]{3,2,1,0:T(8,128)S(1)}, u32[]{:S(2)}, u32[]{:S(2)}) collective-permute-start(f32[2,8,8,128]{3,2,1,0:T(8,128)S(1)} %get-tuple-element.22.sent_cross), channel_id=1, source_target_pairs={{2,4},{4,2},{6,8},{8,6},{10,12},{12,10},{14,16},{16,14},{18,20},{2... | collective-permute-start | bytes 196616 | tf_op jit(solution)/shard_map/ppermute | solution.py:288
  12.6 1.2 %select.1.onehot = bf16[512,2048]{1,0:T(8,128)(2,1)S(1)} custom-call(s32[1]{0:T(128)} %place.1.pos, s32[2,8,128]{2,1,0:T(8,128)S(1)} %copy-done.5), custom_call_target="tpu_custom_call" | custom-call | flops 16777216 | tf_op jit(solution)/shard_map/select/pallas_call | solution.py:320
  13.9 0.0 collective-permute-done.2.got_intra
  13.9 0.0 collective-permute-done.3.got_cross
  13.9 4.1 %end.1 = (f32[2,4,2,8,128]{4,3,2,1,0:T(8,128)}, f32[256,128]{1,0:T(8,128)S(1)}, f32[256,128]{1,0:T(8,128)S(1)}) custom-call(s32[1]{0:T(128)} %place.1.pos, f32[2,4,2,8,128]{4,3,2,1,0:T(8,128)S(1)} %get-tuple-element.14.src, f32[2,4,2,8,128]{4,3,2,1,0:T(8,128)S(1)} %get-tuple-element.20.nxt, f32[2,24,8,128]{3,2,1,0:T(8,128)S(1)} %collective-permute-done.got_intra.block_intra, ...), custom_call_target="tpu_custom_call" | custom-call | tf_op jit(solution)/shard_map/end/pallas_call | solution.py:338
  18.0 4.0 %collective-permute-start.4 = (f32[256,128]{1,0:T(8,128)S(1)}, f32[256,128]{1,0:T(8,128)S(1)}, u32[]{:S(2)}, u32[]{:S(2)}) collective-permute-start(f32[256,128]{1,0:T(8,128)S(1)} %get-tuple-element.25), channel_id=1, source_target_pairs={{0,2},{2,0},{4,6},{6,4},{8,10},{10,8},{12,14},{14,12},{16,18},{18,... | collective-permute-start | bytes 393224 | tf_op jit(solution)/shard_map/ppermute | solution.py:349
  22.0 1.0 %collective-permute-done.4 = f32[256,128]{1,0:T(8,128)S(1)} collective-permute-done((f32[256,128]{1,0:T(8,128)S(1)}, f32[256,128]{1,0:T(8,128)S(1)}, u32[]{:S(2)}, u32[]{:S(2)}) %collective-permute-start.4) | collective-permute-done | bytes 131104 | tf_op jit(solution)/shard_map/ppermute | solution.py:349
  23.0 29.9 %all_to_all.5 = f32[64,4,128]{2,1,0:T(4,128)S(1)} all-to-all(f32[64,4,128]{2,1,0:T(4,128)S(1)} %bitcast.4), channel_id=1, replica_groups={{0,4,8,12,16,20,24,28,32,36,40,44,48,52,56,60,64,68,72,76,80,84,88,92,9..., dimensions={0} | all-to-all | bytes 262144 | tf_op jit(solution)/shard_map/all_to_all | solution.py:351
  53.0 0.1 reduce_sum.9
  53.1 0.4 collective-permute-start.5
  53.5 4.8 %collective-permute-done.5 = f32[4,128]{1,0:T(4,128)S(1)} collective-permute-done((f32[4,128]{1,0:T(4,128)S(1)}, f32[4,128]{1,0:T(4,128)S(1)}, u32[]{:S(2)}, u32[]{:S(2)}) %collective-permute-start.5) | collective-permute-done | bytes 2080 | tf_op jit(solution)/shard_map/ppermute | solution.py:355
  58.2 0.6 add.7
  (3 shorter events, 0.0 us)
Async XLA Ops:
  0.6 0.7 %copy-start.4 = (f32[2,4,256]{2,1,0:T(4,128)S(1)}, f32[2,4,256]{2,1,0:T(4,128)}, u32[]{:S(2)}) copy-start(f32[2,4,256]{2,1,0:T(4,128)} %misfit.1) | copy-start | bytes 24580
  0.6 0.7 %copy-start.6 = (s32[256]{0:T(256)S(1)}, s32[256]{0:T(256)}, u32[]{:S(2)}) copy-start(s32[256]{0:T(256)} %param.11) | copy-start | bytes 3076
  0.7 0.9 %copy-start.2 = (bf16[2,4,4,2,8,128]{5,4,3,2,1,0:T(8,128)(2,1)S(1)}, bf16[2,4,4,2,8,128]{5,4,3,2,1,0:T(8,128)(2,1)}, u32[]{:S(2)}) copy-start(bf16[2,4,4,2,8,128]{5,4,3,2,1,0:T(8,128)(2,1)} %inv_in.1) | copy-start | bytes 393220
  0.7 1.2 %copy-start.1 = (bf16[2,6,4,4,2,8,128]{6,5,4,3,2,1,0:T(8,128)(2,1)S(1)}, bf16[2,6,4,4,2,8,128]{6,5,4,3,2,1,0:T(8,128)(2,1)}, u32[]{:S(2)}) copy-start(bf16[2,6,4,4,2,8,128]{6,5,4,3,2,1,0:T(8,128)(2,1)} %cpl_in.1) | copy-start | bytes 2359300
  0.7 1.2 %copy-start.3 = (f32[2,4,2,8,128]{4,3,2,1,0:T(8,128)S(1)}, f32[2,4,2,8,128]{4,3,2,1,0:T(8,128)}, u32[]{:S(2)}) copy-start(f32[2,4,2,8,128]{4,3,2,1,0:T(8,128)} %later.1) | copy-start | bytes 196612
  0.7 12.0 %copy-start.5 = (s32[2,8,128]{2,1,0:T(8,128)S(1)}, s32[2,8,128]{2,1,0:T(8,128)}, u32[]{:S(2)}) copy-start(s32[2,8,128]{2,1,0:T(8,128)} %bmap.1) | copy-start | bytes 24580
  1.2 12.7 %copy-start = (bf16[2,4,2,8,128,128]{5,4,3,2,1,0:T(8,128)(2,1)S(1)}, bf16[2,4,2,8,128,128]{5,4,3,2,1,0:T(8,128)(2,1)}, u32[]{:S(2)}) copy-start(bf16[2,4,2,8,128,128]{5,4,3,2,1,0:T(8,128)(2,1)} %sens.1) | copy-start | bytes 12582916
  3.3 1.5 %collective-permute-start = (f32[2,24,8,128]{3,2,1,0:T(8,128)S(1)}, f32[2,24,8,128]{3,2,1,0:T(8,128)S(1)}, u32[]{:S(2)}, u32[]{:S(2)}) collective-permute-start(f32[2,24,8,128]{3,2,1,0:T(8,128)S(1)} %get-tuple-element.16.sent_intra), channel_id=1, source_target_pairs={{0,2},{2,0},{4,6},{6,4},{8,10},{10,8},{12,14},{14,12},{16,18},{18,... | collective-permute-start | bytes 589832 | tf_op jit(solution)/shard_map/ppermute | solution.py:288
  3.4 1.4 %collective-permute-start.1 = (f32[2,24,8,128]{3,2,1,0:T(8,128)S(1)}, f32[2,24,8,128]{3,2,1,0:T(8,128)S(1)}, u32[]{:S(2)}, u32[]{:S(2)}) collective-permute-start(f32[2,24,8,128]{3,2,1,0:T(8,128)S(1)} %get-tuple-element.17.sent_cross), channel_id=1, source_target_pairs={{2,4},{4,2},{6,8},{8,6},{10,12},{12,10},{14,16},{16,14},{18,20},{2... | collective-permute-start | bytes 589832 | tf_op jit(solution)/shard_map/ppermute | solution.py:288
  5.8 8.0 %collective-permute-start.2 = (f32[2,8,8,128]{3,2,1,0:T(8,128)S(1)}, f32[2,8,8,128]{3,2,1,0:T(8,128)S(1)}, u32[]{:S(2)}, u32[]{:S(2)}) collective-permute-start(f32[2,8,8,128]{3,2,1,0:T(8,128)S(1)} %get-tuple-element.21.sent_intra), channel_id=1, source_target_pairs={{0,2},{2,0},{4,6},{6,4},{8,10},{10,8},{12,14},{14,12},{16,18},{18,... | collective-permute-start | bytes 196616 | tf_op jit(solution)/shard_map/ppermute | solution.py:288
  12.0 1.9 %collective-permute-start.3 = (f32[2,8,8,128]{3,2,1,0:T(8,128)S(1)}, f32[2,8,8,128]{3,2,1,0:T(8,128)S(1)}, u32[]{:S(2)}, u32[]{:S(2)}) collective-permute-start(f32[2,8,8,128]{3,2,1,0:T(8,128)S(1)} %get-tuple-element.22.sent_cross), channel_id=1, source_target_pairs={{2,4},{4,2},{6,8},{8,6},{10,12},{12,10},{14,16},{16,14},{18,20},{2... | collective-permute-start | bytes 196616 | tf_op jit(solution)/shard_map/ppermute | solution.py:288
  18.0 5.0 %collective-permute-start.4 = (f32[256,128]{1,0:T(8,128)S(1)}, f32[256,128]{1,0:T(8,128)S(1)}, u32[]{:S(2)}, u32[]{:S(2)}) collective-permute-start(f32[256,128]{1,0:T(8,128)S(1)} %get-tuple-element.25), channel_id=1, source_target_pairs={{0,2},{2,0},{4,6},{6,4},{8,10},{10,8},{12,14},{14,12},{16,18},{18,... | collective-permute-start | bytes 393224 | tf_op jit(solution)/shard_map/ppermute | solution.py:349
  53.1 5.2 %collective-permute-start.5 = (f32[4,128]{1,0:T(4,128)S(1)}, f32[4,128]{1,0:T(4,128)S(1)}, u32[]{:S(2)}, u32[]{:S(2)}) collective-permute-start(f32[4,128]{1,0:T(4,128)S(1)} %reduce_sum.9), channel_id=1, source_target_pairs={{0,1},{1,0},{2,3},{3,2},{4,5},{5,4},{6,7},{7,6},{8,9},{9,8},{10,11... | collective-permute-start | bytes 6152 | tf_op jit(solution)/shard_map/ppermute | solution.py:355

commit v4 on v3

--- a/solution.py
+++ b/solution.py
@@ -124,11 +124,11 @@
     return total.reshape(shape)
 
 
-def place_kernel(pos, out):
-    out[0] = pos[0]
-
-
-def start_kernel(pos, wells, misfit, later, cpl_in, inv_in, src, nxt_out, intra_out, cross_out, cpl, inv):
+def first_kernel(out):
+    out[...] = jnp.zeros_like(out)
+
+
+def start_kernel(pos, _, wells, misfit, later, cpl_in, inv_in, src, nxt_out, intra_out, cross_out, cpl, inv):
     shape = src.shape
     members, unk, planes = shape[:3]
     cpl[...] = cpl_in[...]
@@ -290,16 +290,15 @@
     field = shaped(members, unk, planes, rows, lanes)
     first_size = 2 * unk + unk * unk
     wells = well_cells.reshape(1, -1)
-    with jax.named_scope("place"):
-        pos = pl.pallas_call(
-            place_kernel,
-            out_shape=jax.ShapeDtypeStruct((1,), jnp.int32),
-            in_specs=[SM],
-            out_specs=SM,
+    dma = pltpu.SemaphoreType.DMA
+    with jax.named_scope("first"):
+        token = pl.pallas_call(
+            first_kernel,
+            out_shape=shaped(8, 128),
+            out_specs=VM,
             compiler_params=room(1),
             cost_estimate=busy(1 << 31),
-        )(pos)
-    dma = pltpu.SemaphoreType.DMA
+        )()
     with jax.named_scope("start"):
         src, nxt, intra, cross, cpl, inv = pl.pallas_call(
             start_kernel,
@@ -311,10 +310,10 @@
                 jax.ShapeDtypeStruct(coupling.shape, BF16),
                 jax.ShapeDtypeStruct(diag_inverse.shape, BF16),
             ),
-            in_specs=[SM] + [VM] * 5,
+            in_specs=[SM] + [VM] * 6,
             out_specs=(VM,) * 6,
             compiler_params=room(6),
-        )(pos, wells, well_misfit, later_adjoint, coupling, diag_inverse)
+        )(pos, token, wells, well_misfit, later_adjoint, coupling, diag_inverse)
     got_intra, got_cross = exchange(intra, cross)
     with jax.named_scope("select"):
         onehot = pl.pallas_call(

time: 59.1 us -> 57 us (0.964)
  Pallas kernels: 8.25 us -> 5.19 us
  starting transfers between devices: 12 us -> 12.6 us
    pallas_call x1, Pallas kernels: 1.42 us -> 0.55 us  [body(): pl.pallas_call(start_kernel, out_shape=(field, field, shaped(members, fir...]
  transfers between devices with their start and end apart: 6 -> 6, of which waited for: 3 -> 3; matrix products, arithmetic and copies ran while one was open for 0% -> 0% of each run, Pallas kernels for 2% -> 1%
where the time goes in v4:
time: 57 us; the launch traced here: 56.8 us
  blocking collectives  29.9 us (52%)
  starting transfers between devices  12.6 us (22%)
  waiting for transfers between devices  6.5 us (11%)
  Pallas kernels  5.19 us (9%)
  local copies, waits for them, and re-layouts  1.17 us (2%)
  between operations  0.8 us (1%)
  other arithmetic  0.67 us (1%)
    all_to_all x1, blocking collectives, body(): lax.all_to_all(half.reshape(chips, BLK_DEV, params), 'cells', 0, 0, tiled...  29.9 us
    ppermute x2, starting transfers between devices, exchange(): lax.ppermute(intra, 'cells', intra_pairs)  6.22 us
    ppermute x1, waiting for transfers between devices, body(): gradient = owned + lax.ppermute(owned, 'ens', [(0, 1), (1, 0)])  4.75 us
    ppermute x1, starting transfers between devices, body(): half = mine + lax.ppermute(other, 'cells', intra_pairs)  4.6 us
    pallas_call x1, Pallas kernels, body(): pl.pallas_call(make_end(ranks - 1, nblk), out_shape=(field, shaped(nblk /...  3.54 us
    ppermute x2, starting transfers between devices, exchange(): lax.ppermute(cross, 'cells', cross_pairs)  1.33 us
    unnamed x14, local copies, waits for them, and re-layouts  1.17 us
  transfers between devices with their start and end apart: 6, of which 3 were waited for; matrix products, arithmetic and copies ran while one was open for 0% of the time, Pallas kernels for 1%

profile of v4, /device:TPU:16, one launch (start us, length us, event | category | flops | bytes accessed | tf_op | source)
XLA Modules:
  0.0 56.8 jit_solution(567916629420951834)
XLA Ops:
  0.6 0.0 copy-start.4
  0.6 0.0 copy-start.6
  0.7 0.0 copy-start.2
  0.7 0.0 copy-start.1
  0.7 0.0 copy-start.3
  0.7 0.0 copy-start.5
  0.7 0.0 copy-start
  0.7 0.6 %copy-done.4 = f32[2,4,256]{2,1,0:T(4,128)S(1)} copy-done((f32[2,4,256]{2,1,0:T(4,128)S(1)}, f32[2,4,256]{2,1,0:T(4,128)}, u32[]{:S(2)}) %copy-start.4) | copy-done | bytes 8216
  1.3 0.0 copy-done.6
  1.3 0.2 copy-done.2
  1.6 0.3 copy-done.1
  1.9 0.0 copy-done.3
  1.9 0.5 start.1
  2.4 0.1 collective-permute-start
  2.5 0.7 %collective-permute-start.1 = (f32[2,24,8,128]{3,2,1,0:T(8,128)S(1)}, f32[2,24,8,128]{3,2,1,0:T(8,128)S(1)}, u32[]{:S(2)}, u32[]{:S(2)}) collective-permute-start(f32[2,24,8,128]{3,2,1,0:T(8,128)S(1)} %get-tuple-element.17.sent_cross), channel_id=1, source_target_pairs={{2,4},{4,2},{6,8},{8,6},{10,12},{12,10},{14,16},{16,14},{18,20},{2... | collective-permute-start | bytes 589832 | tf_op jit(solution)/shard_map/ppermute | solution.py:288
  3.2 0.7 %collective-permute-done.got_intra.block_intra = f32[2,24,8,128]{3,2,1,0:T(8,128)S(1)} collective-permute-done((f32[2,24,8,128]{3,2,1,0:T(8,128)S(1)}, f32[2,24,8,128]{3,2,1,0:T(8,128)S(1)}, u32[]{:S(2)}, u32[]{:S(2)}) %collective-permute-start) | collective-permute-done | bytes 196640 | tf_op jit(solution)/shard_map/ppermute | solution.py:288
  4.0 0.0 collective-permute-done.1.got_cross.block_cross
  4.0 0.4 middle.1
  4.4 6.1 %collective-permute-start.2 = (f32[2,8,8,128]{3,2,1,0:T(8,128)S(1)}, f32[2,8,8,128]{3,2,1,0:T(8,128)S(1)}, u32[]{:S(2)}, u32[]{:S(2)}) collective-permute-start(f32[2,8,8,128]{3,2,1,0:T(8,128)S(1)} %get-tuple-element.21.sent_intra), channel_id=1, source_target_pairs={{0,2},{2,0},{4,6},{6,4},{8,10},{10,8},{12,14},{14,12},{16,18},{18,... | collective-permute-start | bytes 196616 | tf_op jit(solution)/shard_map/ppermute | solution.py:288
  10.5 0.7 %collective-permute-start.3 = (f32[2,8,8,128]{3,2,1,0:T(8,128)S(1)}, f32[2,8,8,128]{3,2,1,0:T(8,128)S(1)}, u32[]{:S(2)}, u32[]{:S(2)}) collective-permute-start(f32[2,8,8,128]{3,2,1,0:T(8,128)S(1)} %get-tuple-element.22.sent_cross), channel_id=1, source_target_pairs={{2,4},{4,2},{6,8},{8,6},{10,12},{12,10},{14,16},{16,14},{18,20},{2... | collective-permute-start | bytes 196616 | tf_op jit(solution)/shard_map/ppermute | solution.py:288
  11.2 0.0 copy-done.5
  11.2 0.6 %select.1.onehot = bf16[512,2048]{1,0:T(8,128)(2,1)S(1)} custom-call(s32[1]{0:T(128)} %bitcast.pos, s32[2,8,128]{2,1,0:T(8,128)S(1)} %copy-done.5), custom_call_target="tpu_custom_call" | custom-call | flops 16777216 | tf_op jit(solution)/shard_map/select/pallas_call | solution.py:319
  11.9 0.0 collective-permute-done.2.got_intra
  11.9 0.0 collective-permute-done.3.got_cross
  11.9 3.5 %end.1 = (f32[2,4,2,8,128]{4,3,2,1,0:T(8,128)}, f32[256,128]{1,0:T(8,128)S(1)}, f32[256,128]{1,0:T(8,128)S(1)}) custom-call(s32[1]{0:T(128)} %bitcast.pos, f32[2,4,2,8,128]{4,3,2,1,0:T(8,128)S(1)} %get-tuple-element.14.src, f32[2,4,2,8,128]{4,3,2,1,0:T(8,128)S(1)} %get-tuple-element.20.nxt, f32[2,24,8,128]{3,2,1,0:T(8,128)S(1)} %collective-permute-done.got_intra.block_intra, ...), custom_call_target="tpu_custom_call" | custom-call | tf_op jit(solution)/shard_map/end/pallas_call | solution.py:337
  15.5 4.6 %collective-permute-start.4 = (f32[256,128]{1,0:T(8,128)S(1)}, f32[256,128]{1,0:T(8,128)S(1)}, u32[]{:S(2)}, u32[]{:S(2)}) collective-permute-start(f32[256,128]{1,0:T(8,128)S(1)} %get-tuple-element.25), channel_id=1, source_target_pairs={{0,2},{2,0},{4,6},{6,4},{8,10},{10,8},{12,14},{14,12},{16,18},{18,... | collective-permute-start | bytes 393224 | tf_op jit(solution)/shard_map/ppermute | solution.py:348
  20.0 1.0 %collective-permute-done.4 = f32[256,128]{1,0:T(8,128)S(1)} collective-permute-done((f32[256,128]{1,0:T(8,128)S(1)}, f32[256,128]{1,0:T(8,128)S(1)}, u32[]{:S(2)}, u32[]{:S(2)}) %collective-permute-start.4) | collective-permute-done | bytes 131104 | tf_op jit(solution)/shard_map/ppermute | solution.py:348
  21.1 29.9 %all_to_all.5 = f32[64,4,128]{2,1,0:T(4,128)S(1)} all-to-all(f32[64,4,128]{2,1,0:T(4,128)S(1)} %bitcast.4), channel_id=1, replica_groups={{0,4,8,12,16,20,24,28,32,36,40,44,48,52,56,60,64,68,72,76,80,84,88,92,9..., dimensions={0} | all-to-all | bytes 262144 | tf_op jit(solution)/shard_map/all_to_all | solution.py:350
  51.0 0.1 reduce_sum.9
  51.1 0.4 collective-permute-start.5
  51.5 4.8 %collective-permute-done.5 = f32[4,128]{1,0:T(4,128)S(1)} collective-permute-done((f32[4,128]{1,0:T(4,128)S(1)}, f32[4,128]{1,0:T(4,128)S(1)}, u32[]{:S(2)}, u32[]{:S(2)}) %collective-permute-start.5) | collective-permute-done | bytes 2080 | tf_op jit(solution)/shard_map/ppermute | solution.py:354
  56.2 0.6 %add.7 = f32[4,128]{1,0:T(4,128)} add(f32[4,128]{1,0:T(4,128)S(1)} %reduce_sum.9, f32[4,128]{1,0:T(4,128)S(1)} %collective-permute-done.5) | non-fusion elementwise | flops 512 | bytes 6144 | tf_op jit(solution)/shard_map/add | solution.py:354
  (3 shorter events, 0.0 us)
Async XLA Ops:
  0.6 0.7 %copy-start.4 = (f32[2,4,256]{2,1,0:T(4,128)S(1)}, f32[2,4,256]{2,1,0:T(4,128)}, u32[]{:S(2)}) copy-start(f32[2,4,256]{2,1,0:T(4,128)} %misfit.1) | copy-start | bytes 24580
  0.6 0.7 %copy-start.6 = (s32[256]{0:T(256)S(1)}, s32[256]{0:T(256)}, u32[]{:S(2)}) copy-start(s32[256]{0:T(256)} %param.11) | copy-start | bytes 3076
  0.7 0.9 %copy-start.2 = (bf16[2,4,4,2,8,128]{5,4,3,2,1,0:T(8,128)(2,1)S(1)}, bf16[2,4,4,2,8,128]{5,4,3,2,1,0:T(8,128)(2,1)}, u32[]{:S(2)}) copy-start(bf16[2,4,4,2,8,128]{5,4,3,2,1,0:T(8,128)(2,1)} %inv_in.1) | copy-start | bytes 393220
  0.7 1.2 %copy-start.1 = (bf16[2,6,4,4,2,8,128]{6,5,4,3,2,1,0:T(8,128)(2,1)S(1)}, bf16[2,6,4,4,2,8,128]{6,5,4,3,2,1,0:T(8,128)(2,1)}, u32[]{:S(2)}) copy-start(bf16[2,6,4,4,2,8,128]{6,5,4,3,2,1,0:T(8,128)(2,1)} %cpl_in.1) | copy-start | bytes 2359300
  0.7 1.2 %copy-start.3 = (f32[2,4,2,8,128]{4,3,2,1,0:T(8,128)S(1)}, f32[2,4,2,8,128]{4,3,2,1,0:T(8,128)}, u32[]{:S(2)}) copy-start(f32[2,4,2,8,128]{4,3,2,1,0:T(8,128)} %later.1) | copy-start | bytes 196612
  0.7 10.5 %copy-start.5 = (s32[2,8,128]{2,1,0:T(8,128)S(1)}, s32[2,8,128]{2,1,0:T(8,128)}, u32[]{:S(2)}) copy-start(s32[2,8,128]{2,1,0:T(8,128)} %bmap.1) | copy-start | bytes 24580
  0.7 11.2 %copy-start = (bf16[2,4,2,8,128,128]{5,4,3,2,1,0:T(8,128)(2,1)S(1)}, bf16[2,4,2,8,128,128]{5,4,3,2,1,0:T(8,128)(2,1)}, u32[]{:S(2)}) copy-start(bf16[2,4,2,8,128,128]{5,4,3,2,1,0:T(8,128)(2,1)} %sens.1) | copy-start | bytes 12582916
  2.4 1.5 %collective-permute-start = (f32[2,24,8,128]{3,2,1,0:T(8,128)S(1)}, f32[2,24,8,128]{3,2,1,0:T(8,128)S(1)}, u32[]{:S(2)}, u32[]{:S(2)}) collective-permute-start(f32[2,24,8,128]{3,2,1,0:T(8,128)S(1)} %get-tuple-element.16.sent_intra), channel_id=1, source_target_pairs={{0,2},{2,0},{4,6},{6,4},{8,10},{10,8},{12,14},{14,12},{16,18},{18,... | collective-permute-start | bytes 589832 | tf_op jit(solution)/shard_map/ppermute | solution.py:288
  2.5 1.4 %collective-permute-start.1 = (f32[2,24,8,128]{3,2,1,0:T(8,128)S(1)}, f32[2,24,8,128]{3,2,1,0:T(8,128)S(1)}, u32[]{:S(2)}, u32[]{:S(2)}) collective-permute-start(f32[2,24,8,128]{3,2,1,0:T(8,128)S(1)} %get-tuple-element.17.sent_cross), channel_id=1, source_target_pairs={{2,4},{4,2},{6,8},{8,6},{10,12},{12,10},{14,16},{16,14},{18,20},{2... | collective-permute-start | bytes 589832 | tf_op jit(solution)/shard_map/ppermute | solution.py:288
  4.4 7.5 %collective-permute-start.2 = (f32[2,8,8,128]{3,2,1,0:T(8,128)S(1)}, f32[2,8,8,128]{3,2,1,0:T(8,128)S(1)}, u32[]{:S(2)}, u32[]{:S(2)}) collective-permute-start(f32[2,8,8,128]{3,2,1,0:T(8,128)S(1)} %get-tuple-element.21.sent_intra), channel_id=1, source_target_pairs={{0,2},{2,0},{4,6},{6,4},{8,10},{10,8},{12,14},{14,12},{16,18},{18,... | collective-permute-start | bytes 196616 | tf_op jit(solution)/shard_map/ppermute | solution.py:288
  10.5 1.3 %collective-permute-start.3 = (f32[2,8,8,128]{3,2,1,0:T(8,128)S(1)}, f32[2,8,8,128]{3,2,1,0:T(8,128)S(1)}, u32[]{:S(2)}, u32[]{:S(2)}) collective-permute-start(f32[2,8,8,128]{3,2,1,0:T(8,128)S(1)} %get-tuple-element.22.sent_cross), channel_id=1, source_target_pairs={{2,4},{4,2},{6,8},{8,6},{10,12},{12,10},{14,16},{16,14},{18,20},{2... | collective-permute-start | bytes 196616 | tf_op jit(solution)/shard_map/ppermute | solution.py:288
  15.5 5.6 %collective-permute-start.4 = (f32[256,128]{1,0:T(8,128)S(1)}, f32[256,128]{1,0:T(8,128)S(1)}, u32[]{:S(2)}, u32[]{:S(2)}) collective-permute-start(f32[256,128]{1,0:T(8,128)S(1)} %get-tuple-element.25), channel_id=1, source_target_pairs={{0,2},{2,0},{4,6},{6,4},{8,10},{10,8},{12,14},{14,12},{16,18},{18,... | collective-permute-start | bytes 393224 | tf_op jit(solution)/shard_map/ppermute | solution.py:348
  51.1 5.2 %collective-permute-start.5 = (f32[4,128]{1,0:T(4,128)S(1)}, f32[4,128]{1,0:T(4,128)S(1)}, u32[]{:S(2)}, u32[]{:S(2)}) collective-permute-start(f32[4,128]{1,0:T(4,128)S(1)} %reduce_sum.9), channel_id=1, source_target_pairs={{0,1},{1,0},{2,3},{3,2},{4,5},{5,4},{6,7},{7,6},{8,9},{9,8},{10,11... | collective-permute-start | bytes 6152 | tf_op jit(solution)/shard_map/ppermute | solution.py:354

commit v5 on v4

--- a/solution.py
+++ b/solution.py
@@ -149,29 +149,38 @@
             cross_out[m, j] = jnp.where(even, down[j], up[j])
 
 
-def incoming(pos, last, m, unk, blocks, sent_intra, sent_cross, got_intra, got_cross):
+def incoming(pos, last, m, unk, near, far):
     even = pos[0] % 2 == 0
     has_cross = (pos[0] != 0) & (pos[0] != last)
-    out = []
     sides = []
-    for sent, got, block in ((sent_intra, got_intra, blocks[0]), (sent_cross, got_cross, blocks[1])):
-        first = [got[m, v] for v in range(unk)]
+    for sent, got, block in (near, far):
+        first = [got(m, v) for v in range(unk)]
         second = []
         for v in range(unk):
-            total = got[m, unk + v]
+            total = got(m, unk + v)
             for w in range(unk):
-                total = total - block[m, 2 * unk + w * unk + v] * sent[m, w]
+                total = total - block(m, 2 * unk + w * unk + v) * sent(m, w)
             second.append(total)
         sides.append((first, second))
+    out = []
     for n in range(2):
         low, high = [], []
         for v in range(unk):
-            near = sides[0][n][v]
-            far = jnp.where(has_cross, sides[1][n][v], 0.0)
-            low.append(jnp.where(even, far, near))
-            high.append(jnp.where(even, near, far))
+            near_v = sides[0][n][v]
+            far_v = jnp.where(has_cross, sides[1][n][v], 0.0)
+            low.append(jnp.where(even, far_v, near_v))
+            high.append(jnp.where(even, near_v, far_v))
         out.append([jnp.stack([lo, hi], axis=0) for lo, hi in zip(low, high)])
     return out
+
+
+def reader(ref):
+    return lambda m, j: ref[m, j]
+
+
+def either(pos, if_even, if_odd):
+    even = pos[0] % 2 == 0
+    return lambda m, j: jnp.where(even, if_even[m, j], if_odd[m, j])
 
 
 def finish_two(cpl, inv, m, src, nxt, arrived):
@@ -180,24 +189,54 @@
     return apply_inverse(inv, m, [s - b - p for s, b, p in zip(src, inner, arrived[1])])
 
 
-def make_middle(last):
-    def middle_kernel(pos, src, nxt, sent_intra, sent_cross, got_intra, got_cross, cpl, inv, nxt_out, intra_out, cross_out):
-        members, unk = src.shape[:2]
-        even = pos[0] % 2 == 0
-        for m in range(members):
-            arrived = incoming(
-                pos, last, m, unk, (got_intra, got_cross), sent_intra, sent_cross, got_intra, got_cross
-            )
-            s = [src[m, u] for u in range(unk)]
-            a = finish_two(cpl, inv, m, s, [nxt[m, u] for u in range(unk)], arrived)
-            ahead, up, down = two_sweep_payload(cpl, inv, m, s, a)
-            for u in range(unk):
-                nxt_out[m, u] = ahead[u]
-            for j in range(len(up)):
-                intra_out[m, j] = jnp.where(even, up[j], down[j])
-                cross_out[m, j] = jnp.where(even, down[j], up[j])
-
-    return middle_kernel
+def advance(pos, last, src, nxt, sent_near, sent_far, got_near, got_far, cpl, inv, nxt_out, near_out, far_out):
+    members, unk = src.shape[:2]
+    even = pos[0] % 2 == 0
+    near = (reader(sent_near), reader(got_near), reader(got_near))
+    far = (reader(sent_far), reader(got_far), reader(got_far))
+    for m in range(members):
+        arrived = incoming(pos, last, m, unk, near, far)
+        s = [src[m, u] for u in range(unk)]
+        a = finish_two(cpl, inv, m, s, [nxt[m, u] for u in range(unk)], arrived)
+        ahead, up, down = two_sweep_payload(cpl, inv, m, s, a)
+        for u in range(unk):
+            nxt_out[m, u] = ahead[u]
+        for j in range(len(up)):
+            near_out[m, j] = jnp.where(even, up[j], down[j])
+            far_out[m, j] = jnp.where(even, down[j], up[j])
+
+
+def make_even_middle(last):
+    def even_middle(*refs):
+        pos, outs = refs[0], refs[9:]
+
+        @pl.when(pos[0] % 2 == 0)
+        def _():
+            advance(pos, last, *refs[1:9], *outs)
+
+        @pl.when(pos[0] % 2 == 1)
+        def _():
+            for out in outs:
+                out[...] = jnp.zeros_like(out)
+
+    return even_middle
+
+
+def make_odd_middle(last):
+    def odd_middle(*refs):
+        pos, (nxt_even, near_even), outs = refs[0], refs[9:11], refs[11:]
+
+        @pl.when(pos[0] % 2 == 1)
+        def _():
+            advance(pos, last, *refs[1:9], *outs)
+
+        @pl.when(pos[0] % 2 == 0)
+        def _():
+            outs[0][...] = nxt_even[...]
+            outs[1][...] = near_even[...]
+            outs[2][...] = jnp.zeros_like(outs[2])
+
+    return odd_middle
 
 
 def select_kernel(pos, bmap, onehot):
@@ -216,17 +255,19 @@
 
 def make_end(last, nblk):
     def end_kernel(
-        pos, src, nxt, block_intra, block_cross, sent_intra, sent_cross, got_intra, got_cross, cpl, inv, onehot, sens,
-        adj_out, mine_out, other_out, adj, grads, sems,
+        pos, src, nxt, block_near, block_even, block_odd, sent_near, sent_even, sent_odd, got_near, got_even, got_odd,
+        cpl, inv, onehot, sens, adj_out, mine_out, other_out, adj, grads, sems,
     ):
         members, unk, planes, rows, lanes = src.shape
         params = sens.shape[-1]
         groups = planes * rows
         half_rows = nblk // 2
+        near = (reader(sent_near), reader(got_near), reader(block_near))
+        far = (
+            either(pos, sent_even, sent_odd), either(pos, got_even, got_odd), either(pos, block_even, block_odd),
+        )
         for m in range(members):
-            arrived = incoming(
-                pos, last, m, unk, (block_intra, block_cross), sent_intra, sent_cross, got_intra, got_cross
-            )
+            arrived = incoming(pos, last, m, unk, near, far)
             a = finish_two(
                 cpl, inv, m, [src[m, u] for u in range(unk)], [nxt[m, u] for u in range(unk)], arrived
             )
@@ -282,10 +323,8 @@
     nblk = ranks * BLK_DEV
     pos = lax.axis_index("cells").astype(jnp.int32).reshape(1)
     intra_pairs = [(i, i ^ 1) for i in range(ranks)]
-    cross_pairs = [(i, i + 1 if i % 2 else i - 1) for i in range(1, ranks - 1)] + [(0, 0), (ranks - 1, ranks - 1)]
-
-    def exchange(intra, cross):
-        return lax.ppermute(intra, "cells", intra_pairs), lax.ppermute(cross, "cells", cross_pairs)
+    up_pairs = [(i, i + 1) for i in range(1, ranks - 1, 2)]
+    down_pairs = [(i + 1, i) for i in range(1, ranks - 1, 2)]
 
     field = shaped(members, unk, planes, rows, lanes)
     first_size = 2 * unk + unk * unk
@@ -300,7 +339,7 @@
             cost_estimate=busy(1 << 31),
         )()
     with jax.named_scope("start"):
-        src, nxt, intra, cross, cpl, inv = pl.pallas_call(
+        src, nxt, near, far, cpl, inv = pl.pallas_call(
             start_kernel,
             out_shape=(
                 field,
@@ -314,7 +353,9 @@
             out_specs=(VM,) * 6,
             compiler_params=room(6),
         )(pos, token, wells, well_misfit, later_adjoint, coupling, diag_inverse)
-    got_intra, got_cross = exchange(intra, cross)
+    got_near = lax.ppermute(near, "cells", intra_pairs)
+    got_up = lax.ppermute(far, "cells", up_pairs)
+    got_down = lax.ppermute(far, "cells", down_pairs)
     with jax.named_scope("select"):
         onehot = pl.pallas_call(
             select_kernel,
@@ -324,25 +365,37 @@
             compiler_params=room(6),
             cost_estimate=busy(1 << 24),
         )(pos, block_map)
-    with jax.named_scope("middle"):
-        nxt2, intra2, cross2 = pl.pallas_call(
-            make_middle(ranks - 1),
-            out_shape=(field, shaped(members, 2 * unk, rows, lanes), shaped(members, 2 * unk, rows, lanes)),
+    wide = shaped(members, 2 * unk, rows, lanes)
+    with jax.named_scope("even"):
+        nxt_even, near_even, far_even = pl.pallas_call(
+            make_even_middle(ranks - 1),
+            out_shape=(field, wide, wide),
             in_specs=[SM] + [VM] * 8,
             out_specs=(VM, VM, VM),
             compiler_params=room(6),
-        )(pos, src, nxt, intra, cross, got_intra, got_cross, cpl, inv)
-    got_intra2, got_cross2 = exchange(intra2, cross2)
+        )(pos, src, nxt, near, far, got_near, got_up, cpl, inv)
+    got_down2 = lax.ppermute(far_even, "cells", down_pairs)
+    with jax.named_scope("odd"):
+        nxt2, near2, far_odd = pl.pallas_call(
+            make_odd_middle(ranks - 1),
+            out_shape=(field, wide, wide),
+            in_specs=[SM] + [VM] * 10,
+            out_specs=(VM, VM, VM),
+            compiler_params=room(6),
+        )(pos, src, nxt, near, far, got_near, got_down, cpl, inv, nxt_even, near_even)
+    got_near2 = lax.ppermute(near2, "cells", intra_pairs)
+    got_up2 = lax.ppermute(far_odd, "cells", up_pairs)
     with jax.named_scope("end"):
         adjoint, mine, other = pl.pallas_call(
             make_end(ranks - 1, nblk),
             out_shape=(field, shaped(nblk // 2, params), shaped(nblk // 2, params)),
-            in_specs=[SM] + [VM] * 12,
+            in_specs=[SM] + [VM] * 15,
             out_specs=(HB, VM, VM),
             scratch_shapes=[pltpu.VMEM(field.shape, F32), pltpu.VMEM((count, 2 * params), BF16), dma((1,))],
             compiler_params=room(16),
         )(
-            pos, src, nxt2, got_intra, got_cross, intra2, cross2, got_intra2, got_cross2, cpl, inv, onehot, sensitivity,
+            pos, src, nxt2, got_near, got_up, got_down, near2, far_even, far_odd, got_near2, got_up2, got_down2,
+            cpl, inv, onehot, sensitivity,
         )
     chips = ranks // 2
     half = mine + lax.ppermute(other, "cells", intra_pairs)

time: 57 us -> 54.9 us (0.963)
  blocking collectives: 29.9 us -> 24.9 us
  starting transfers between devices: 12.6 us -> 16.3 us
  waiting for transfers between devices: 6.5 us -> 5.53 us
    all_to_all x1, blocking collectives: 29.9 us -> 24.9 us  [body(): lax.all_to_all(half.reshape(chips, BLK_DEV, params), 'cells', 0, 0, tiled...]
    ppermute x4 -> x6, starting transfers between devices: 7.55 us -> 11.6 us  [the longest x1 8.87 us: body(): got_near2 = lax.ppermute(near2, 'cells', intra_pairs)]
    ppermute x4 -> x6, waiting for transfers between devices: 0.76 us -> 0.08 us  [the longest x1 0.07 us: body(): got_near = lax.ppermute(near, 'cells', intra_pairs)]
    ppermute x1, starting transfers between devices: 4.6 us -> 3.96 us  [body(): half = mine + lax.ppermute(other, 'cells', intra_pairs)]
  transfers between devices with their start and end apart: 6 -> 8, of which waited for: 3 -> 3; matrix products, arithmetic and copies ran while one was open for 0% -> 0% of each run, Pallas kernels for 1% -> 2%
where the time goes in v5:
time: 54.9 us; the launch traced here: 54.7 us
  blocking collectives  24.9 us (45%)
  starting transfers between devices  16.3 us (30%)
  waiting for transfers between devices  5.53 us (10%)
  Pallas kernels  5.27 us (10%)
  local copies, waits for them, and re-layouts  1.17 us (2%)
  between operations  0.84 us (2%)
  other arithmetic  0.67 us (1%)
    all_to_all x1, blocking collectives, body(): lax.all_to_all(half.reshape(chips, BLK_DEV, params), 'cells', 0, 0, tiled...  24.9 us
    ppermute x1, starting transfers between devices, body(): got_near2 = lax.ppermute(near2, 'cells', intra_pairs)  8.87 us
    ppermute x1, waiting for transfers between devices, body(): gradient = owned + lax.ppermute(owned, 'ens', [(0, 1), (1, 0)])  4.46 us
    ppermute x1, starting transfers between devices, body(): half = mine + lax.ppermute(other, 'cells', intra_pairs)  3.96 us
    pallas_call x1, Pallas kernels, body(): pl.pallas_call(make_end(ranks - 1, nblk), out_shape=(field, shaped(nblk /...  3.56 us
    unnamed x14, local copies, waits for them, and re-layouts  1.17 us
  transfers between devices with their start and end apart: 8, of which 3 were waited for; matrix products, arithmetic and copies ran while one was open for 0% of the time, Pallas kernels for 2%

profile of v5, /device:TPU:16, one launch (start us, length us, event | category | flops | bytes accessed | tf_op | source)
XLA Modules:
  0.0 54.7 jit_solution(7516619713115635624)
XLA Ops:
  0.6 0.0 copy-start.4
  0.6 0.0 copy-start.6
  0.7 0.0 copy-start.2
  0.7 0.0 copy-start.5
  0.7 0.0 copy-start
  0.7 0.6 %copy-done.4 = f32[2,4,256]{2,1,0:T(4,128)S(1)} copy-done((f32[2,4,256]{2,1,0:T(4,128)S(1)}, f32[2,4,256]{2,1,0:T(4,128)}, u32[]{:S(2)}) %copy-start.4) | copy-done | bytes 8216
  1.3 0.2 copy-done.2
  1.6 0.3 copy-done.1
  1.9 0.0 copy-done.3
  1.9 0.5 %start.1 = (f32[2,4,2,8,128]{4,3,2,1,0:T(8,128)S(1)}, f32[2,4,2,8,128]{4,3,2,1,0:T(8,128)S(1)}, f32[2,24,8,128]{3,2,1,0:T(8,128)S(1)}, f32[2,24,8,128]{3,2,1,0:T...) custom-call(s32[1]{0:T(128)} %bitcast.pos.refs_0_, ...), custom_call_target="tpu_custom_call" | custom-call | tf_op jit(solution)/shard_map/start/pallas_call | solution.py:342
  2.4 0.1 collective-permute-start
  2.5 0.7 %collective-permute-start.2 = (f32[2,24,8,128]{3,2,1,0:T(8,128)S(1)}, f32[2,24,8,128]{3,2,1,0:T(8,128)S(1)}, u32[]{:S(2)}, u32[]{:S(2)}) collective-permute-start(f32[2,24,8,128]{3,2,1,0:T(8,128)S(1)} %get-tuple-element.20.refs_4_), channel_id=1, source_target_pairs={{2,4},{6,8},{10,12},{14,16},{18,20},{22,24},{26,28},{30,32},{34,36... | collective-permute-start | bytes 589832 | tf_op jit(solution)/shard_map/ppermute | solution.py:357
  3.2 0.7 %collective-permute-start.1 = (f32[2,24,8,128]{3,2,1,0:T(8,128)S(1)}, f32[2,24,8,128]{3,2,1,0:T(8,128)S(1)}, u32[]{:S(2)}, u32[]{:S(2)}) collective-permute-start(f32[2,24,8,128]{3,2,1,0:T(8,128)S(1)} %get-tuple-element.20.refs_4_), channel_id=1, source_target_pairs={{4,2},{8,6},{12,10},{16,14},{20,18},{24,22},{28,26},{32,30},{36,34... | collective-permute-start | bytes 589832 | tf_op jit(solution)/shard_map/ppermute | solution.py:358
  3.9 0.1 collective-permute-done.refs_5_.block_near
  4.0 0.0 collective-permute-done.2.refs_6_.block_even
  4.0 0.5 even.1
  4.4 0.7 %collective-permute-start.5 = (f32[2,8,8,128]{3,2,1,0:T(8,128)S(1)}, f32[2,8,8,128]{3,2,1,0:T(8,128)S(1)}, u32[]{:S(2)}, u32[]{:S(2)}) collective-permute-start(f32[2,8,8,128]{3,2,1,0:T(8,128)S(1)} %get-tuple-element.27.sent_even), channel_id=1, source_target_pairs={{4,2},{8,6},{12,10},{16,14},{20,18},{24,22},{28,26},{32,30},{36,34... | collective-permute-start | bytes 196616 | tf_op jit(solution)/shard_map/ppermute | solution.py:377
  5.1 0.0 collective-permute-done.1.refs_6_.block_odd
  5.2 8.9 %collective-permute-start.3 = (f32[2,8,8,128]{3,2,1,0:T(8,128)S(1)}, f32[2,8,8,128]{3,2,1,0:T(8,128)S(1)}, u32[]{:S(2)}, u32[]{:S(2)}) collective-permute-start(f32[2,8,8,128]{3,2,1,0:T(8,128)S(1)} %get-tuple-element.26.sent_near), channel_id=1, source_target_pairs={{0,2},{2,0},{4,6},{6,4},{8,10},{10,8},{12,14},{14,12},{16,18},{18,... | collective-permute-start | bytes 196616 | tf_op jit(solution)/shard_map/ppermute | solution.py:386
  14.0 0.7 %collective-permute-start.4 = (f32[2,8,8,128]{3,2,1,0:T(8,128)S(1)}, f32[2,8,8,128]{3,2,1,0:T(8,128)S(1)}, u32[]{:S(2)}, u32[]{:S(2)}) collective-permute-start(f32[2,8,8,128]{3,2,1,0:T(8,128)S(1)} %get-tuple-element.28.sent_odd), channel_id=1, source_target_pairs={{2,4},{6,8},{10,12},{14,16},{18,20},{22,24},{26,28},{30,32},{34,36... | collective-permute-start | bytes 196616 | tf_op jit(solution)/shard_map/ppermute | solution.py:387
  14.7 0.6 %select.1.onehot = bf16[512,2048]{1,0:T(8,128)(2,1)S(1)} custom-call(s32[1]{0:T(128)} %bitcast.pos.refs_0_, s32[2,8,128]{2,1,0:T(8,128)S(1)} %copy-done.5), custom_call_target="tpu_custom_call" | custom-call | flops 16777216 | tf_op jit(solution)/shard_map/select/pallas_call | solution.py:360
  15.4 0.0 collective-permute-done.5.got_odd
  15.4 0.0 collective-permute-done.3.got_near
  15.4 0.0 collective-permute-done.4.got_even
  15.4 3.6 %end.1 = (f32[2,4,2,8,128]{4,3,2,1,0:T(8,128)}, f32[256,128]{1,0:T(8,128)S(1)}, f32[256,128]{1,0:T(8,128)S(1)}) custom-call(s32[1]{0:T(128)} %bitcast.pos.refs_0_, f32[2,4,2,8,128]{4,3,2,1,0:T(8,128)S(1)} %get-tuple-element.17.refs_1_.src, f32[2,4,2,8,128]{4,3,2,1,0:T(8,128)S(1)} %get-tuple-element.25.nxt, ...), custom_call_target="tpu_custom_call" | custom-call | tf_op jit(solution)/shard_map/end/pallas_call | solution.py:389
  19.0 4.0 %collective-permute-start.6 = (f32[256,128]{1,0:T(8,128)S(1)}, f32[256,128]{1,0:T(8,128)S(1)}, u32[]{:S(2)}, u32[]{:S(2)}) collective-permute-start(f32[256,128]{1,0:T(8,128)S(1)} %get-tuple-element.31), channel_id=1, source_target_pairs={{0,2},{2,0},{4,6},{6,4},{8,10},{10,8},{12,14},{14,12},{16,18},{18,... | collective-permute-start | bytes 393224 | tf_op jit(solution)/shard_map/ppermute | solution.py:401
  22.9 1.0 %collective-permute-done.6 = f32[256,128]{1,0:T(8,128)S(1)} collective-permute-done((f32[256,128]{1,0:T(8,128)S(1)}, f32[256,128]{1,0:T(8,128)S(1)}, u32[]{:S(2)}, u32[]{:S(2)}) %collective-permute-start.6) | collective-permute-done | bytes 131104 | tf_op jit(solution)/shard_map/ppermute | solution.py:401
  23.9 24.9 %all_to_all.5 = f32[64,4,128]{2,1,0:T(4,128)S(1)} all-to-all(f32[64,4,128]{2,1,0:T(4,128)S(1)} %bitcast.4), channel_id=1, replica_groups={{0,4,8,12,16,20,24,28,32,36,40,44,48,52,56,60,64,68,72,76,80,84,88,92,9..., dimensions={0} | all-to-all | bytes 262144 | tf_op jit(solution)/shard_map/all_to_all | solution.py:403
  48.8 0.1 reduce_sum.9
  48.9 0.7 %collective-permute-start.7 = (f32[4,128]{1,0:T(4,128)S(1)}, f32[4,128]{1,0:T(4,128)S(1)}, u32[]{:S(2)}, u32[]{:S(2)}) collective-permute-start(f32[4,128]{1,0:T(4,128)S(1)} %reduce_sum.9), channel_id=1, source_target_pairs={{0,1},{1,0},{2,3},{3,2},{4,5},{5,4},{6,7},{7,6},{8,9},{9,8},{10,11... | collective-permute-start | bytes 6152 | tf_op jit(solution)/shard_map/ppermute | solution.py:407
  49.6 4.5 %collective-permute-done.7 = f32[4,128]{1,0:T(4,128)S(1)} collective-permute-done((f32[4,128]{1,0:T(4,128)S(1)}, f32[4,128]{1,0:T(4,128)S(1)}, u32[]{:S(2)}, u32[]{:S(2)}) %collective-permute-start.7) | collective-permute-done | bytes 2080 | tf_op jit(solution)/shard_map/ppermute | solution.py:407
  54.1 0.6 %add.7 = f32[4,128]{1,0:T(4,128)} add(f32[4,128]{1,0:T(4,128)S(1)} %reduce_sum.9, f32[4,128]{1,0:T(4,128)S(1)} %collective-permute-done.7) | non-fusion elementwise | flops 512 | bytes 6144 | tf_op jit(solution)/shard_map/add | solution.py:407
  (8 shorter events, 0.1 us)
Async XLA Ops:
  0.6 0.7 %copy-start.4 = (f32[2,4,256]{2,1,0:T(4,128)S(1)}, f32[2,4,256]{2,1,0:T(4,128)}, u32[]{:S(2)}) copy-start(f32[2,4,256]{2,1,0:T(4,128)} %misfit.1) | copy-start | bytes 24580
  0.6 0.7 %copy-start.6 = (s32[256]{0:T(256)S(1)}, s32[256]{0:T(256)}, u32[]{:S(2)}) copy-start(s32[256]{0:T(256)} %param.11) | copy-start | bytes 3076
  0.7 0.9 %copy-start.2 = (bf16[2,4,4,2,8,128]{5,4,3,2,1,0:T(8,128)(2,1)S(1)}, bf16[2,4,4,2,8,128]{5,4,3,2,1,0:T(8,128)(2,1)}, u32[]{:S(2)}) copy-start(bf16[2,4,4,2,8,128]{5,4,3,2,1,0:T(8,128)(2,1)} %inv_in.1) | copy-start | bytes 393220
  0.7 1.2 %copy-start.1 = (bf16[2,6,4,4,2,8,128]{6,5,4,3,2,1,0:T(8,128)(2,1)S(1)}, bf16[2,6,4,4,2,8,128]{6,5,4,3,2,1,0:T(8,128)(2,1)}, u32[]{:S(2)}) copy-start(bf16[2,6,4,4,2,8,128]{6,5,4,3,2,1,0:T(8,128)(2,1)} %cpl_in.1) | copy-start | bytes 2359300
  0.7 1.2 %copy-start.3 = (f32[2,4,2,8,128]{4,3,2,1,0:T(8,128)S(1)}, f32[2,4,2,8,128]{4,3,2,1,0:T(8,128)}, u32[]{:S(2)}) copy-start(f32[2,4,2,8,128]{4,3,2,1,0:T(8,128)} %later.1) | copy-start | bytes 196612
  0.7 14.0 %copy-start.5 = (s32[2,8,128]{2,1,0:T(8,128)S(1)}, s32[2,8,128]{2,1,0:T(8,128)}, u32[]{:S(2)}) copy-start(s32[2,8,128]{2,1,0:T(8,128)} %bmap.1) | copy-start | bytes 24580
  0.7 14.7 %copy-start = (bf16[2,4,2,8,128,128]{5,4,3,2,1,0:T(8,128)(2,1)S(1)}, bf16[2,4,2,8,128,128]{5,4,3,2,1,0:T(8,128)(2,1)}, u32[]{:S(2)}) copy-start(bf16[2,4,2,8,128,128]{5,4,3,2,1,0:T(8,128)(2,1)} %sens.1) | copy-start | bytes 12582916
  2.4 1.5 %collective-permute-start = (f32[2,24,8,128]{3,2,1,0:T(8,128)S(1)}, f32[2,24,8,128]{3,2,1,0:T(8,128)S(1)}, u32[]{:S(2)}, u32[]{:S(2)}) collective-permute-start(f32[2,24,8,128]{3,2,1,0:T(8,128)S(1)} %get-tuple-element.19.refs_3_), channel_id=1, source_target_pairs={{0,2},{2,0},{4,6},{6,4},{8,10},{10,8},{12,14},{14,12},{16,18},{18,... | collective-permute-start | bytes 589832 | tf_op jit(solution)/shard_map/ppermute | solution.py:356
  2.5 1.4 %collective-permute-start.2 = (f32[2,24,8,128]{3,2,1,0:T(8,128)S(1)}, f32[2,24,8,128]{3,2,1,0:T(8,128)S(1)}, u32[]{:S(2)}, u32[]{:S(2)}) collective-permute-start(f32[2,24,8,128]{3,2,1,0:T(8,128)S(1)} %get-tuple-element.20.refs_4_), channel_id=1, source_target_pairs={{2,4},{6,8},{10,12},{14,16},{18,20},{22,24},{26,28},{30,32},{34,36... | collective-permute-start | bytes 589832 | tf_op jit(solution)/shard_map/ppermute | solution.py:357
  3.2 1.9 %collective-permute-start.1 = (f32[2,24,8,128]{3,2,1,0:T(8,128)S(1)}, f32[2,24,8,128]{3,2,1,0:T(8,128)S(1)}, u32[]{:S(2)}, u32[]{:S(2)}) collective-permute-start(f32[2,24,8,128]{3,2,1,0:T(8,128)S(1)} %get-tuple-element.20.refs_4_), channel_id=1, source_target_pairs={{4,2},{8,6},{12,10},{16,14},{20,18},{24,22},{28,26},{32,30},{36,34... | collective-permute-start | bytes 589832 | tf_op jit(solution)/shard_map/ppermute | solution.py:358
  4.4 10.9 %collective-permute-start.5 = (f32[2,8,8,128]{3,2,1,0:T(8,128)S(1)}, f32[2,8,8,128]{3,2,1,0:T(8,128)S(1)}, u32[]{:S(2)}, u32[]{:S(2)}) collective-permute-start(f32[2,8,8,128]{3,2,1,0:T(8,128)S(1)} %get-tuple-element.27.sent_even), channel_id=1, source_target_pairs={{4,2},{8,6},{12,10},{16,14},{20,18},{24,22},{28,26},{32,30},{36,34... | collective-permute-start | bytes 196616 | tf_op jit(solution)/shard_map/ppermute | solution.py:377
  5.2 10.2 %collective-permute-start.3 = (f32[2,8,8,128]{3,2,1,0:T(8,128)S(1)}, f32[2,8,8,128]{3,2,1,0:T(8,128)S(1)}, u32[]{:S(2)}, u32[]{:S(2)}) collective-permute-start(f32[2,8,8,128]{3,2,1,0:T(8,128)S(1)} %get-tuple-element.26.sent_near), channel_id=1, source_target_pairs={{0,2},{2,0},{4,6},{6,4},{8,10},{10,8},{12,14},{14,12},{16,18},{18,... | collective-permute-start | bytes 196616 | tf_op jit(solution)/shard_map/ppermute | solution.py:386
  14.0 1.4 %collective-permute-start.4 = (f32[2,8,8,128]{3,2,1,0:T(8,128)S(1)}, f32[2,8,8,128]{3,2,1,0:T(8,128)S(1)}, u32[]{:S(2)}, u32[]{:S(2)}) collective-permute-start(f32[2,8,8,128]{3,2,1,0:T(8,128)S(1)} %get-tuple-element.28.sent_odd), channel_id=1, source_target_pairs={{2,4},{6,8},{10,12},{14,16},{18,20},{22,24},{26,28},{30,32},{34,36... | collective-permute-start | bytes 196616 | tf_op jit(solution)/shard_map/ppermute | solution.py:387
  19.0 4.9 %collective-permute-start.6 = (f32[256,128]{1,0:T(8,128)S(1)}, f32[256,128]{1,0:T(8,128)S(1)}, u32[]{:S(2)}, u32[]{:S(2)}) collective-permute-start(f32[256,128]{1,0:T(8,128)S(1)} %get-tuple-element.31), channel_id=1, source_target_pairs={{0,2},{2,0},{4,6},{6,4},{8,10},{10,8},{12,14},{14,12},{16,18},{18,... | collective-permute-start | bytes 393224 | tf_op jit(solution)/shard_map/ppermute | solution.py:401
  48.9 5.2 %collective-permute-start.7 = (f32[4,128]{1,0:T(4,128)S(1)}, f32[4,128]{1,0:T(4,128)S(1)}, u32[]{:S(2)}, u32[]{:S(2)}) collective-permute-start(f32[4,128]{1,0:T(4,128)S(1)} %reduce_sum.9), channel_id=1, source_target_pairs={{0,1},{1,0},{2,3},{3,2},{4,5},{5,4},{6,7},{7,6},{8,9},{9,8},{10,11... | collective-permute-start | bytes 6152 | tf_op jit(solution)/shard_map/ppermute | solution.py:407

commit v6 on v5

--- a/solution.py
+++ b/solution.py
@@ -323,8 +323,8 @@
     nblk = ranks * BLK_DEV
     pos = lax.axis_index("cells").astype(jnp.int32).reshape(1)
     intra_pairs = [(i, i ^ 1) for i in range(ranks)]
-    up_pairs = [(i, i + 1) for i in range(1, ranks - 1, 2)]
-    down_pairs = [(i + 1, i) for i in range(1, ranks - 1, 2)]
+    up_pairs = [(i, (i + 1) % ranks) for i in range(ranks)]
+    down_pairs = [((i + 1) % ranks, i) for i in range(ranks)]
 
     field = shaped(members, unk, planes, rows, lanes)
     first_size = 2 * unk + unk * unk

time: 54.9 us -> 50.8 us (0.925)
  waiting for transfers between devices: 5.53 us -> 16.3 us
  blocking collectives: 24.9 us -> 15.5 us
  starting transfers between devices: 16.3 us -> 10.9 us
    all_to_all x1, blocking collectives: 24.9 us -> 15.5 us  [body(): lax.all_to_all(half.reshape(chips, BLK_DEV, params), 'cells', 0, 0, tiled...]
    ppermute x1, starting transfers between devices: 8.87 us -> 1 us  [body(): got_near2 = lax.ppermute(near2, 'cells', intra_pairs)]
    ppermute x1, starting transfers between devices: 0.67 us -> 8.38 us  [body(): got_down = lax.ppermute(far, 'cells', down_pairs)]
    ppermute x1, waiting for transfers between devices: 0.01 us -> 7.01 us  [body(): got_up2 = lax.ppermute(far_odd, 'cells', up_pairs)]
    ppermute x1, starting transfers between devices: 3.96 us -> 0.09 us  [body(): half = mine + lax.ppermute(other, 'cells', intra_pairs)]
    ppermute x1, waiting for transfers between devices: 0.01 us -> 3.35 us  [body(): got_up = lax.ppermute(far, 'cells', up_pairs)]
    ppermute x1, starting transfers between devices: 0.66 us -> 0.08 us  [body(): got_down2 = lax.ppermute(far_even, 'cells', down_pairs)]
    ppermute x1, starting transfers between devices: 0.65 us -> 0.09 us  [body(): got_up2 = lax.ppermute(far_odd, 'cells', up_pairs)]
  transfers between devices with their start and end apart: 8 -> 8, of which waited for: 3 -> 6; matrix products, arithmetic and copies ran while one was open for 0% -> 0% of each run, Pallas kernels for 2% -> 2%
where the time goes in v6:
time: 50.8 us; the launch traced here: 50.6 us
  waiting for transfers between devices  16.3 us (32%)
  blocking collectives  15.5 us (31%)
  starting transfers between devices  10.9 us (21%)
  Pallas kernels  5.25 us (10%)
  local copies, waits for them, and re-layouts  1.17 us (2%)
  between operations  0.79 us (2%)
  other arithmetic  0.67 us (1%)
    all_to_all x1, blocking collectives, body(): lax.all_to_all(half.reshape(chips, BLK_DEV, params), 'cells', 0, 0, tiled...  15.5 us
    ppermute x1, starting transfers between devices, body(): got_down = lax.ppermute(far, 'cells', down_pairs)  8.38 us
    ppermute x1, waiting for transfers between devices, body(): got_up2 = lax.ppermute(far_odd, 'cells', up_pairs)  7.01 us
    ppermute x1, waiting for transfers between devices, body(): gradient = owned + lax.ppermute(owned, 'ens', [(0, 1), (1, 0)])  4.46 us
    pallas_call x1, Pallas kernels, body(): pl.pallas_call(make_end(ranks - 1, nblk), out_shape=(field, shaped(nblk /...  3.55 us
    ppermute x1, waiting for transfers between devices, body(): got_up = lax.ppermute(far, 'cells', up_pairs)  3.35 us
    ppermute x1, waiting for transfers between devices, body(): half = mine + lax.ppermute(other, 'cells', intra_pairs)  1.33 us
    unnamed x14, local copies, waits for them, and re-layouts  1.17 us
  transfers between devices with their start and end apart: 8, of which 6 were waited for; matrix products, arithmetic and copies ran while one was open for 0% of the time, Pallas kernels for 2%

profile of v6, /device:TPU:16, one launch (start us, length us, event | category | flops | bytes accessed | tf_op | source)
XLA Modules:
  0.0 50.6 jit_solution(17972688110600123497)
XLA Ops:
  0.6 0.0 copy-start.4
  0.6 0.0 copy-start.6
  0.7 0.0 copy-start.2
  0.7 0.0 copy-start.5
  0.7 0.0 copy-start
  0.7 0.6 %copy-done.4 = f32[2,4,256]{2,1,0:T(4,128)S(1)} copy-done((f32[2,4,256]{2,1,0:T(4,128)S(1)}, f32[2,4,256]{2,1,0:T(4,128)}, u32[]{:S(2)}) %copy-start.4) | copy-done | bytes 8216
  1.3 0.2 copy-done.2
  1.6 0.3 copy-done.1
  1.9 0.5 %start.1 = (f32[2,4,2,8,128]{4,3,2,1,0:T(8,128)S(1)}, f32[2,4,2,8,128]{4,3,2,1,0:T(8,128)S(1)}, f32[2,24,8,128]{3,2,1,0:T(8,128)S(1)}, f32[2,24,8,128]{3,2,1,0:T...) custom-call(s32[1]{0:T(128)} %bitcast.pos.refs_0_, ...), custom_call_target="tpu_custom_call" | custom-call | tf_op jit(solution)/shard_map/start/pallas_call | solution.py:342
  2.4 0.1 collective-permute-start
  2.5 0.5 collective-permute-start.2
  3.0 8.4 %collective-permute-start.1 = (f32[2,24,8,128]{3,2,1,0:T(8,128)S(1)}, f32[2,24,8,128]{3,2,1,0:T(8,128)S(1)}, u32[]{:S(2)}, u32[]{:S(2)}) collective-permute-start(f32[2,24,8,128]{3,2,1,0:T(8,128)S(1)} %get-tuple-element.20.refs_4_), channel_id=1, source_target_pairs={{2,0},{4,2},{6,4},{8,6},{10,8},{12,10},{14,12},{16,14},{18,16},{20... | collective-permute-start | bytes 589832 | tf_op jit(solution)/shard_map/ppermute | solution.py:358
  11.4 0.0 collective-permute-done.refs_5_.block_near
  11.4 3.3 %collective-permute-done.2.refs_6_.block_even = f32[2,24,8,128]{3,2,1,0:T(8,128)S(1)} collective-permute-done((f32[2,24,8,128]{3,2,1,0:T(8,128)S(1)}, f32[2,24,8,128]{3,2,1,0:T(8,128)S(1)}, u32[]{:S(2)}, u32[]{:S(2)}) %collective-permute-start.2) | collective-permute-done | bytes 196640 | tf_op jit(solution)/shard_map/ppermute | solution.py:357
  14.8 0.5 even.1
  15.2 0.1 collective-permute-start.5
  15.3 0.0 collective-permute-done.1.refs_6_.block_odd
  15.4 1.0 %collective-permute-start.3 = (f32[2,8,8,128]{3,2,1,0:T(8,128)S(1)}, f32[2,8,8,128]{3,2,1,0:T(8,128)S(1)}, u32[]{:S(2)}, u32[]{:S(2)}) collective-permute-start(f32[2,8,8,128]{3,2,1,0:T(8,128)S(1)} %get-tuple-element.26.sent_near), channel_id=1, source_target_pairs={{0,2},{2,0},{4,6},{6,4},{8,10},{10,8},{12,14},{14,12},{16,18},{18,... | collective-permute-start | bytes 196616 | tf_op jit(solution)/shard_map/ppermute | solution.py:386
  16.4 0.1 collective-permute-start.4
  16.5 0.6 %select.1.onehot = bf16[512,2048]{1,0:T(8,128)(2,1)S(1)} custom-call(s32[1]{0:T(128)} %bitcast.pos.refs_0_, s32[2,8,128]{2,1,0:T(8,128)S(1)} %copy-done.5), custom_call_target="tpu_custom_call" | custom-call | flops 16777216 | tf_op jit(solution)/shard_map/select/pallas_call | solution.py:360
  17.1 0.1 collective-permute-done.5.got_odd
  17.2 0.1 collective-permute-done.3.got_near
  17.3 7.0 %collective-permute-done.4.got_even = f32[2,8,8,128]{3,2,1,0:T(8,128)S(1)} collective-permute-done((f32[2,8,8,128]{3,2,1,0:T(8,128)S(1)}, f32[2,8,8,128]{3,2,1,0:T(8,128)S(1)}, u32[]{:S(2)}, u32[]{:S(2)}) %collective-permute-start.4) | collective-permute-done | bytes 65568 | tf_op jit(solution)/shard_map/ppermute | solution.py:387
  24.3 0.0 copy-done
  24.3 3.6 %end.1 = (f32[2,4,2,8,128]{4,3,2,1,0:T(8,128)}, f32[256,128]{1,0:T(8,128)S(1)}, f32[256,128]{1,0:T(8,128)S(1)}) custom-call(s32[1]{0:T(128)} %bitcast.pos.refs_0_, f32[2,4,2,8,128]{4,3,2,1,0:T(8,128)S(1)} %get-tuple-element.17.refs_1_.src, f32[2,4,2,8,128]{4,3,2,1,0:T(8,128)S(1)} %get-tuple-element.25.nxt, ...), custom_call_target="tpu_custom_call" | custom-call | tf_op jit(solution)/shard_map/end/pallas_call | solution.py:389
  27.9 0.1 collective-permute-start.6
  28.0 1.3 %collective-permute-done.6 = f32[256,128]{1,0:T(8,128)S(1)} collective-permute-done((f32[256,128]{1,0:T(8,128)S(1)}, f32[256,128]{1,0:T(8,128)S(1)}, u32[]{:S(2)}, u32[]{:S(2)}) %collective-permute-start.6) | collective-permute-done | bytes 131104 | tf_op jit(solution)/shard_map/ppermute | solution.py:401
  29.3 15.5 %all_to_all.5 = f32[64,4,128]{2,1,0:T(4,128)S(1)} all-to-all(f32[64,4,128]{2,1,0:T(4,128)S(1)} %bitcast.4), channel_id=1, replica_groups={{0,4,8,12,16,20,24,28,32,36,40,44,48,52,56,60,64,68,72,76,80,84,88,92,9..., dimensions={0} | all-to-all | bytes 262144 | tf_op jit(solution)/shard_map/all_to_all | solution.py:403
  44.8 0.1 reduce_sum.9
  44.9 0.7 %collective-permute-start.7 = (f32[4,128]{1,0:T(4,128)S(1)}, f32[4,128]{1,0:T(4,128)S(1)}, u32[]{:S(2)}, u32[]{:S(2)}) collective-permute-start(f32[4,128]{1,0:T(4,128)S(1)} %reduce_sum.9), channel_id=1, source_target_pairs={{0,1},{1,0},{2,3},{3,2},{4,5},{5,4},{6,7},{7,6},{8,9},{9,8},{10,11... | collective-permute-start | bytes 6152 | tf_op jit(solution)/shard_map/ppermute | solution.py:407
  45.6 4.5 %collective-permute-done.7 = f32[4,128]{1,0:T(4,128)S(1)} collective-permute-done((f32[4,128]{1,0:T(4,128)S(1)}, f32[4,128]{1,0:T(4,128)S(1)}, u32[]{:S(2)}, u32[]{:S(2)}) %collective-permute-start.7) | collective-permute-done | bytes 2080 | tf_op jit(solution)/shard_map/ppermute | solution.py:407
  50.1 0.6 %add.7 = f32[4,128]{1,0:T(4,128)} add(f32[4,128]{1,0:T(4,128)S(1)} %reduce_sum.9, f32[4,128]{1,0:T(4,128)S(1)} %collective-permute-done.7) | non-fusion elementwise | flops 512 | bytes 6144 | tf_op jit(solution)/shard_map/add | solution.py:407
  (8 shorter events, 0.1 us)
Async XLA Ops:
  0.6 0.7 %copy-start.4 = (f32[2,4,256]{2,1,0:T(4,128)S(1)}, f32[2,4,256]{2,1,0:T(4,128)}, u32[]{:S(2)}) copy-start(f32[2,4,256]{2,1,0:T(4,128)} %misfit.1) | copy-start | bytes 24580
  0.6 0.7 %copy-start.6 = (s32[256]{0:T(256)S(1)}, s32[256]{0:T(256)}, u32[]{:S(2)}) copy-start(s32[256]{0:T(256)} %param.11) | copy-start | bytes 3076
  0.7 0.9 %copy-start.2 = (bf16[2,4,4,2,8,128]{5,4,3,2,1,0:T(8,128)(2,1)S(1)}, bf16[2,4,4,2,8,128]{5,4,3,2,1,0:T(8,128)(2,1)}, u32[]{:S(2)}) copy-start(bf16[2,4,4,2,8,128]{5,4,3,2,1,0:T(8,128)(2,1)} %inv_in.1) | copy-start | bytes 393220
  0.7 1.2 %copy-start.1 = (bf16[2,6,4,4,2,8,128]{6,5,4,3,2,1,0:T(8,128)(2,1)S(1)}, bf16[2,6,4,4,2,8,128]{6,5,4,3,2,1,0:T(8,128)(2,1)}, u32[]{:S(2)}) copy-start(bf16[2,6,4,4,2,8,128]{6,5,4,3,2,1,0:T(8,128)(2,1)} %cpl_in.1) | copy-start | bytes 2359300
  0.7 1.2 %copy-start.3 = (f32[2,4,2,8,128]{4,3,2,1,0:T(8,128)S(1)}, f32[2,4,2,8,128]{4,3,2,1,0:T(8,128)}, u32[]{:S(2)}) copy-start(f32[2,4,2,8,128]{4,3,2,1,0:T(8,128)} %later.1) | copy-start | bytes 196612
  0.7 15.8 %copy-start.5 = (s32[2,8,128]{2,1,0:T(8,128)S(1)}, s32[2,8,128]{2,1,0:T(8,128)}, u32[]{:S(2)}) copy-start(s32[2,8,128]{2,1,0:T(8,128)} %bmap.1) | copy-start | bytes 24580
  0.7 23.6 %copy-start = (bf16[2,4,2,8,128,128]{5,4,3,2,1,0:T(8,128)(2,1)S(1)}, bf16[2,4,2,8,128,128]{5,4,3,2,1,0:T(8,128)(2,1)}, u32[]{:S(2)}) copy-start(bf16[2,4,2,8,128,128]{5,4,3,2,1,0:T(8,128)(2,1)} %sens.1) | copy-start | bytes 12582916
  2.4 9.0 %collective-permute-start = (f32[2,24,8,128]{3,2,1,0:T(8,128)S(1)}, f32[2,24,8,128]{3,2,1,0:T(8,128)S(1)}, u32[]{:S(2)}, u32[]{:S(2)}) collective-permute-start(f32[2,24,8,128]{3,2,1,0:T(8,128)S(1)} %get-tuple-element.19.refs_3_), channel_id=1, source_target_pairs={{0,2},{2,0},{4,6},{6,4},{8,10},{10,8},{12,14},{14,12},{16,18},{18,... | collective-permute-start | bytes 589832 | tf_op jit(solution)/shard_map/ppermute | solution.py:356
  2.5 12.2 %collective-permute-start.2 = (f32[2,24,8,128]{3,2,1,0:T(8,128)S(1)}, f32[2,24,8,128]{3,2,1,0:T(8,128)S(1)}, u32[]{:S(2)}, u32[]{:S(2)}) collective-permute-start(f32[2,24,8,128]{3,2,1,0:T(8,128)S(1)} %get-tuple-element.20.refs_4_), channel_id=1, source_target_pairs={{0,2},{2,4},{4,6},{6,8},{8,10},{10,12},{12,14},{14,16},{16,18},{18... | collective-permute-start | bytes 589832 | tf_op jit(solution)/shard_map/ppermute | solution.py:357
  3.0 12.3 %collective-permute-start.1 = (f32[2,24,8,128]{3,2,1,0:T(8,128)S(1)}, f32[2,24,8,128]{3,2,1,0:T(8,128)S(1)}, u32[]{:S(2)}, u32[]{:S(2)}) collective-permute-start(f32[2,24,8,128]{3,2,1,0:T(8,128)S(1)} %get-tuple-element.20.refs_4_), channel_id=1, source_target_pairs={{2,0},{4,2},{6,4},{8,6},{10,8},{12,10},{14,12},{16,14},{18,16},{20... | collective-permute-start | bytes 589832 | tf_op jit(solution)/shard_map/ppermute | solution.py:358
  15.2 2.0 %collective-permute-start.5 = (f32[2,8,8,128]{3,2,1,0:T(8,128)S(1)}, f32[2,8,8,128]{3,2,1,0:T(8,128)S(1)}, u32[]{:S(2)}, u32[]{:S(2)}) collective-permute-start(f32[2,8,8,128]{3,2,1,0:T(8,128)S(1)} %get-tuple-element.27.sent_even), channel_id=1, source_target_pairs={{2,0},{4,2},{6,4},{8,6},{10,8},{12,10},{14,12},{16,14},{18,16},{20... | collective-permute-start | bytes 196616 | tf_op jit(solution)/shard_map/ppermute | solution.py:377
  15.4 1.9 %collective-permute-start.3 = (f32[2,8,8,128]{3,2,1,0:T(8,128)S(1)}, f32[2,8,8,128]{3,2,1,0:T(8,128)S(1)}, u32[]{:S(2)}, u32[]{:S(2)}) collective-permute-start(f32[2,8,8,128]{3,2,1,0:T(8,128)S(1)} %get-tuple-element.26.sent_near), channel_id=1, source_target_pairs={{0,2},{2,0},{4,6},{6,4},{8,10},{10,8},{12,14},{14,12},{16,18},{18,... | collective-permute-start | bytes 196616 | tf_op jit(solution)/shard_map/ppermute | solution.py:386
  16.4 7.9 %collective-permute-start.4 = (f32[2,8,8,128]{3,2,1,0:T(8,128)S(1)}, f32[2,8,8,128]{3,2,1,0:T(8,128)S(1)}, u32[]{:S(2)}, u32[]{:S(2)}) collective-permute-start(f32[2,8,8,128]{3,2,1,0:T(8,128)S(1)} %get-tuple-element.28.sent_odd), channel_id=1, source_target_pairs={{0,2},{2,4},{4,6},{6,8},{8,10},{10,12},{12,14},{14,16},{16,18},{18... | collective-permute-start | bytes 196616 | tf_op jit(solution)/shard_map/ppermute | solution.py:387
  27.9 1.4 %collective-permute-start.6 = (f32[256,128]{1,0:T(8,128)S(1)}, f32[256,128]{1,0:T(8,128)S(1)}, u32[]{:S(2)}, u32[]{:S(2)}) collective-permute-start(f32[256,128]{1,0:T(8,128)S(1)} %get-tuple-element.31), channel_id=1, source_target_pairs={{0,2},{2,0},{4,6},{6,4},{8,10},{10,8},{12,14},{14,12},{16,18},{18,... | collective-permute-start | bytes 393224 | tf_op jit(solution)/shard_map/ppermute | solution.py:401
  44.9 5.2 %collective-permute-start.7 = (f32[4,128]{1,0:T(4,128)S(1)}, f32[4,128]{1,0:T(4,128)S(1)}, u32[]{:S(2)}, u32[]{:S(2)}) collective-permute-start(f32[4,128]{1,0:T(4,128)S(1)} %reduce_sum.9), channel_id=1, source_target_pairs={{0,1},{1,0},{2,3},{3,2},{4,5},{5,4},{6,7},{7,6},{8,9},{9,8},{10,11... | collective-permute-start | bytes 6152 | tf_op jit(solution)/shard_map/ppermute | solution.py:407

commit v7 on v6

--- a/solution.py
+++ b/solution.py
@@ -4,6 +4,7 @@
 from jax.experimental import pallas as pl
 from jax.experimental.pallas import tpu as pltpu
 from jax.sharding import PartitionSpec as P
+
 
 BLK_DEV = 4
 F32 = jnp.float32
@@ -315,7 +316,7 @@
     return jax.ShapeDtypeStruct(shape, F32)
 
 
-def body(later_adjoint, coupling, diag_inverse, sensitivity, well_cells, well_misfit, block_map):
+def timestep(later_adjoint, coupling, diag_inverse, sensitivity, well_cells, well_misfit, block_map):
     members, unk, planes, rows, lanes = later_adjoint.shape
     count = planes * rows * lanes
     params = sensitivity.shape[-1]
@@ -330,73 +331,67 @@
     first_size = 2 * unk + unk * unk
     wells = well_cells.reshape(1, -1)
     dma = pltpu.SemaphoreType.DMA
-    with jax.named_scope("first"):
-        token = pl.pallas_call(
-            first_kernel,
-            out_shape=shaped(8, 128),
-            out_specs=VM,
-            compiler_params=room(1),
-            cost_estimate=busy(1 << 31),
-        )()
-    with jax.named_scope("start"):
-        src, nxt, near, far, cpl, inv = pl.pallas_call(
-            start_kernel,
-            out_shape=(
-                field,
-                field,
-                shaped(members, first_size, rows, lanes),
-                shaped(members, first_size, rows, lanes),
-                jax.ShapeDtypeStruct(coupling.shape, BF16),
-                jax.ShapeDtypeStruct(diag_inverse.shape, BF16),
-            ),
-            in_specs=[SM] + [VM] * 6,
-            out_specs=(VM,) * 6,
-            compiler_params=room(6),
-        )(pos, token, wells, well_misfit, later_adjoint, coupling, diag_inverse)
-    got_near = lax.ppermute(near, "cells", intra_pairs)
+    token = pl.pallas_call(
+        first_kernel,
+        out_shape=shaped(8, 128),
+        out_specs=VM,
+        compiler_params=room(1),
+        cost_estimate=busy(1 << 31),
+    )()
+    src, nxt, near, far, cpl, inv = pl.pallas_call(
+        start_kernel,
+        out_shape=(
+            field,
+            field,
+            shaped(members, first_size, rows, lanes),
+            shaped(members, first_size, rows, lanes),
+            jax.ShapeDtypeStruct(coupling.shape, BF16),
+            jax.ShapeDtypeStruct(diag_inverse.shape, BF16),
+        ),
+        in_specs=[SM] + [VM] * 6,
+        out_specs=(VM,) * 6,
+        compiler_params=room(6),
+    )(pos, token, wells, well_misfit, later_adjoint, coupling, diag_inverse)
     got_up = lax.ppermute(far, "cells", up_pairs)
     got_down = lax.ppermute(far, "cells", down_pairs)
-    with jax.named_scope("select"):
-        onehot = pl.pallas_call(
-            select_kernel,
-            out_shape=jax.ShapeDtypeStruct((nblk, count), BF16),
-            in_specs=[SM, VM],
-            out_specs=VM,
-            compiler_params=room(6),
-            cost_estimate=busy(1 << 24),
-        )(pos, block_map)
+    got_near = lax.ppermute(near, "cells", intra_pairs)
+    onehot = pl.pallas_call(
+        select_kernel,
+        out_shape=jax.ShapeDtypeStruct((nblk, count), BF16),
+        in_specs=[SM, VM],
+        out_specs=VM,
+        compiler_params=room(6),
+        cost_estimate=busy(1 << 24),
+    )(pos, block_map)
     wide = shaped(members, 2 * unk, rows, lanes)
-    with jax.named_scope("even"):
-        nxt_even, near_even, far_even = pl.pallas_call(
-            make_even_middle(ranks - 1),
-            out_shape=(field, wide, wide),
-            in_specs=[SM] + [VM] * 8,
-            out_specs=(VM, VM, VM),
-            compiler_params=room(6),
-        )(pos, src, nxt, near, far, got_near, got_up, cpl, inv)
+    nxt_even, near_even, far_even = pl.pallas_call(
+        make_even_middle(ranks - 1),
+        out_shape=(field, wide, wide),
+        in_specs=[SM] + [VM] * 8,
+        out_specs=(VM, VM, VM),
+        compiler_params=room(6),
+    )(pos, src, nxt, near, far, got_near, got_up, cpl, inv)
     got_down2 = lax.ppermute(far_even, "cells", down_pairs)
-    with jax.named_scope("odd"):
-        nxt2, near2, far_odd = pl.pallas_call(
-            make_odd_middle(ranks - 1),
-            out_shape=(field, wide, wide),
-            in_specs=[SM] + [VM] * 10,
-            out_specs=(VM, VM, VM),
-            compiler_params=room(6),
-        )(pos, src, nxt, near, far, got_near, got_down, cpl, inv, nxt_even, near_even)
+    nxt2, near2, far_odd = pl.pallas_call(
+        make_odd_middle(ranks - 1),
+        out_shape=(field, wide, wide),
+        in_specs=[SM] + [VM] * 10,
+        out_specs=(VM, VM, VM),
+        compiler_params=room(6),
+    )(pos, src, nxt, near, far, got_near, got_down, cpl, inv, nxt_even, near_even)
+    got_up2 = lax.ppermute(far_odd, "cells", up_pairs)
     got_near2 = lax.ppermute(near2, "cells", intra_pairs)
-    got_up2 = lax.ppermute(far_odd, "cells", up_pairs)
-    with jax.named_scope("end"):
-        adjoint, mine, other = pl.pallas_call(
-            make_end(ranks - 1, nblk),
-            out_shape=(field, shaped(nblk // 2, params), shaped(nblk // 2, params)),
-            in_specs=[SM] + [VM] * 15,
-            out_specs=(HB, VM, VM),
-            scratch_shapes=[pltpu.VMEM(field.shape, F32), pltpu.VMEM((count, 2 * params), BF16), dma((1,))],
-            compiler_params=room(16),
-        )(
-            pos, src, nxt2, got_near, got_up, got_down, near2, far_even, far_odd, got_near2, got_up2, got_down2,
-            cpl, inv, onehot, sensitivity,
-        )
+    adjoint, mine, other = pl.pallas_call(
+        make_end(ranks - 1, nblk),
+        out_shape=(field, shaped(nblk // 2, params), shaped(nblk // 2, params)),
+        in_specs=[SM] + [VM] * 15,
+        out_specs=(HB, VM, VM),
+        scratch_shapes=[pltpu.VMEM(field.shape, F32), pltpu.VMEM((count, 2 * params), BF16), dma((1,))],
+        compiler_params=room(16),
+    )(
+        pos, src, nxt2, got_near, got_up, got_down, near2, far_even, far_odd, got_near2, got_up2, got_down2,
+        cpl, inv, onehot, sensitivity,
+    )
     chips = ranks // 2
     half = mine + lax.ppermute(other, "cells", intra_pairs)
     same_core = [[core + 2 * chip for chip in range(chips)] for core in range(2)]
@@ -419,7 +414,7 @@
         P("cells", None, None),
     )
     return jax.shard_map(
-        body,
+        timestep,
         mesh=mesh,
         in_specs=placed,
         out_specs=(P("ens", None, "cells", None, None), P("cells", None)),

time: 50.8 us -> 50.8 us (level)
  no operation moved by 1% of the time
where the time goes in v7:
time: 50.8 us; the launch traced here: 50.6 us
  waiting for transfers between devices  16.3 us (32%)
  blocking collectives  15.5 us (31%)
  starting transfers between devices  10.9 us (21%)
  Pallas kernels  5.25 us (10%)
  local copies, waits for them, and re-layouts  1.17 us (2%)
  between operations  0.79 us (2%)
  other arithmetic  0.67 us (1%)
    all_to_all x1, blocking collectives, timestep(): lax.all_to_all(half.reshape(chips, BLK_DEV, params), 'cells', 0, 0, tiled...  15.5 us
    ppermute x1, starting transfers between devices, timestep(): got_down = lax.ppermute(far, 'cells', down_pairs)  8.38 us
    ppermute x1, waiting for transfers between devices, timestep(): got_up2 = lax.ppermute(far_odd, 'cells', up_pairs)  7.01 us
    ppermute x1, waiting for transfers between devices, timestep(): gradient = owned + lax.ppermute(owned, 'ens', [(0, 1), (1, 0)])  4.46 us
    pallas_call x1, Pallas kernels, timestep(): pl.pallas_call(make_end(ranks - 1, nblk), out_shape=(field, shaped(nblk /...  3.55 us
    ppermute x1, waiting for transfers between devices, timestep(): got_up = lax.ppermute(far, 'cells', up_pairs)  3.35 us
    ppermute x1, waiting for transfers between devices, timestep(): half = mine + lax.ppermute(other, 'cells', intra_pairs)  1.33 us
    unnamed x14, local copies, waits for them, and re-layouts  1.17 us
  transfers between devices with their start and end apart: 8, of which 6 were waited for; matrix products, arithmetic and copies ran while one was open for 0% of the time, Pallas kernels for 2%

profile of v7, /device:TPU:16, one launch (start us, length us, event | category | flops | bytes accessed | tf_op | source)
XLA Modules:
  0.0 50.6 jit_solution(17972688110600123497)
XLA Ops:
  0.6 0.0 copy-start.4
  0.6 0.0 copy-start.6
  0.7 0.0 copy-start.2
  0.7 0.0 copy-start.1
  0.7 0.0 copy-start.5
  0.7 0.0 copy-start
  0.7 0.6 %copy-done.4 = f32[2,4,256]{2,1,0:T(4,128)S(1)} copy-done((f32[2,4,256]{2,1,0:T(4,128)S(1)}, f32[2,4,256]{2,1,0:T(4,128)}, u32[]{:S(2)}) %copy-start.4) | copy-done | bytes 8216
  1.3 0.2 copy-done.2
  1.6 0.3 copy-done.1
  1.9 0.5 %shard_map.87 = (f32[2,4,2,8,128]{4,3,2,1,0:T(8,128)S(1)}, f32[2,4,2,8,128]{4,3,2,1,0:T(8,128)S(1)}, f32[2,24,8,128]{3,2,1,0:T(8,128)S(1)}, f32[2,24,8,128]{3,2,...) custom-call(s32[1]{0:T(128)} %bitcast.pos.refs_0_, ...), custom_call_target="tpu_custom_call" | custom-call | tf_op jit(solution)/shard_map/pallas_call | solution.py:341
  2.4 0.1 collective-permute-start
  2.5 0.5 collective-permute-start.2
  3.0 8.4 %collective-permute-start.1 = (f32[2,24,8,128]{3,2,1,0:T(8,128)S(1)}, f32[2,24,8,128]{3,2,1,0:T(8,128)S(1)}, u32[]{:S(2)}, u32[]{:S(2)}) collective-permute-start(f32[2,24,8,128]{3,2,1,0:T(8,128)S(1)} %get-tuple-element.20.refs_4_), channel_id=1, source_target_pairs={{2,0},{4,2},{6,4},{8,6},{10,8},{12,10},{14,12},{16,14},{18,16},{20... | collective-permute-start | bytes 589832 | tf_op jit(solution)/shard_map/ppermute | solution.py:356
  11.4 0.0 collective-permute-done.refs_5_.block_near
  11.4 3.3 %collective-permute-done.2.refs_6_.block_even = f32[2,24,8,128]{3,2,1,0:T(8,128)S(1)} collective-permute-done((f32[2,24,8,128]{3,2,1,0:T(8,128)S(1)}, f32[2,24,8,128]{3,2,1,0:T(8,128)S(1)}, u32[]{:S(2)}, u32[]{:S(2)}) %collective-permute-start.2) | collective-permute-done | bytes 196640 | tf_op jit(solution)/shard_map/ppermute | solution.py:355
  14.8 0.5 shard_map.88
  15.2 0.1 collective-permute-start.5
  15.3 0.0 collective-permute-done.1.refs_6_.block_odd
  15.4 1.0 %collective-permute-start.3 = (f32[2,8,8,128]{3,2,1,0:T(8,128)S(1)}, f32[2,8,8,128]{3,2,1,0:T(8,128)S(1)}, u32[]{:S(2)}, u32[]{:S(2)}) collective-permute-start(f32[2,8,8,128]{3,2,1,0:T(8,128)S(1)} %get-tuple-element.26.sent_near), channel_id=1, source_target_pairs={{0,2},{2,0},{4,6},{6,4},{8,10},{10,8},{12,14},{14,12},{16,18},{18,... | collective-permute-start | bytes 196616 | tf_op jit(solution)/shard_map/ppermute | solution.py:383
  16.4 0.1 collective-permute-start.4
  16.5 0.6 %shard_map.90.onehot = bf16[512,2048]{1,0:T(8,128)(2,1)S(1)} custom-call(s32[1]{0:T(128)} %bitcast.pos.refs_0_, s32[2,8,128]{2,1,0:T(8,128)S(1)} %copy-done.5), custom_call_target="tpu_custom_call" | custom-call | flops 16777216 | tf_op jit(solution)/shard_map/pallas_call | solution.py:358
  17.1 0.1 collective-permute-done.5.got_odd
  17.2 0.1 collective-permute-done.3.got_near
  17.3 7.0 %collective-permute-done.4.got_even = f32[2,8,8,128]{3,2,1,0:T(8,128)S(1)} collective-permute-done((f32[2,8,8,128]{3,2,1,0:T(8,128)S(1)}, f32[2,8,8,128]{3,2,1,0:T(8,128)S(1)}, u32[]{:S(2)}, u32[]{:S(2)}) %collective-permute-start.4) | collective-permute-done | bytes 65568 | tf_op jit(solution)/shard_map/ppermute | solution.py:382
  24.3 3.6 %shard_map.91 = (f32[2,4,2,8,128]{4,3,2,1,0:T(8,128)}, f32[256,128]{1,0:T(8,128)S(1)}, f32[256,128]{1,0:T(8,128)S(1)}) custom-call(s32[1]{0:T(128)} %bitcast.pos.refs_0_, f32[2,4,2,8,128]{4,3,2,1,0:T(8,128)S(1)} %get-tuple-element.17.refs_1_.src, f32[2,4,2,8,128]{4,3,2,1,0:T(8,128)S(1)} %get-tuple-element.25.nxt, ...), custom_call_target="tpu_custom_call" | custom-call | tf_op jit(solution)/shard_map/pallas_call | solution.py:384
  27.9 0.1 collective-permute-start.6
  28.0 1.3 %collective-permute-done.6 = f32[256,128]{1,0:T(8,128)S(1)} collective-permute-done((f32[256,128]{1,0:T(8,128)S(1)}, f32[256,128]{1,0:T(8,128)S(1)}, u32[]{:S(2)}, u32[]{:S(2)}) %collective-permute-start.6) | collective-permute-done | bytes 131104 | tf_op jit(solution)/shard_map/ppermute | solution.py:396
  29.3 15.5 %all_to_all.5 = f32[64,4,128]{2,1,0:T(4,128)S(1)} all-to-all(f32[64,4,128]{2,1,0:T(4,128)S(1)} %bitcast.4), channel_id=1, replica_groups={{0,4,8,12,16,20,24,28,32,36,40,44,48,52,56,60,64,68,72,76,80,84,88,92,9..., dimensions={0} | all-to-all | bytes 262144 | tf_op jit(solution)/shard_map/all_to_all | solution.py:398
  44.8 0.1 reduce_sum.9
  44.9 0.7 %collective-permute-start.7 = (f32[4,128]{1,0:T(4,128)S(1)}, f32[4,128]{1,0:T(4,128)S(1)}, u32[]{:S(2)}, u32[]{:S(2)}) collective-permute-start(f32[4,128]{1,0:T(4,128)S(1)} %reduce_sum.9), channel_id=1, source_target_pairs={{0,1},{1,0},{2,3},{3,2},{4,5},{5,4},{6,7},{7,6},{8,9},{9,8},{10,11... | collective-permute-start | bytes 6152 | tf_op jit(solution)/shard_map/ppermute | solution.py:402
  45.6 4.5 %collective-permute-done.7 = f32[4,128]{1,0:T(4,128)S(1)} collective-permute-done((f32[4,128]{1,0:T(4,128)S(1)}, f32[4,128]{1,0:T(4,128)S(1)}, u32[]{:S(2)}, u32[]{:S(2)}) %collective-permute-start.7) | collective-permute-done | bytes 2080 | tf_op jit(solution)/shard_map/ppermute | solution.py:402
  50.1 0.6 %add.7 = f32[4,128]{1,0:T(4,128)} add(f32[4,128]{1,0:T(4,128)S(1)} %reduce_sum.9, f32[4,128]{1,0:T(4,128)S(1)} %collective-permute-done.7) | non-fusion elementwise | flops 512 | bytes 6144 | tf_op jit(solution)/shard_map/add | solution.py:402
  (8 shorter events, 0.1 us)
Async XLA Ops:
  0.6 0.7 %copy-start.4 = (f32[2,4,256]{2,1,0:T(4,128)S(1)}, f32[2,4,256]{2,1,0:T(4,128)}, u32[]{:S(2)}) copy-start(f32[2,4,256]{2,1,0:T(4,128)} %misfit.1) | copy-start | bytes 24580
  0.6 0.7 %copy-start.6 = (s32[256]{0:T(256)S(1)}, s32[256]{0:T(256)}, u32[]{:S(2)}) copy-start(s32[256]{0:T(256)} %param.11) | copy-start | bytes 3076
  0.7 0.9 %copy-start.2 = (bf16[2,4,4,2,8,128]{5,4,3,2,1,0:T(8,128)(2,1)S(1)}, bf16[2,4,4,2,8,128]{5,4,3,2,1,0:T(8,128)(2,1)}, u32[]{:S(2)}) copy-start(bf16[2,4,4,2,8,128]{5,4,3,2,1,0:T(8,128)(2,1)} %inv_in.1) | copy-start | bytes 393220
  0.7 1.2 %copy-start.1 = (bf16[2,6,4,4,2,8,128]{6,5,4,3,2,1,0:T(8,128)(2,1)S(1)}, bf16[2,6,4,4,2,8,128]{6,5,4,3,2,1,0:T(8,128)(2,1)}, u32[]{:S(2)}) copy-start(bf16[2,6,4,4,2,8,128]{6,5,4,3,2,1,0:T(8,128)(2,1)} %cpl_in.1) | copy-start | bytes 2359300
  0.7 1.2 %copy-start.3 = (f32[2,4,2,8,128]{4,3,2,1,0:T(8,128)S(1)}, f32[2,4,2,8,128]{4,3,2,1,0:T(8,128)}, u32[]{:S(2)}) copy-start(f32[2,4,2,8,128]{4,3,2,1,0:T(8,128)} %later.1) | copy-start | bytes 196612
  0.7 15.8 %copy-start.5 = (s32[2,8,128]{2,1,0:T(8,128)S(1)}, s32[2,8,128]{2,1,0:T(8,128)}, u32[]{:S(2)}) copy-start(s32[2,8,128]{2,1,0:T(8,128)} %bmap.1) | copy-start | bytes 24580
  0.7 23.6 %copy-start = (bf16[2,4,2,8,128,128]{5,4,3,2,1,0:T(8,128)(2,1)S(1)}, bf16[2,4,2,8,128,128]{5,4,3,2,1,0:T(8,128)(2,1)}, u32[]{:S(2)}) copy-start(bf16[2,4,2,8,128,128]{5,4,3,2,1,0:T(8,128)(2,1)} %sens.1) | copy-start | bytes 12582916
  2.4 9.0 %collective-permute-start = (f32[2,24,8,128]{3,2,1,0:T(8,128)S(1)}, f32[2,24,8,128]{3,2,1,0:T(8,128)S(1)}, u32[]{:S(2)}, u32[]{:S(2)}) collective-permute-start(f32[2,24,8,128]{3,2,1,0:T(8,128)S(1)} %get-tuple-element.19.refs_3_), channel_id=1, source_target_pairs={{0,2},{2,0},{4,6},{6,4},{8,10},{10,8},{12,14},{14,12},{16,18},{18,... | collective-permute-start | bytes 589832 | tf_op jit(solution)/shard_map/ppermute | solution.py:357
  2.5 12.2 %collective-permute-start.2 = (f32[2,24,8,128]{3,2,1,0:T(8,128)S(1)}, f32[2,24,8,128]{3,2,1,0:T(8,128)S(1)}, u32[]{:S(2)}, u32[]{:S(2)}) collective-permute-start(f32[2,24,8,128]{3,2,1,0:T(8,128)S(1)} %get-tuple-element.20.refs_4_), channel_id=1, source_target_pairs={{0,2},{2,4},{4,6},{6,8},{8,10},{10,12},{12,14},{14,16},{16,18},{18... | collective-permute-start | bytes 589832 | tf_op jit(solution)/shard_map/ppermute | solution.py:355
  3.0 12.3 %collective-permute-start.1 = (f32[2,24,8,128]{3,2,1,0:T(8,128)S(1)}, f32[2,24,8,128]{3,2,1,0:T(8,128)S(1)}, u32[]{:S(2)}, u32[]{:S(2)}) collective-permute-start(f32[2,24,8,128]{3,2,1,0:T(8,128)S(1)} %get-tuple-element.20.refs_4_), channel_id=1, source_target_pairs={{2,0},{4,2},{6,4},{8,6},{10,8},{12,10},{14,12},{16,14},{18,16},{20... | collective-permute-start | bytes 589832 | tf_op jit(solution)/shard_map/ppermute | solution.py:356
  15.2 2.0 %collective-permute-start.5 = (f32[2,8,8,128]{3,2,1,0:T(8,128)S(1)}, f32[2,8,8,128]{3,2,1,0:T(8,128)S(1)}, u32[]{:S(2)}, u32[]{:S(2)}) collective-permute-start(f32[2,8,8,128]{3,2,1,0:T(8,128)S(1)} %get-tuple-element.27.sent_even), channel_id=1, source_target_pairs={{2,0},{4,2},{6,4},{8,6},{10,8},{12,10},{14,12},{16,14},{18,16},{20... | collective-permute-start | bytes 196616 | tf_op jit(solution)/shard_map/ppermute | solution.py:374
  15.4 1.9 %collective-permute-start.3 = (f32[2,8,8,128]{3,2,1,0:T(8,128)S(1)}, f32[2,8,8,128]{3,2,1,0:T(8,128)S(1)}, u32[]{:S(2)}, u32[]{:S(2)}) collective-permute-start(f32[2,8,8,128]{3,2,1,0:T(8,128)S(1)} %get-tuple-element.26.sent_near), channel_id=1, source_target_pairs={{0,2},{2,0},{4,6},{6,4},{8,10},{10,8},{12,14},{14,12},{16,18},{18,... | collective-permute-start | bytes 196616 | tf_op jit(solution)/shard_map/ppermute | solution.py:383
  16.4 7.9 %collective-permute-start.4 = (f32[2,8,8,128]{3,2,1,0:T(8,128)S(1)}, f32[2,8,8,128]{3,2,1,0:T(8,128)S(1)}, u32[]{:S(2)}, u32[]{:S(2)}) collective-permute-start(f32[2,8,8,128]{3,2,1,0:T(8,128)S(1)} %get-tuple-element.28.sent_odd), channel_id=1, source_target_pairs={{0,2},{2,4},{4,6},{6,8},{8,10},{10,12},{12,14},{14,16},{16,18},{18... | collective-permute-start | bytes 196616 | tf_op jit(solution)/shard_map/ppermute | solution.py:382
  27.9 1.4 %collective-permute-start.6 = (f32[256,128]{1,0:T(8,128)S(1)}, f32[256,128]{1,0:T(8,128)S(1)}, u32[]{:S(2)}, u32[]{:S(2)}) collective-permute-start(f32[256,128]{1,0:T(8,128)S(1)} %get-tuple-element.31), channel_id=1, source_target_pairs={{0,2},{2,0},{4,6},{6,4},{8,10},{10,8},{12,14},{14,12},{16,18},{18,... | collective-permute-start | bytes 393224 | tf_op jit(solution)/shard_map/ppermute | solution.py:396
  44.9 5.2 %collective-permute-start.7 = (f32[4,128]{1,0:T(4,128)S(1)}, f32[4,128]{1,0:T(4,128)S(1)}, u32[]{:S(2)}, u32[]{:S(2)}) collective-permute-start(f32[4,128]{1,0:T(4,128)S(1)} %reduce_sum.9), channel_id=1, source_target_pairs={{0,1},{1,0},{2,3},{3,2},{4,5},{5,4},{6,7},{7,6},{8,9},{9,8},{10,11... | collective-permute-start | bytes 6152 | tf_op jit(solution)/shard_map/ppermute | solution.py:402

commit v8 on v7

--- a/solution.py
+++ b/solution.py
@@ -240,7 +240,7 @@
     return odd_middle
 
 
-def select_kernel(pos, bmap, onehot):
+def select_kernel(pos, bmap, sens, onehot, turned):
     rows, lanes = bmap.shape[1:]
     nblk = onehot.shape[0]
     core = pos[0] % 2
@@ -252,15 +252,19 @@
     for g in range(bmap.shape[0] * rows):
         row = bmap[g // rows, g % rows : g % rows + 1, :]
         onehot[:, g * lanes : (g + 1) * lanes] = (block == row).astype(F32).astype(BF16)
+    for m in range(sens.shape[0]):
+        for u in range(sens.shape[1]):
+            for g in range(bmap.shape[0] * rows):
+                turned[m, u, g] = sens[m, u, g // rows, g % rows].astype(F32).T
 
 
 def make_end(last, nblk):
     def end_kernel(
         pos, src, nxt, block_near, block_even, block_odd, sent_near, sent_even, sent_odd, got_near, got_even, got_odd,
-        cpl, inv, onehot, sens, adj_out, mine_out, other_out, adj, grads, sems,
+        cpl, inv, onehot, turned, adj_out, mine_out, other_out, adj, grads, sems,
     ):
         members, unk, planes, rows, lanes = src.shape
-        params = sens.shape[-1]
+        params = turned.shape[-2]
         groups = planes * rows
         half_rows = nblk // 2
         near = (reader(sent_near), reader(got_near), reader(block_near))
@@ -276,20 +280,22 @@
                 adj[m, u] = a[u]
         store = pltpu.make_async_copy(adj, adj_out, sems.at[0])
         store.start()
-        turned = adj[...].reshape(members * unk * groups, lanes).T
+        step = 32
         for g in range(groups):
             x, y = g // rows, g % rows
-            total = None
-            for m in range(members):
-                for u in range(unk):
-                    col = (m * unk + u) * groups + g
-                    term = turned[:, col : col + 1] * sens[m, u, x, y].astype(F32)
-                    total = term if total is None else total + term
-            hi = total.astype(BF16)
-            lo = (total - hi.astype(F32)).astype(BF16)
-            grads[g * lanes : (g + 1) * lanes, :params] = hi
-            grads[g * lanes : (g + 1) * lanes, params:] = lo
-        both = jnp.dot(onehot[...], grads[...], preferred_element_type=F32)
+            for p in range(0, params, step):
+                total = None
+                for m in range(members):
+                    for u in range(unk):
+                        term = adj[m, u, x, y : y + 1] * turned[m, u, g, p : p + step]
+                        total = term if total is None else total + term
+                hi = total.astype(BF16)
+                lo = (total - hi.astype(F32)).astype(BF16)
+                grads[p : p + step, g * lanes : (g + 1) * lanes] = hi
+                grads[params + p : params + p + step, g * lanes : (g + 1) * lanes] = lo
+        both = lax.dot_general(
+            onehot[...], grads[...], (((1,), (1,)), ((), ())), preferred_element_type=F32
+        )
         out = both[:, :params] + both[:, params:]
         mine_out[...] = out[:half_rows]
         other_out[...] = out[half_rows:]
@@ -355,14 +361,16 @@
     got_up = lax.ppermute(far, "cells", up_pairs)
     got_down = lax.ppermute(far, "cells", down_pairs)
     got_near = lax.ppermute(near, "cells", intra_pairs)
-    onehot = pl.pallas_call(
+    onehot, turned = pl.pallas_call(
         select_kernel,
-        out_shape=jax.ShapeDtypeStruct((nblk, count), BF16),
-        in_specs=[SM, VM],
-        out_specs=VM,
+        out_shape=(
+            jax.ShapeDtypeStruct((nblk, count), BF16), shaped(members, unk, planes * rows, params, lanes)
+        ),
+        in_specs=[SM, VM, VM],
+        out_specs=(VM, VM),
         compiler_params=room(6),
         cost_estimate=busy(1 << 24),
-    )(pos, block_map)
+    )(pos, block_map, sensitivity)
     wide = shaped(members, 2 * unk, rows, lanes)
     nxt_even, near_even, far_even = pl.pallas_call(
         make_even_middle(ranks - 1),
@@ -386,11 +394,11 @@
         out_shape=(field, shaped(nblk // 2, params), shaped(nblk // 2, params)),
         in_specs=[SM] + [VM] * 15,
         out_specs=(HB, VM, VM),
-        scratch_shapes=[pltpu.VMEM(field.shape, F32), pltpu.VMEM((count, 2 * params), BF16), dma((1,))],
+        scratch_shapes=[pltpu.VMEM(field.shape, F32), pltpu.VMEM((2 * params, count), BF16), dma((1,))],
         compiler_params=room(16),
     )(
         pos, src, nxt2, got_near, got_up, got_down, near2, far_even, far_odd, got_near2, got_up2, got_down2,
-        cpl, inv, onehot, sensitivity,
+        cpl, inv, onehot, turned,
     )
     chips = ranks // 2
     half = mine + lax.ppermute(other, "cells", intra_pairs)

time: 50.8 us -> 49.1 us (0.967)
  waiting for transfers between devices: 16.3 us -> 15 us
    pallas_call x1, Pallas kernels: 3.55 us -> 1.89 us  [timestep(): pl.pallas_call(make_end(ranks - 1, nblk), out_shape=(field, shaped(nblk /...]
    pallas_call x1, Pallas kernels: 0.65 us -> 1.98 us  [timestep(): pl.pallas_call(select_kernel, out_shape=(jax.ShapeDtypeStruct((nblk, coun...]
    ppermute x1, waiting for transfers between devices: 7.01 us -> 5.8 us  [timestep(): got_up2 = lax.ppermute(far_odd, 'cells', up_pairs)]
  transfers between devices with their start and end apart: 8 -> 8, of which waited for: 6 -> 4; matrix products, arithmetic and copies ran while one was open for 0% -> 0% of each run, Pallas kernels for 2% -> 5%
where the time goes in v8:
time: 49.1 us; the launch traced here: 49 us
  blocking collectives  15.5 us (32%)
  waiting for transfers between devices  15 us (31%)
  starting transfers between devices  10.9 us (22%)
  Pallas kernels  4.93 us (10%)
  local copies, waits for them, and re-layouts  1.17 us (2%)
  between operations  0.8 us (2%)
  other arithmetic  0.67 us (1%)
    all_to_all x1, blocking collectives, timestep(): lax.all_to_all(half.reshape(chips, BLK_DEV, params), 'cells', 0, 0, tiled...  15.5 us
    ppermute x1, starting transfers between devices, timestep(): got_down = lax.ppermute(far, 'cells', down_pairs)  8.38 us
    ppermute x1, waiting for transfers between devices, timestep(): got_up2 = lax.ppermute(far_odd, 'cells', up_pairs)  5.8 us
    ppermute x1, waiting for transfers between devices, timestep(): gradient = owned + lax.ppermute(owned, 'ens', [(0, 1), (1, 0)])  4.46 us
    ppermute x1, waiting for transfers between devices, timestep(): got_up = lax.ppermute(far, 'cells', up_pairs)  3.35 us
    pallas_call x1, Pallas kernels, timestep(): pl.pallas_call(select_kernel, out_shape=(jax.ShapeDtypeStruct((nblk, coun...  1.98 us
    pallas_call x1, Pallas kernels, timestep(): pl.pallas_call(make_end(ranks - 1, nblk), out_shape=(field, shaped(nblk /...  1.89 us
    ppermute x1, waiting for transfers between devices, timestep(): half = mine + lax.ppermute(other, 'cells', intra_pairs)  1.33 us
  transfers between devices with their start and end apart: 8, of which 4 were waited for; matrix products, arithmetic and copies ran while one was open for 0% of the time, Pallas kernels for 5%

profile of v8, /device:TPU:16, one launch (start us, length us, event | category | flops | bytes accessed | tf_op | source)
XLA Modules:
  0.0 49.0 jit_solution(1715077506956475151)
XLA Ops:
  0.6 0.0 copy-start.4
  0.6 0.0 copy-start.6
  0.7 0.0 copy-start.2
  0.7 0.0 copy-start.1
  0.7 0.0 copy-start.5
  0.7 0.0 copy-start
  0.7 0.6 %copy-done.4 = f32[2,4,256]{2,1,0:T(4,128)S(1)} copy-done((f32[2,4,256]{2,1,0:T(4,128)S(1)}, f32[2,4,256]{2,1,0:T(4,128)}, u32[]{:S(2)}) %copy-start.4) | copy-done | bytes 8216
  1.3 0.2 copy-done.2
  1.6 0.3 copy-done.1
  1.9 0.5 %shard_map.87 = (f32[2,4,2,8,128]{4,3,2,1,0:T(8,128)S(1)}, f32[2,4,2,8,128]{4,3,2,1,0:T(8,128)S(1)}, f32[2,24,8,128]{3,2,1,0:T(8,128)S(1)}, f32[2,24,8,128]{3,2,...) custom-call(s32[1]{0:T(128)} %bitcast.pos.refs_0_, ...), custom_call_target="tpu_custom_call" | custom-call | tf_op jit(solution)/shard_map/pallas_call | solution.py:347
  2.4 0.1 collective-permute-start
  2.5 0.5 %collective-permute-start.2 = (f32[2,24,8,128]{3,2,1,0:T(8,128)S(1)}, f32[2,24,8,128]{3,2,1,0:T(8,128)S(1)}, u32[]{:S(2)}, u32[]{:S(2)}) collective-permute-start(f32[2,24,8,128]{3,2,1,0:T(8,128)S(1)} %get-tuple-element.22.refs_4_), channel_id=1, source_target_pairs={{0,2},{2,4},{4,6},{6,8},{8,10},{10,12},{12,14},{14,16},{16,18},{18... | collective-permute-start | bytes 589832 | tf_op jit(solution)/shard_map/ppermute | solution.py:361
  3.0 8.4 %collective-permute-start.1 = (f32[2,24,8,128]{3,2,1,0:T(8,128)S(1)}, f32[2,24,8,128]{3,2,1,0:T(8,128)S(1)}, u32[]{:S(2)}, u32[]{:S(2)}) collective-permute-start(f32[2,24,8,128]{3,2,1,0:T(8,128)S(1)} %get-tuple-element.22.refs_4_), channel_id=1, source_target_pairs={{2,0},{4,2},{6,4},{8,6},{10,8},{12,10},{14,12},{16,14},{18,16},{20... | collective-permute-start | bytes 589832 | tf_op jit(solution)/shard_map/ppermute | solution.py:362
  11.4 0.0 collective-permute-done.refs_5_.block_near
  11.4 3.3 %collective-permute-done.2.refs_6_.block_even = f32[2,24,8,128]{3,2,1,0:T(8,128)S(1)} collective-permute-done((f32[2,24,8,128]{3,2,1,0:T(8,128)S(1)}, f32[2,24,8,128]{3,2,1,0:T(8,128)S(1)}, u32[]{:S(2)}, u32[]{:S(2)}) %collective-permute-start.2) | collective-permute-done | bytes 196640 | tf_op jit(solution)/shard_map/ppermute | solution.py:361
  14.8 0.5 shard_map.88
  15.2 0.1 collective-permute-start.5
  15.3 0.0 collective-permute-done.1.refs_6_.block_odd
  15.4 1.0 %collective-permute-start.3 = (f32[2,8,8,128]{3,2,1,0:T(8,128)S(1)}, f32[2,8,8,128]{3,2,1,0:T(8,128)S(1)}, u32[]{:S(2)}, u32[]{:S(2)}) collective-permute-start(f32[2,8,8,128]{3,2,1,0:T(8,128)S(1)} %get-tuple-element.28.sent_near), channel_id=1, source_target_pairs={{0,2},{2,0},{4,6},{6,4},{8,10},{10,8},{12,14},{14,12},{16,18},{18,... | collective-permute-start | bytes 196616 | tf_op jit(solution)/shard_map/ppermute | solution.py:391
  16.4 0.1 collective-permute-start.4
  16.5 2.0 %shard_map.90 = (bf16[512,2048]{1,0:T(8,128)(2,1)S(1)}, f32[2,4,16,128,128]{4,3,2,1,0:T(8,128)S(1)}) custom-call(s32[1]{0:T(128)} %bitcast.pos.refs_0_, s32[2,8,128]{2,1,0:T(8,128)S(1)} %copy-done.5, bf16[2,4,2,8,128,128]{5,4,3,2,1,0:T(8,128)(2,1)S(1)} %copy-done), custom_call_target="tpu_custom_call" | custom-call | flops 16777216 | tf_op jit(solution)/shard_map/pallas_call | solution.py:364
  18.5 0.0 collective-permute-done.5.got_odd
  18.5 0.0 collective-permute-done.3.got_near
  18.5 5.8 %collective-permute-done.4.got_even = f32[2,8,8,128]{3,2,1,0:T(8,128)S(1)} collective-permute-done((f32[2,8,8,128]{3,2,1,0:T(8,128)S(1)}, f32[2,8,8,128]{3,2,1,0:T(8,128)S(1)}, u32[]{:S(2)}, u32[]{:S(2)}) %collective-permute-start.4) | collective-permute-done | bytes 65568 | tf_op jit(solution)/shard_map/ppermute | solution.py:390
  24.3 1.9 %shard_map.91 = (f32[2,4,2,8,128]{4,3,2,1,0:T(8,128)}, f32[256,128]{1,0:T(8,128)S(1)}, f32[256,128]{1,0:T(8,128)S(1)}) custom-call(s32[1]{0:T(128)} %bitcast.pos.refs_0_, f32[2,4,2,8,128]{4,3,2,1,0:T(8,128)S(1)} %get-tuple-element.19.refs_1_.src, f32[2,4,2,8,128]{4,3,2,1,0:T(8,128)S(1)} %get-tuple-element.27.nxt, ...), custom_call_target="tpu_custom_call" | custom-call | tf_op jit(solution)/shard_map/pallas_call | solution.py:392
  26.2 0.1 collective-permute-start.6
  26.3 1.3 %collective-permute-done.6 = f32[256,128]{1,0:T(8,128)S(1)} collective-permute-done((f32[256,128]{1,0:T(8,128)S(1)}, f32[256,128]{1,0:T(8,128)S(1)}, u32[]{:S(2)}, u32[]{:S(2)}) %collective-permute-start.6) | collective-permute-done | bytes 131104 | tf_op jit(solution)/shard_map/ppermute | solution.py:404
  27.6 15.5 %all_to_all.5 = f32[64,4,128]{2,1,0:T(4,128)S(1)} all-to-all(f32[64,4,128]{2,1,0:T(4,128)S(1)} %bitcast.4), channel_id=1, replica_groups={{0,4,8,12,16,20,24,28,32,36,40,44,48,52,56,60,64,68,72,76,80,84,88,92,9..., dimensions={0} | all-to-all | bytes 262144 | tf_op jit(solution)/shard_map/all_to_all | solution.py:406
  43.1 0.1 reduce_sum.9
  43.2 0.7 %collective-permute-start.7 = (f32[4,128]{1,0:T(4,128)S(1)}, f32[4,128]{1,0:T(4,128)S(1)}, u32[]{:S(2)}, u32[]{:S(2)}) collective-permute-start(f32[4,128]{1,0:T(4,128)S(1)} %reduce_sum.9), channel_id=1, source_target_pairs={{0,1},{1,0},{2,3},{3,2},{4,5},{5,4},{6,7},{7,6},{8,9},{9,8},{10,11... | collective-permute-start | bytes 6152 | tf_op jit(solution)/shard_map/ppermute | solution.py:410
  43.9 4.5 %collective-permute-done.7 = f32[4,128]{1,0:T(4,128)S(1)} collective-permute-done((f32[4,128]{1,0:T(4,128)S(1)}, f32[4,128]{1,0:T(4,128)S(1)}, u32[]{:S(2)}, u32[]{:S(2)}) %collective-permute-start.7) | collective-permute-done | bytes 2080 | tf_op jit(solution)/shard_map/ppermute | solution.py:410
  48.4 0.6 %add.7 = f32[4,128]{1,0:T(4,128)} add(f32[4,128]{1,0:T(4,128)S(1)} %reduce_sum.9, f32[4,128]{1,0:T(4,128)S(1)} %collective-permute-done.7) | non-fusion elementwise | flops 512 | bytes 6144 | tf_op jit(solution)/shard_map/add | solution.py:410
  (8 shorter events, 0.1 us)
Async XLA Ops:
  0.6 0.7 %copy-start.4 = (f32[2,4,256]{2,1,0:T(4,128)S(1)}, f32[2,4,256]{2,1,0:T(4,128)}, u32[]{:S(2)}) copy-start(f32[2,4,256]{2,1,0:T(4,128)} %misfit.1) | copy-start | bytes 24580
  0.6 0.7 %copy-start.6 = (s32[256]{0:T(256)S(1)}, s32[256]{0:T(256)}, u32[]{:S(2)}) copy-start(s32[256]{0:T(256)} %param.11) | copy-start | bytes 3076
  0.7 0.9 %copy-start.2 = (bf16[2,4,4,2,8,128]{5,4,3,2,1,0:T(8,128)(2,1)S(1)}, bf16[2,4,4,2,8,128]{5,4,3,2,1,0:T(8,128)(2,1)}, u32[]{:S(2)}) copy-start(bf16[2,4,4,2,8,128]{5,4,3,2,1,0:T(8,128)(2,1)} %inv_in.1) | copy-start | bytes 393220
  0.7 1.2 %copy-start.1 = (bf16[2,6,4,4,2,8,128]{6,5,4,3,2,1,0:T(8,128)(2,1)S(1)}, bf16[2,6,4,4,2,8,128]{6,5,4,3,2,1,0:T(8,128)(2,1)}, u32[]{:S(2)}) copy-start(bf16[2,6,4,4,2,8,128]{6,5,4,3,2,1,0:T(8,128)(2,1)} %cpl_in.1) | copy-start | bytes 2359300
  0.7 1.2 %copy-start.3 = (f32[2,4,2,8,128]{4,3,2,1,0:T(8,128)S(1)}, f32[2,4,2,8,128]{4,3,2,1,0:T(8,128)}, u32[]{:S(2)}) copy-start(f32[2,4,2,8,128]{4,3,2,1,0:T(8,128)} %later.1) | copy-start | bytes 196612
  0.7 15.8 %copy-start.5 = (s32[2,8,128]{2,1,0:T(8,128)S(1)}, s32[2,8,128]{2,1,0:T(8,128)}, u32[]{:S(2)}) copy-start(s32[2,8,128]{2,1,0:T(8,128)} %bmap.1) | copy-start | bytes 24580
  0.7 15.8 %copy-start = (bf16[2,4,2,8,128,128]{5,4,3,2,1,0:T(8,128)(2,1)S(1)}, bf16[2,4,2,8,128,128]{5,4,3,2,1,0:T(8,128)(2,1)}, u32[]{:S(2)}) copy-start(bf16[2,4,2,8,128,128]{5,4,3,2,1,0:T(8,128)(2,1)} %sens.1) | copy-start | bytes 12582916
  2.4 9.0 %collective-permute-start = (f32[2,24,8,128]{3,2,1,0:T(8,128)S(1)}, f32[2,24,8,128]{3,2,1,0:T(8,128)S(1)}, u32[]{:S(2)}, u32[]{:S(2)}) collective-permute-start(f32[2,24,8,128]{3,2,1,0:T(8,128)S(1)} %get-tuple-element.21.refs_3_), channel_id=1, source_target_pairs={{0,2},{2,0},{4,6},{6,4},{8,10},{10,8},{12,14},{14,12},{16,18},{18,... | collective-permute-start | bytes 589832 | tf_op jit(solution)/shard_map/ppermute | solution.py:363
  2.5 12.2 %collective-permute-start.2 = (f32[2,24,8,128]{3,2,1,0:T(8,128)S(1)}, f32[2,24,8,128]{3,2,1,0:T(8,128)S(1)}, u32[]{:S(2)}, u32[]{:S(2)}) collective-permute-start(f32[2,24,8,128]{3,2,1,0:T(8,128)S(1)} %get-tuple-element.22.refs_4_), channel_id=1, source_target_pairs={{0,2},{2,4},{4,6},{6,8},{8,10},{10,12},{12,14},{14,16},{16,18},{18... | collective-permute-start | bytes 589832 | tf_op jit(solution)/shard_map/ppermute | solution.py:361
  3.0 12.3 %collective-permute-start.1 = (f32[2,24,8,128]{3,2,1,0:T(8,128)S(1)}, f32[2,24,8,128]{3,2,1,0:T(8,128)S(1)}, u32[]{:S(2)}, u32[]{:S(2)}) collective-permute-start(f32[2,24,8,128]{3,2,1,0:T(8,128)S(1)} %get-tuple-element.22.refs_4_), channel_id=1, source_target_pairs={{2,0},{4,2},{6,4},{8,6},{10,8},{12,10},{14,12},{16,14},{18,16},{20... | collective-permute-start | bytes 589832 | tf_op jit(solution)/shard_map/ppermute | solution.py:362
  15.2 3.2 %collective-permute-start.5 = (f32[2,8,8,128]{3,2,1,0:T(8,128)S(1)}, f32[2,8,8,128]{3,2,1,0:T(8,128)S(1)}, u32[]{:S(2)}, u32[]{:S(2)}) collective-permute-start(f32[2,8,8,128]{3,2,1,0:T(8,128)S(1)} %get-tuple-element.29.sent_even), channel_id=1, source_target_pairs={{2,0},{4,2},{6,4},{8,6},{10,8},{12,10},{14,12},{16,14},{18,16},{20... | collective-permute-start | bytes 196616 | tf_op jit(solution)/shard_map/ppermute | solution.py:382
  15.4 3.1 %collective-permute-start.3 = (f32[2,8,8,128]{3,2,1,0:T(8,128)S(1)}, f32[2,8,8,128]{3,2,1,0:T(8,128)S(1)}, u32[]{:S(2)}, u32[]{:S(2)}) collective-permute-start(f32[2,8,8,128]{3,2,1,0:T(8,128)S(1)} %get-tuple-element.28.sent_near), channel_id=1, source_target_pairs={{0,2},{2,0},{4,6},{6,4},{8,10},{10,8},{12,14},{14,12},{16,18},{18,... | collective-permute-start | bytes 196616 | tf_op jit(solution)/shard_map/ppermute | solution.py:391
  16.4 7.9 %collective-permute-start.4 = (f32[2,8,8,128]{3,2,1,0:T(8,128)S(1)}, f32[2,8,8,128]{3,2,1,0:T(8,128)S(1)}, u32[]{:S(2)}, u32[]{:S(2)}) collective-permute-start(f32[2,8,8,128]{3,2,1,0:T(8,128)S(1)} %get-tuple-element.30.sent_odd), channel_id=1, source_target_pairs={{0,2},{2,4},{4,6},{6,8},{8,10},{10,12},{12,14},{14,16},{16,18},{18... | collective-permute-start | bytes 196616 | tf_op jit(solution)/shard_map/ppermute | solution.py:390
  26.2 1.4 %collective-permute-start.6 = (f32[256,128]{1,0:T(8,128)S(1)}, f32[256,128]{1,0:T(8,128)S(1)}, u32[]{:S(2)}, u32[]{:S(2)}) collective-permute-start(f32[256,128]{1,0:T(8,128)S(1)} %get-tuple-element.35), channel_id=1, source_target_pairs={{0,2},{2,0},{4,6},{6,4},{8,10},{10,8},{12,14},{14,12},{16,18},{18,... | collective-permute-start | bytes 393224 | tf_op jit(solution)/shard_map/ppermute | solution.py:404
  43.2 5.2 %collective-permute-start.7 = (f32[4,128]{1,0:T(4,128)S(1)}, f32[4,128]{1,0:T(4,128)S(1)}, u32[]{:S(2)}, u32[]{:S(2)}) collective-permute-start(f32[4,128]{1,0:T(4,128)S(1)} %reduce_sum.9), channel_id=1, source_target_pairs={{0,1},{1,0},{2,3},{3,2},{4,5},{5,4},{6,7},{7,6},{8,9},{9,8},{10,11... | collective-permute-start | bytes 6152 | tf_op jit(solution)/shard_map/ppermute | solution.py:410

commit v9 on v8

--- a/solution.py
+++ b/solution.py
@@ -129,11 +129,9 @@
     out[...] = jnp.zeros_like(out)
 
 
-def start_kernel(pos, _, wells, misfit, later, cpl_in, inv_in, src, nxt_out, intra_out, cross_out, cpl, inv):
+def start_kernel(pos, _, wells, misfit, later, cpl, inv, src, nxt_out, intra_out, cross_out):
     shape = src.shape
     members, unk, planes = shape[:3]
-    cpl[...] = cpl_in[...]
-    inv[...] = inv_in[...]
     even = pos[0] % 2 == 0
     count = planes * shape[3] * shape[4]
     src[...] = later[...] + injected(wells, misfit, pos[0] * count, shape)
@@ -336,6 +334,7 @@
     field = shaped(members, unk, planes, rows, lanes)
     first_size = 2 * unk + unk * unk
     wells = well_cells.reshape(1, -1)
+    cpl, inv = coupling, diag_inverse
     dma = pltpu.SemaphoreType.DMA
     token = pl.pallas_call(
         first_kernel,
@@ -344,18 +343,11 @@
         compiler_params=room(1),
         cost_estimate=busy(1 << 31),
     )()
-    src, nxt, near, far, cpl, inv = pl.pallas_call(
+    src, nxt, near, far = pl.pallas_call(
         start_kernel,
-        out_shape=(
-            field,
-            field,
-            shaped(members, first_size, rows, lanes),
-            shaped(members, first_size, rows, lanes),
-            jax.ShapeDtypeStruct(coupling.shape, BF16),
-            jax.ShapeDtypeStruct(diag_inverse.shape, BF16),
-        ),
+        out_shape=(field, field, shaped(members, first_size, rows, lanes), shaped(members, first_size, rows, lanes)),
         in_specs=[SM] + [VM] * 6,
-        out_specs=(VM,) * 6,
+        out_specs=(VM,) * 4,
         compiler_params=room(6),
     )(pos, token, wells, well_misfit, later_adjoint, coupling, diag_inverse)
     got_up = lax.ppermute(far, "cells", up_pairs)
@@ -378,6 +370,7 @@
         in_specs=[SM] + [VM] * 8,
         out_specs=(VM, VM, VM),
         compiler_params=room(6),
+        cost_estimate=busy(1 << 31),
     )(pos, src, nxt, near, far, got_near, got_up, cpl, inv)
     got_down2 = lax.ppermute(far_even, "cells", down_pairs)
     nxt2, near2, far_odd = pl.pallas_call(
@@ -386,6 +379,7 @@
         in_specs=[SM] + [VM] * 10,
         out_specs=(VM, VM, VM),
         compiler_params=room(6),
+        cost_estimate=busy(1 << 31),
     )(pos, src, nxt, near, far, got_near, got_down, cpl, inv, nxt_even, near_even)
     got_up2 = lax.ppermute(far_odd, "cells", up_pairs)
     got_near2 = lax.ppermute(near2, "cells", intra_pairs)

time: 49.1 us -> 49.1 us (level)
  waiting for transfers between devices: 15 us -> 14 us
  local copies, waits for them, and re-layouts: 1.17 us -> 2.1 us
    unnamed x14, local copies, waits for them, and re-layouts: 1.17 us -> 2.1 us
    ppermute x1, waiting for transfers between devices: 5.8 us -> 4.88 us  [timestep(): got_up2 = lax.ppermute(far_odd, 'cells', up_pairs)]
where the time goes in v9:
time: 49.1 us; the launch traced here: 48.9 us
  blocking collectives  15.5 us (32%)
  waiting for transfers between devices  14 us (29%)
  starting transfers between devices  10.9 us (22%)
  Pallas kernels  4.91 us (10%)
  local copies, waits for them, and re-layouts  2.1 us (4%)
  between operations  0.8 us (2%)
  other arithmetic  0.67 us (1%)
    all_to_all x1, blocking collectives, timestep(): lax.all_to_all(half.reshape(chips, BLK_DEV, params), 'cells', 0, 0, tiled...  15.5 us
    ppermute x1, starting transfers between devices, timestep(): got_down = lax.ppermute(far, 'cells', down_pairs)  8.38 us
    ppermute x1, waiting for transfers between devices, timestep(): got_up2 = lax.ppermute(far_odd, 'cells', up_pairs)  4.88 us
    ppermute x1, waiting for transfers between devices, timestep(): gradient = owned + lax.ppermute(owned, 'ens', [(0, 1), (1, 0)])  4.46 us
    ppermute x1, waiting for transfers between devices, timestep(): got_up = lax.ppermute(far, 'cells', up_pairs)  3.35 us
    unnamed x14, local copies, waits for them, and re-layouts  2.1 us
    pallas_call x1, Pallas kernels, timestep(): pl.pallas_call(select_kernel, out_shape=(jax.ShapeDtypeStruct((nblk, coun...  1.98 us
    pallas_call x1, Pallas kernels, timestep(): pl.pallas_call(make_end(ranks - 1, nblk), out_shape=(field, shaped(nblk /...  1.9 us
  transfers between devices with their start and end apart: 8, of which 4 were waited for; matrix products, arithmetic and copies ran while one was open for 0% of the time, Pallas kernels for 5%

profile of v9, /device:TPU:16, one launch (start us, length us, event | category | flops | bytes accessed | tf_op | source)
XLA Modules:
  0.0 48.9 jit_solution(9588121700875239141)
XLA Ops:
  0.6 0.0 copy-start.2
  0.6 0.0 copy-start.1
  0.7 0.0 copy-start.4
  0.7 0.8 %copy-done.2 = bf16[2,4,4,2,8,128]{5,4,3,2,1,0:T(8,128)(2,1)S(1)} copy-done((bf16[2,4,4,2,8,128]{5,4,3,2,1,0:T(8,128)(2,1)S(1)}, bf16[2,4,4,2,8,128]{5,4,3,2,1,0:T(8,128)(2,1)}, u32[]{:S(2)}) %copy-start.2) | copy-done | bytes 131096
  1.5 0.3 copy-done.1
  1.8 0.0 copy-done.3
  1.9 0.5 %shard_map.87 = (f32[2,4,2,8,128]{4,3,2,1,0:T(8,128)S(1)}, f32[2,4,2,8,128]{4,3,2,1,0:T(8,128)S(1)}, f32[2,24,8,128]{3,2,1,0:T(8,128)S(1)}, f32[2,24,8,128]{3,2,1,0:T(8,128)S(1)}) custom-call(s32[1]{0:T(128)} %bitcast.pos.refs_0_, f32[8,128]{1,0:T(8,128)S(1)} %shard_map.86._, s32[1,256]{1,0:T(1,128)S(1)} %bitcast.3, f32[2,4,256]{2,1,0:T(4,128)S(1)} %copy-done.4, ...), custom_call_target="tpu_custom_call" | custom-call | tf_op jit(solution)/shard_map/pallas_call | solution.py:346
  2.4 0.1 collective-permute-start
  2.5 0.5 %collective-permute-start.2 = (f32[2,24,8,128]{3,2,1,0:T(8,128)S(1)}, f32[2,24,8,128]{3,2,1,0:T(8,128)S(1)}, u32[]{:S(2)}, u32[]{:S(2)}) collective-permute-start(f32[2,24,8,128]{3,2,1,0:T(8,128)S(1)} %get-tuple-element.20.refs_4_), channel_id=1, source_target_pairs={{0,2},{2,4},{4,6},{6,8},{8,10},{10,12},{12,14},{14,16},{16,18},{18... | collective-permute-start | bytes 589832 | tf_op jit(solution)/shard_map/ppermute | solution.py:353
  3.0 8.4 %collective-permute-start.1 = (f32[2,24,8,128]{3,2,1,0:T(8,128)S(1)}, f32[2,24,8,128]{3,2,1,0:T(8,128)S(1)}, u32[]{:S(2)}, u32[]{:S(2)}) collective-permute-start(f32[2,24,8,128]{3,2,1,0:T(8,128)S(1)} %get-tuple-element.20.refs_4_), channel_id=1, source_target_pairs={{2,0},{4,2},{6,4},{8,6},{10,8},{12,10},{14,12},{16,14},{18,16},{20... | collective-permute-start | bytes 589832 | tf_op jit(solution)/shard_map/ppermute | solution.py:354
  11.4 0.0 collective-permute-done.refs_5_.block_near
  11.4 3.3 %collective-permute-done.2.refs_6_.block_even = f32[2,24,8,128]{3,2,1,0:T(8,128)S(1)} collective-permute-done((f32[2,24,8,128]{3,2,1,0:T(8,128)S(1)}, f32[2,24,8,128]{3,2,1,0:T(8,128)S(1)}, u32[]{:S(2)}, u32[]{:S(2)}) %collective-permute-start.2) | collective-permute-done | bytes 196640 | tf_op jit(solution)/shard_map/ppermute | solution.py:353
  14.7 0.5 shard_map.88
  15.2 0.0 copy-start
  15.2 0.0 copy-start.5
  15.2 0.1 collective-permute-start.5
  15.3 0.0 collective-permute-done.1.refs_6_.block_odd
  15.3 1.0 %collective-permute-start.3 = (f32[2,8,8,128]{3,2,1,0:T(8,128)S(1)}, f32[2,8,8,128]{3,2,1,0:T(8,128)S(1)}, u32[]{:S(2)}, u32[]{:S(2)}) collective-permute-start(f32[2,8,8,128]{3,2,1,0:T(8,128)S(1)} %get-tuple-element.24.sent_near), channel_id=1, source_target_pairs={{0,2},{2,0},{4,6},{6,4},{8,10},{10,8},{12,14},{14,12},{16,18},{18,... | collective-permute-start | bytes 196616 | tf_op jit(solution)/shard_map/ppermute | solution.py:385
  16.3 0.1 collective-permute-start.4
  16.4 0.9 %copy-done = bf16[2,4,2,8,128,128]{5,4,3,2,1,0:T(8,128)(2,1)S(1)} copy-done((bf16[2,4,2,8,128,128]{5,4,3,2,1,0:T(8,128)(2,1)S(1)}, bf16[2,4,2,8,128,128]{5,4,3,2,1,0:T(8,128)(2,1)}, u32[]{:S(2)}) %copy-start) | copy-done | bytes 4194328
  17.4 2.0 %shard_map.90 = (bf16[512,2048]{1,0:T(8,128)(2,1)S(1)}, f32[2,4,16,128,128]{4,3,2,1,0:T(8,128)S(1)}) custom-call(s32[1]{0:T(128)} %bitcast.pos.refs_0_, s32[2,8,128]{2,1,0:T(8,128)S(1)} %copy-done.5, bf16[2,4,2,8,128,128]{5,4,3,2,1,0:T(8,128)(2,1)S(1)} %copy-done), custom_call_target="tpu_custom_call" | custom-call | flops 16777216 | tf_op jit(solution)/shard_map/pallas_call | solution.py:356
  19.4 0.0 collective-permute-done.5.got_odd
  19.4 0.0 collective-permute-done.3.got_near
  19.4 4.9 %collective-permute-done.4.got_even = f32[2,8,8,128]{3,2,1,0:T(8,128)S(1)} collective-permute-done((f32[2,8,8,128]{3,2,1,0:T(8,128)S(1)}, f32[2,8,8,128]{3,2,1,0:T(8,128)S(1)}, u32[]{:S(2)}, u32[]{:S(2)}) %collective-permute-start.4) | collective-permute-done | bytes 65568 | tf_op jit(solution)/shard_map/ppermute | solution.py:384
  24.3 1.9 %shard_map.91 = (f32[2,4,2,8,128]{4,3,2,1,0:T(8,128)}, f32[256,128]{1,0:T(8,128)S(1)}, f32[256,128]{1,0:T(8,128)S(1)}) custom-call(s32[1]{0:T(128)} %bitcast.pos.refs_0_, f32[2,4,2,8,128]{4,3,2,1,0:T(8,128)S(1)} %get-tuple-element.17.refs_1_.src, f32[2,4,2,8,128]{4,3,2,1,0:T(8,128)S(1)} %get-tuple-element.23.nxt, ...), custom_call_target="tpu_custom_call" | custom-call | tf_op jit(solution)/shard_map/pallas_call | solution.py:386
  26.2 0.1 collective-permute-start.6
  26.3 1.3 %collective-permute-done.6 = f32[256,128]{1,0:T(8,128)S(1)} collective-permute-done((f32[256,128]{1,0:T(8,128)S(1)}, f32[256,128]{1,0:T(8,128)S(1)}, u32[]{:S(2)}, u32[]{:S(2)}) %collective-permute-start.6) | collective-permute-done | bytes 131104 | tf_op jit(solution)/shard_map/ppermute | solution.py:398
  27.6 15.5 %all_to_all.5 = f32[64,4,128]{2,1,0:T(4,128)S(1)} all-to-all(f32[64,4,128]{2,1,0:T(4,128)S(1)} %bitcast.4), channel_id=1, replica_groups={{0,4,8,12,16,20,24,28,32,36,40,44,48,52,56,60,64,68,72,76,80,84,88,92,9..., dimensions={0} | all-to-all | bytes 262144 | tf_op jit(solution)/shard_map/all_to_all | solution.py:400
  43.1 0.1 reduce_sum.9
  43.2 0.7 %collective-permute-start.7 = (f32[4,128]{1,0:T(4,128)S(1)}, f32[4,128]{1,0:T(4,128)S(1)}, u32[]{:S(2)}, u32[]{:S(2)}) collective-permute-start(f32[4,128]{1,0:T(4,128)S(1)} %reduce_sum.9), channel_id=1, source_target_pairs={{0,1},{1,0},{2,3},{3,2},{4,5},{5,4},{6,7},{7,6},{8,9},{9,8},{10,11... | collective-permute-start | bytes 6152 | tf_op jit(solution)/shard_map/ppermute | solution.py:404
  43.9 4.5 %collective-permute-done.7 = f32[4,128]{1,0:T(4,128)S(1)} collective-permute-done((f32[4,128]{1,0:T(4,128)S(1)}, f32[4,128]{1,0:T(4,128)S(1)}, u32[]{:S(2)}, u32[]{:S(2)}) %collective-permute-start.7) | collective-permute-done | bytes 2080 | tf_op jit(solution)/shard_map/ppermute | solution.py:404
  48.4 0.6 %add.7 = f32[4,128]{1,0:T(4,128)} add(f32[4,128]{1,0:T(4,128)S(1)} %reduce_sum.9, f32[4,128]{1,0:T(4,128)S(1)} %collective-permute-done.7) | non-fusion elementwise | flops 512 | bytes 6144 | tf_op jit(solution)/shard_map/add | solution.py:404
  (8 shorter events, 0.1 us)
Async XLA Ops:
  0.6 0.9 %copy-start.2 = (bf16[2,4,4,2,8,128]{5,4,3,2,1,0:T(8,128)(2,1)S(1)}, bf16[2,4,4,2,8,128]{5,4,3,2,1,0:T(8,128)(2,1)}, u32[]{:S(2)}) copy-start(bf16[2,4,4,2,8,128]{5,4,3,2,1,0:T(8,128)(2,1)} %inv.3) | copy-start | bytes 393220
  0.6 1.2 %copy-start.1 = (bf16[2,6,4,4,2,8,128]{6,5,4,3,2,1,0:T(8,128)(2,1)S(1)}, bf16[2,6,4,4,2,8,128]{6,5,4,3,2,1,0:T(8,128)(2,1)}, u32[]{:S(2)}) copy-start(bf16[2,6,4,4,2,8,128]{6,5,4,3,2,1,0:T(8,128)(2,1)} %cpl.3) | copy-start | bytes 2359300
  0.7 1.2 %copy-start.4 = (f32[2,4,256]{2,1,0:T(4,128)S(1)}, f32[2,4,256]{2,1,0:T(4,128)}, u32[]{:S(2)}) copy-start(f32[2,4,256]{2,1,0:T(4,128)} %misfit.1) | copy-start | bytes 24580
  0.7 1.2 %copy-start.6 = (s32[256]{0:T(256)S(1)}, s32[256]{0:T(256)}, u32[]{:S(2)}) copy-start(s32[256]{0:T(256)} %param.11) | copy-start | bytes 3076
  0.7 1.2 %copy-start.3 = (f32[2,4,2,8,128]{4,3,2,1,0:T(8,128)S(1)}, f32[2,4,2,8,128]{4,3,2,1,0:T(8,128)}, u32[]{:S(2)}) copy-start(f32[2,4,2,8,128]{4,3,2,1,0:T(8,128)} %later.1) | copy-start | bytes 196612
  2.4 9.0 %collective-permute-start = (f32[2,24,8,128]{3,2,1,0:T(8,128)S(1)}, f32[2,24,8,128]{3,2,1,0:T(8,128)S(1)}, u32[]{:S(2)}, u32[]{:S(2)}) collective-permute-start(f32[2,24,8,128]{3,2,1,0:T(8,128)S(1)} %get-tuple-element.19.refs_3_), channel_id=1, source_target_pairs={{0,2},{2,0},{4,6},{6,4},{8,10},{10,8},{12,14},{14,12},{16,18},{18,... | collective-permute-start | bytes 589832 | tf_op jit(solution)/shard_map/ppermute | solution.py:355
  2.5 12.2 %collective-permute-start.2 = (f32[2,24,8,128]{3,2,1,0:T(8,128)S(1)}, f32[2,24,8,128]{3,2,1,0:T(8,128)S(1)}, u32[]{:S(2)}, u32[]{:S(2)}) collective-permute-start(f32[2,24,8,128]{3,2,1,0:T(8,128)S(1)} %get-tuple-element.20.refs_4_), channel_id=1, source_target_pairs={{0,2},{2,4},{4,6},{6,8},{8,10},{10,12},{12,14},{14,16},{16,18},{18... | collective-permute-start | bytes 589832 | tf_op jit(solution)/shard_map/ppermute | solution.py:353
  3.0 12.3 %collective-permute-start.1 = (f32[2,24,8,128]{3,2,1,0:T(8,128)S(1)}, f32[2,24,8,128]{3,2,1,0:T(8,128)S(1)}, u32[]{:S(2)}, u32[]{:S(2)}) collective-permute-start(f32[2,24,8,128]{3,2,1,0:T(8,128)S(1)} %get-tuple-element.20.refs_4_), channel_id=1, source_target_pairs={{2,0},{4,2},{6,4},{8,6},{10,8},{12,10},{14,12},{16,14},{18,16},{20... | collective-permute-start | bytes 589832 | tf_op jit(solution)/shard_map/ppermute | solution.py:354
  15.2 2.2 %copy-start = (bf16[2,4,2,8,128,128]{5,4,3,2,1,0:T(8,128)(2,1)S(1)}, bf16[2,4,2,8,128,128]{5,4,3,2,1,0:T(8,128)(2,1)}, u32[]{:S(2)}) copy-start(bf16[2,4,2,8,128,128]{5,4,3,2,1,0:T(8,128)(2,1)} %sens.1) | copy-start | bytes 12582916
  15.2 2.2 %copy-start.5 = (s32[2,8,128]{2,1,0:T(8,128)S(1)}, s32[2,8,128]{2,1,0:T(8,128)}, u32[]{:S(2)}) copy-start(s32[2,8,128]{2,1,0:T(8,128)} %bmap.1) | copy-start | bytes 24580
  15.2 4.2 %collective-permute-start.5 = (f32[2,8,8,128]{3,2,1,0:T(8,128)S(1)}, f32[2,8,8,128]{3,2,1,0:T(8,128)S(1)}, u32[]{:S(2)}, u32[]{:S(2)}) collective-permute-start(f32[2,8,8,128]{3,2,1,0:T(8,128)S(1)} %get-tuple-element.25.sent_even), channel_id=1, source_target_pairs={{2,0},{4,2},{6,4},{8,6},{10,8},{12,10},{14,12},{16,14},{18,16},{20... | collective-permute-start | bytes 196616 | tf_op jit(solution)/shard_map/ppermute | solution.py:375
  15.3 4.0 %collective-permute-start.3 = (f32[2,8,8,128]{3,2,1,0:T(8,128)S(1)}, f32[2,8,8,128]{3,2,1,0:T(8,128)S(1)}, u32[]{:S(2)}, u32[]{:S(2)}) collective-permute-start(f32[2,8,8,128]{3,2,1,0:T(8,128)S(1)} %get-tuple-element.24.sent_near), channel_id=1, source_target_pairs={{0,2},{2,0},{4,6},{6,4},{8,10},{10,8},{12,14},{14,12},{16,18},{18,... | collective-permute-start | bytes 196616 | tf_op jit(solution)/shard_map/ppermute | solution.py:385
  16.3 7.9 %collective-permute-start.4 = (f32[2,8,8,128]{3,2,1,0:T(8,128)S(1)}, f32[2,8,8,128]{3,2,1,0:T(8,128)S(1)}, u32[]{:S(2)}, u32[]{:S(2)}) collective-permute-start(f32[2,8,8,128]{3,2,1,0:T(8,128)S(1)} %get-tuple-element.26.sent_odd), channel_id=1, source_target_pairs={{0,2},{2,4},{4,6},{6,8},{8,10},{10,12},{12,14},{14,16},{16,18},{18... | collective-permute-start | bytes 196616 | tf_op jit(solution)/shard_map/ppermute | solution.py:384
  26.2 1.4 %collective-permute-start.6 = (f32[256,128]{1,0:T(8,128)S(1)}, f32[256,128]{1,0:T(8,128)S(1)}, u32[]{:S(2)}, u32[]{:S(2)}) collective-permute-start(f32[256,128]{1,0:T(8,128)S(1)} %get-tuple-element.31), channel_id=1, source_target_pairs={{0,2},{2,0},{4,6},{6,4},{8,10},{10,8},{12,14},{14,12},{16,18},{18,... | collective-permute-start | bytes 393224 | tf_op jit(solution)/shard_map/ppermute | solution.py:398
  43.2 5.2 %collective-permute-start.7 = (f32[4,128]{1,0:T(4,128)S(1)}, f32[4,128]{1,0:T(4,128)S(1)}, u32[]{:S(2)}, u32[]{:S(2)}) collective-permute-start(f32[4,128]{1,0:T(4,128)S(1)} %reduce_sum.9), channel_id=1, source_target_pairs={{0,1},{1,0},{2,3},{3,2},{4,5},{5,4},{6,7},{7,6},{8,9},{9,8},{10,11... | collective-permute-start | bytes 6152 | tf_op jit(solution)/shard_map/ppermute | solution.py:404

commit v10 on v9

--- a/solution.py
+++ b/solution.py
@@ -320,6 +320,21 @@
     return jax.ShapeDtypeStruct(shape, F32)
 
 
+def closed_ring(ranks):
+    target = {i: i + 1 for i in range(ranks - 1)}
+    row = ranks // 8
+    if ranks % 64 or row < 8:
+        target[ranks - 1] = 0
+        return sorted(target.items())
+    spare = ranks - 1
+    stops = [row * k + row - 2 for k in range(3, -1, -1)] + list(range(row - 6, 0, -4))
+    for even in stops:
+        target[spare] = even + 1
+        spare = even
+    target[spare] = 0
+    return sorted(target.items())
+
+
 def timestep(later_adjoint, coupling, diag_inverse, sensitivity, well_cells, well_misfit, block_map):
     members, unk, planes, rows, lanes = later_adjoint.shape
     count = planes * rows * lanes
@@ -328,8 +343,8 @@
     nblk = ranks * BLK_DEV
     pos = lax.axis_index("cells").astype(jnp.int32).reshape(1)
     intra_pairs = [(i, i ^ 1) for i in range(ranks)]
-    up_pairs = [(i, (i + 1) % ranks) for i in range(ranks)]
-    down_pairs = [((i + 1) % ranks, i) for i in range(ranks)]
+    up_pairs = closed_ring(ranks)
+    down_pairs = [(there, here) for here, there in up_pairs]
 
     field = shaped(members, unk, planes, rows, lanes)
     first_size = 2 * unk + unk * unk

time: 49.1 us -> 48.6 us (0.990)
  blocking collectives: 15.5 us -> 20.9 us
  starting transfers between devices: 10.9 us -> 6.43 us
  local copies, waits for them, and re-layouts: 2.1 us -> 1.17 us
    ppermute x1, starting transfers between devices: 8.38 us -> 1.61 us  [timestep(): got_down = lax.ppermute(far, 'cells', down_pairs)]
    all_to_all x1, blocking collectives: 15.5 us -> 20.9 us  [timestep(): lax.all_to_all(half.reshape(chips, BLK_DEV, params), 'cells', 0, 0, tiled...]
    ppermute x1, starting transfers between devices: 0.08 us -> 2.84 us  [timestep(): got_down2 = lax.ppermute(far_even, 'cells', down_pairs)]
    unnamed x14, local copies, waits for them, and re-layouts: 2.1 us -> 1.17 us
    ppermute x1, starting transfers between devices: 1 us -> 0.09 us  [timestep(): got_near2 = lax.ppermute(near2, 'cells', intra_pairs)]
    ppermute x1, waiting for transfers between devices: 4.88 us -> 4.23 us  [timestep(): got_up2 = lax.ppermute(far_odd, 'cells', up_pairs)]
where the time goes in v10:
time: 48.6 us; the launch traced here: 48.5 us
  blocking collectives  20.9 us (43%)
  waiting for transfers between devices  13.7 us (28%)
  starting transfers between devices  6.43 us (13%)
  Pallas kernels  4.89 us (10%)
  local copies, waits for them, and re-layouts  1.17 us (2%)
  between operations  0.79 us (2%)
  other arithmetic  0.67 us (1%)
    all_to_all x1, blocking collectives, timestep(): lax.all_to_all(half.reshape(chips, BLK_DEV, params), 'cells', 0, 0, tiled...  20.9 us
    ppermute x1, waiting for transfers between devices, timestep(): gradient = owned + lax.ppermute(owned, 'ens', [(0, 1), (1, 0)])  4.46 us
    ppermute x1, waiting for transfers between devices, timestep(): got_up2 = lax.ppermute(far_odd, 'cells', up_pairs)  4.23 us
    ppermute x1, waiting for transfers between devices, timestep(): got_up = lax.ppermute(far, 'cells', up_pairs)  3.64 us
    ppermute x1, starting transfers between devices, timestep(): got_down2 = lax.ppermute(far_even, 'cells', down_pairs)  2.84 us
    pallas_call x1, Pallas kernels, timestep(): pl.pallas_call(select_kernel, out_shape=(jax.ShapeDtypeStruct((nblk, coun...  1.98 us
    pallas_call x1, Pallas kernels, timestep(): pl.pallas_call(make_end(ranks - 1, nblk), out_shape=(field, shaped(nblk /...  1.9 us
    ppermute x1, starting transfers between devices, timestep(): got_down = lax.ppermute(far, 'cells', down_pairs)  1.61 us
  transfers between devices with their start and end apart: 8, of which 4 were waited for; matrix products, arithmetic and copies ran while one was open for 0% of the time, Pallas kernels for 5%

profile of v10, /device:TPU:16, one launch (start us, length us, event | category | flops | bytes accessed | tf_op | source)
XLA Modules:
  0.0 48.5 jit_solution(8211275853290289156)
XLA Ops:
  0.6 0.0 copy-start.2
  0.6 0.0 copy-start.1
  0.7 0.0 copy-start.4
  0.7 0.0 copy-start.6
  0.7 0.8 %copy-done.2 = bf16[2,4,4,2,8,128]{5,4,3,2,1,0:T(8,128)(2,1)S(1)} copy-done((bf16[2,4,4,2,8,128]{5,4,3,2,1,0:T(8,128)(2,1)S(1)}, bf16[2,4,4,2,8,128]{5,4,3,2,1,0:T(8,128)(2,1)}, u32[]{:S(2)}) %copy-start.2) | copy-done | bytes 131096
  1.5 0.3 copy-done.1
  1.8 0.0 copy-done.3
  1.9 0.5 %shard_map.87 = (f32[2,4,2,8,128]{4,3,2,1,0:T(8,128)S(1)}, f32[2,4,2,8,128]{4,3,2,1,0:T(8,128)S(1)}, f32[2,24,8,128]{3,2,1,0:T(8,128)S(1)}, f32[2,24,8,128]{3,2,1,0:T(8,128)S(1)}) custom-call(s32[1]{0:T(128)} %bitcast.pos.refs_0_, f32[8,128]{1,0:T(8,128)S(1)} %shard_map.86._, s32[1,256]{1,0:T(1,128)S(1)} %bitcast.3, f32[2,4,256]{2,1,0:T(4,128)S(1)} %copy-done.4, ...), custom_call_target="tpu_custom_call" | custom-call | tf_op jit(solution)/shard_map/pallas_call | solution.py:361
  2.4 0.1 collective-permute-start
  2.5 0.5 %collective-permute-start.2 = (f32[2,24,8,128]{3,2,1,0:T(8,128)S(1)}, f32[2,24,8,128]{3,2,1,0:T(8,128)S(1)}, u32[]{:S(2)}, u32[]{:S(2)}) collective-permute-start(f32[2,24,8,128]{3,2,1,0:T(8,128)S(1)} %get-tuple-element.20.refs_4_), channel_id=1, source_target_pairs={{0,2},{2,4},{4,0},{6,8},{8,10},{10,12},{12,6},{14,16},{16,18},{18,... | collective-permute-start | bytes 589832 | tf_op jit(solution)/shard_map/ppermute | solution.py:368
  3.0 1.6 %collective-permute-start.1 = (f32[2,24,8,128]{3,2,1,0:T(8,128)S(1)}, f32[2,24,8,128]{3,2,1,0:T(8,128)S(1)}, u32[]{:S(2)}, u32[]{:S(2)}) collective-permute-start(f32[2,24,8,128]{3,2,1,0:T(8,128)S(1)} %get-tuple-element.20.refs_4_), channel_id=1, source_target_pairs={{2,0},{4,2},{0,4},{8,6},{10,8},{12,10},{6,12},{16,14},{18,16},{20,... | collective-permute-start | bytes 589832 | tf_op jit(solution)/shard_map/ppermute | solution.py:369
  4.6 0.0 collective-permute-done.refs_5_.block_near
  4.6 3.6 %collective-permute-done.2.refs_6_.block_even = f32[2,24,8,128]{3,2,1,0:T(8,128)S(1)} collective-permute-done((f32[2,24,8,128]{3,2,1,0:T(8,128)S(1)}, f32[2,24,8,128]{3,2,1,0:T(8,128)S(1)}, u32[]{:S(2)}, u32[]{:S(2)}) %collective-permute-start.2) | collective-permute-done | bytes 196640 | tf_op jit(solution)/shard_map/ppermute | solution.py:368
  8.2 0.5 shard_map.88
  8.7 0.0 copy-start
  8.7 0.0 copy-start.5
  8.7 2.8 %collective-permute-start.5 = (f32[2,8,8,128]{3,2,1,0:T(8,128)S(1)}, f32[2,8,8,128]{3,2,1,0:T(8,128)S(1)}, u32[]{:S(2)}, u32[]{:S(2)}) collective-permute-start(f32[2,8,8,128]{3,2,1,0:T(8,128)S(1)} %get-tuple-element.25.sent_even), channel_id=1, source_target_pairs={{2,0},{4,2},{0,4},{8,6},{10,8},{12,10},{6,12},{16,14},{18,16},{20,... | collective-permute-start | bytes 196616 | tf_op jit(solution)/shard_map/ppermute | solution.py:390
  11.6 0.0 collective-permute-done.1.refs_6_.block_odd
  11.6 0.1 collective-permute-start.3
  11.7 0.5 %collective-permute-start.4 = (f32[2,8,8,128]{3,2,1,0:T(8,128)S(1)}, f32[2,8,8,128]{3,2,1,0:T(8,128)S(1)}, u32[]{:S(2)}, u32[]{:S(2)}) collective-permute-start(f32[2,8,8,128]{3,2,1,0:T(8,128)S(1)} %get-tuple-element.26.sent_odd), channel_id=1, source_target_pairs={{0,2},{2,4},{4,0},{6,8},{8,10},{10,12},{12,6},{14,16},{16,18},{18,... | collective-permute-start | bytes 196616 | tf_op jit(solution)/shard_map/ppermute | solution.py:399
  12.2 2.0 %shard_map.90 = (bf16[512,2048]{1,0:T(8,128)(2,1)S(1)}, f32[2,4,16,128,128]{4,3,2,1,0:T(8,128)S(1)}) custom-call(s32[1]{0:T(128)} %bitcast.pos.refs_0_, s32[2,8,128]{2,1,0:T(8,128)S(1)} %copy-done.5, bf16[2,4,2,8,128,128]{5,4,3,2,1,0:T(8,128)(2,1)S(1)} %copy-done), custom_call_target="tpu_custom_call" | custom-call | flops 16777216 | tf_op jit(solution)/shard_map/pallas_call | solution.py:371
  14.2 0.0 collective-permute-done.5.got_odd
  14.2 0.0 collective-permute-done.3.got_near
  14.2 4.2 %collective-permute-done.4.got_even = f32[2,8,8,128]{3,2,1,0:T(8,128)S(1)} collective-permute-done((f32[2,8,8,128]{3,2,1,0:T(8,128)S(1)}, f32[2,8,8,128]{3,2,1,0:T(8,128)S(1)}, u32[]{:S(2)}, u32[]{:S(2)}) %collective-permute-start.4) | collective-permute-done | bytes 65568 | tf_op jit(solution)/shard_map/ppermute | solution.py:399
  18.4 1.9 %shard_map.91 = (f32[2,4,2,8,128]{4,3,2,1,0:T(8,128)}, f32[256,128]{1,0:T(8,128)S(1)}, f32[256,128]{1,0:T(8,128)S(1)}) custom-call(s32[1]{0:T(128)} %bitcast.pos.refs_0_, f32[2,4,2,8,128]{4,3,2,1,0:T(8,128)S(1)} %get-tuple-element.17.refs_1_.src, f32[2,4,2,8,128]{4,3,2,1,0:T(8,128)S(1)} %get-tuple-element.23.nxt, ...), custom_call_target="tpu_custom_call" | custom-call | tf_op jit(solution)/shard_map/pallas_call | solution.py:401
  20.3 0.1 collective-permute-start.6
  20.4 1.3 %collective-permute-done.6 = f32[256,128]{1,0:T(8,128)S(1)} collective-permute-done((f32[256,128]{1,0:T(8,128)S(1)}, f32[256,128]{1,0:T(8,128)S(1)}, u32[]{:S(2)}, u32[]{:S(2)}) %collective-permute-start.6) | collective-permute-done | bytes 131104 | tf_op jit(solution)/shard_map/ppermute | solution.py:413
  21.8 20.9 %all_to_all.5 = f32[64,4,128]{2,1,0:T(4,128)S(1)} all-to-all(f32[64,4,128]{2,1,0:T(4,128)S(1)} %bitcast.4), channel_id=1, replica_groups={{0,4,8,12,16,20,24,28,32,36,40,44,48,52,56,60,64,68,72,76,80,84,88,92,9..., dimensions={0} | all-to-all | bytes 262144 | tf_op jit(solution)/shard_map/all_to_all | solution.py:415
  42.7 0.1 reduce_sum.9
  42.8 0.7 %collective-permute-start.7 = (f32[4,128]{1,0:T(4,128)S(1)}, f32[4,128]{1,0:T(4,128)S(1)}, u32[]{:S(2)}, u32[]{:S(2)}) collective-permute-start(f32[4,128]{1,0:T(4,128)S(1)} %reduce_sum.9), channel_id=1, source_target_pairs={{0,1},{1,0},{2,3},{3,2},{4,5},{5,4},{6,7},{7,6},{8,9},{9,8},{10,11... | collective-permute-start | bytes 6152 | tf_op jit(solution)/shard_map/ppermute | solution.py:419
  43.5 4.5 %collective-permute-done.7 = f32[4,128]{1,0:T(4,128)S(1)} collective-permute-done((f32[4,128]{1,0:T(4,128)S(1)}, f32[4,128]{1,0:T(4,128)S(1)}, u32[]{:S(2)}, u32[]{:S(2)}) %collective-permute-start.7) | collective-permute-done | bytes 2080 | tf_op jit(solution)/shard_map/ppermute | solution.py:419
  47.9 0.6 %add.7 = f32[4,128]{1,0:T(4,128)} add(f32[4,128]{1,0:T(4,128)S(1)} %reduce_sum.9, f32[4,128]{1,0:T(4,128)S(1)} %collective-permute-done.7) | non-fusion elementwise | flops 512 | bytes 6144 | tf_op jit(solution)/shard_map/add | solution.py:419
  (8 shorter events, 0.0 us)
Async XLA Ops:
  0.6 0.9 %copy-start.2 = (bf16[2,4,4,2,8,128]{5,4,3,2,1,0:T(8,128)(2,1)S(1)}, bf16[2,4,4,2,8,128]{5,4,3,2,1,0:T(8,128)(2,1)}, u32[]{:S(2)}) copy-start(bf16[2,4,4,2,8,128]{5,4,3,2,1,0:T(8,128)(2,1)} %inv.3) | copy-start | bytes 393220
  0.6 1.2 %copy-start.1 = (bf16[2,6,4,4,2,8,128]{6,5,4,3,2,1,0:T(8,128)(2,1)S(1)}, bf16[2,6,4,4,2,8,128]{6,5,4,3,2,1,0:T(8,128)(2,1)}, u32[]{:S(2)}) copy-start(bf16[2,6,4,4,2,8,128]{6,5,4,3,2,1,0:T(8,128)(2,1)} %cpl.3) | copy-start | bytes 2359300
  0.7 1.2 %copy-start.4 = (f32[2,4,256]{2,1,0:T(4,128)S(1)}, f32[2,4,256]{2,1,0:T(4,128)}, u32[]{:S(2)}) copy-start(f32[2,4,256]{2,1,0:T(4,128)} %misfit.1) | copy-start | bytes 24580
  0.7 1.2 %copy-start.6 = (s32[256]{0:T(256)S(1)}, s32[256]{0:T(256)}, u32[]{:S(2)}) copy-start(s32[256]{0:T(256)} %param.11) | copy-start | bytes 3076
  0.7 1.2 %copy-start.3 = (f32[2,4,2,8,128]{4,3,2,1,0:T(8,128)S(1)}, f32[2,4,2,8,128]{4,3,2,1,0:T(8,128)}, u32[]{:S(2)}) copy-start(f32[2,4,2,8,128]{4,3,2,1,0:T(8,128)} %later.1) | copy-start | bytes 196612
  2.4 2.2 %collective-permute-start = (f32[2,24,8,128]{3,2,1,0:T(8,128)S(1)}, f32[2,24,8,128]{3,2,1,0:T(8,128)S(1)}, u32[]{:S(2)}, u32[]{:S(2)}) collective-permute-start(f32[2,24,8,128]{3,2,1,0:T(8,128)S(1)} %get-tuple-element.19.refs_3_), channel_id=1, source_target_pairs={{0,2},{2,0},{4,6},{6,4},{8,10},{10,8},{12,14},{14,12},{16,18},{18,... | collective-permute-start | bytes 589832 | tf_op jit(solution)/shard_map/ppermute | solution.py:370
  2.5 5.8 %collective-permute-start.2 = (f32[2,24,8,128]{3,2,1,0:T(8,128)S(1)}, f32[2,24,8,128]{3,2,1,0:T(8,128)S(1)}, u32[]{:S(2)}, u32[]{:S(2)}) collective-permute-start(f32[2,24,8,128]{3,2,1,0:T(8,128)S(1)} %get-tuple-element.20.refs_4_), channel_id=1, source_target_pairs={{0,2},{2,4},{4,0},{6,8},{8,10},{10,12},{12,6},{14,16},{16,18},{18,... | collective-permute-start | bytes 589832 | tf_op jit(solution)/shard_map/ppermute | solution.py:368
  3.0 8.6 %collective-permute-start.1 = (f32[2,24,8,128]{3,2,1,0:T(8,128)S(1)}, f32[2,24,8,128]{3,2,1,0:T(8,128)S(1)}, u32[]{:S(2)}, u32[]{:S(2)}) collective-permute-start(f32[2,24,8,128]{3,2,1,0:T(8,128)S(1)} %get-tuple-element.20.refs_4_), channel_id=1, source_target_pairs={{2,0},{4,2},{0,4},{8,6},{10,8},{12,10},{6,12},{16,14},{18,16},{20,... | collective-permute-start | bytes 589832 | tf_op jit(solution)/shard_map/ppermute | solution.py:369
  8.7 3.5 %copy-start = (bf16[2,4,2,8,128,128]{5,4,3,2,1,0:T(8,128)(2,1)S(1)}, bf16[2,4,2,8,128,128]{5,4,3,2,1,0:T(8,128)(2,1)}, u32[]{:S(2)}) copy-start(bf16[2,4,2,8,128,128]{5,4,3,2,1,0:T(8,128)(2,1)} %sens.1) | copy-start | bytes 12582916
  8.7 3.5 %copy-start.5 = (s32[2,8,128]{2,1,0:T(8,128)S(1)}, s32[2,8,128]{2,1,0:T(8,128)}, u32[]{:S(2)}) copy-start(s32[2,8,128]{2,1,0:T(8,128)} %bmap.1) | copy-start | bytes 24580
  8.7 5.5 %collective-permute-start.5 = (f32[2,8,8,128]{3,2,1,0:T(8,128)S(1)}, f32[2,8,8,128]{3,2,1,0:T(8,128)S(1)}, u32[]{:S(2)}, u32[]{:S(2)}) collective-permute-start(f32[2,8,8,128]{3,2,1,0:T(8,128)S(1)} %get-tuple-element.25.sent_even), channel_id=1, source_target_pairs={{2,0},{4,2},{0,4},{8,6},{10,8},{12,10},{6,12},{16,14},{18,16},{20,... | collective-permute-start | bytes 196616 | tf_op jit(solution)/shard_map/ppermute | solution.py:390
  11.6 2.6 %collective-permute-start.3 = (f32[2,8,8,128]{3,2,1,0:T(8,128)S(1)}, f32[2,8,8,128]{3,2,1,0:T(8,128)S(1)}, u32[]{:S(2)}, u32[]{:S(2)}) collective-permute-start(f32[2,8,8,128]{3,2,1,0:T(8,128)S(1)} %get-tuple-element.24.sent_near), channel_id=1, source_target_pairs={{0,2},{2,0},{4,6},{6,4},{8,10},{10,8},{12,14},{14,12},{16,18},{18,... | collective-permute-start | bytes 196616 | tf_op jit(solution)/shard_map/ppermute | solution.py:400
  11.7 6.7 %collective-permute-start.4 = (f32[2,8,8,128]{3,2,1,0:T(8,128)S(1)}, f32[2,8,8,128]{3,2,1,0:T(8,128)S(1)}, u32[]{:S(2)}, u32[]{:S(2)}) collective-permute-start(f32[2,8,8,128]{3,2,1,0:T(8,128)S(1)} %get-tuple-element.26.sent_odd), channel_id=1, source_target_pairs={{0,2},{2,4},{4,0},{6,8},{8,10},{10,12},{12,6},{14,16},{16,18},{18,... | collective-permute-start | bytes 196616 | tf_op jit(solution)/shard_map/ppermute | solution.py:399
  20.3 1.4 %collective-permute-start.6 = (f32[256,128]{1,0:T(8,128)S(1)}, f32[256,128]{1,0:T(8,128)S(1)}, u32[]{:S(2)}, u32[]{:S(2)}) collective-permute-start(f32[256,128]{1,0:T(8,128)S(1)} %get-tuple-element.31), channel_id=1, source_target_pairs={{0,2},{2,0},{4,6},{6,4},{8,10},{10,8},{12,14},{14,12},{16,18},{18,... | collective-permute-start | bytes 393224 | tf_op jit(solution)/shard_map/ppermute | solution.py:413
  42.8 5.2 %collective-permute-start.7 = (f32[4,128]{1,0:T(4,128)S(1)}, f32[4,128]{1,0:T(4,128)S(1)}, u32[]{:S(2)}, u32[]{:S(2)}) collective-permute-start(f32[4,128]{1,0:T(4,128)S(1)} %reduce_sum.9), channel_id=1, source_target_pairs={{0,1},{1,0},{2,3},{3,2},{4,5},{5,4},{6,7},{7,6},{8,9},{9,8},{10,11... | collective-permute-start | bytes 6152 | tf_op jit(solution)/shard_map/ppermute | solution.py:419

commit v11 on v10

--- a/solution.py
+++ b/solution.py
@@ -256,10 +256,19 @@
                 turned[m, u, g] = sens[m, u, g // rows, g % rows].astype(F32).T
 
 
+def block_sums(rows, grads, params):
+    both = lax.dot_general(rows, grads, (((1,), (1,)), ((), ())), preferred_element_type=F32)
+    return both[:, :params] + both[:, params:]
+
+
+def own_kernel(onehot, grads, out):
+    out[...] = block_sums(onehot[: out.shape[0]], grads[...], out.shape[1])
+
+
 def make_end(last, nblk):
     def end_kernel(
         pos, src, nxt, block_near, block_even, block_odd, sent_near, sent_even, sent_odd, got_near, got_even, got_odd,
-        cpl, inv, onehot, turned, adj_out, mine_out, other_out, adj, grads, sems,
+        cpl, inv, onehot, turned, adj_out, other_out, grads, adj, sems,
     ):
         members, unk, planes, rows, lanes = src.shape
         params = turned.shape[-2]
@@ -291,12 +300,7 @@
                 lo = (total - hi.astype(F32)).astype(BF16)
                 grads[p : p + step, g * lanes : (g + 1) * lanes] = hi
                 grads[params + p : params + p + step, g * lanes : (g + 1) * lanes] = lo
-        both = lax.dot_general(
-            onehot[...], grads[...], (((1,), (1,)), ((), ())), preferred_element_type=F32
-        )
-        out = both[:, :params] + both[:, params:]
-        mine_out[...] = out[:half_rows]
-        other_out[...] = out[half_rows:]
+        other_out[...] = block_sums(onehot[half_rows:], grads[...], params)
         store.wait()
 
     return end_kernel
@@ -327,10 +331,13 @@
         target[ranks - 1] = 0
         return sorted(target.items())
     spare = ranks - 1
-    stops = [row * k + row - 2 for k in range(3, -1, -1)] + list(range(row - 6, 0, -4))
+    near_end = row - 4
+    stops = [ranks - 4] + [row * k + near_end for k in range(3, -1, -1)] + list(range(near_end - 4, 3, -4))
     for even in stops:
         target[spare] = even + 1
         spare = even
+    target[spare] = 3
+    spare = 2
     target[spare] = 0
     return sorted(target.items())
 
@@ -398,19 +405,29 @@
     )(pos, src, nxt, near, far, got_near, got_down, cpl, inv, nxt_even, near_even)
     got_up2 = lax.ppermute(far_odd, "cells", up_pairs)
     got_near2 = lax.ppermute(near2, "cells", intra_pairs)
-    adjoint, mine, other = pl.pallas_call(
+    adjoint, other, grads = pl.pallas_call(
         make_end(ranks - 1, nblk),
-        out_shape=(field, shaped(nblk // 2, params), shaped(nblk // 2, params)),
+        out_shape=(
+            field, shaped(nblk // 2, params), jax.ShapeDtypeStruct((2 * params, count), BF16)
+        ),
         in_specs=[SM] + [VM] * 15,
         out_specs=(HB, VM, VM),
-        scratch_shapes=[pltpu.VMEM(field.shape, F32), pltpu.VMEM((2 * params, count), BF16), dma((1,))],
+        scratch_shapes=[pltpu.VMEM(field.shape, F32), dma((1,))],
         compiler_params=room(16),
     )(
         pos, src, nxt2, got_near, got_up, got_down, near2, far_even, far_odd, got_near2, got_up2, got_down2,
         cpl, inv, onehot, turned,
     )
     chips = ranks // 2
-    half = mine + lax.ppermute(other, "cells", intra_pairs)
+    got_half = lax.ppermute(other, "cells", intra_pairs)
+    mine = pl.pallas_call(
+        own_kernel,
+        out_shape=shaped(nblk // 2, params),
+        in_specs=[VM, VM],
+        out_specs=VM,
+        compiler_params=room(6),
+    )(onehot, grads)
+    half = mine + got_half
     same_core = [[core + 2 * chip for chip in range(chips)] for core in range(2)]
     parts = lax.all_to_all(
         half.reshape(chips, BLK_DEV, params), "cells", 0, 0, tiled=True, axis_index_groups=same_core

time: 48.6 us -> 48.7 us (level)
  waiting for transfers between devices: 13.7 us -> 10.8 us
  blocking collectives: 20.9 us -> 23.3 us
  Pallas kernels: 4.89 us -> 5.41 us
    all_to_all x1, blocking collectives: 20.9 us -> 23.3 us  [timestep(): lax.all_to_all(half.reshape(chips, BLK_DEV, params), 'cells', 0, 0, tiled...]
    ppermute x1, waiting for transfers between devices: 4.23 us -> 1.83 us  [timestep(): got_up2 = lax.ppermute(far_odd, 'cells', up_pairs)]
  transfers between devices with their start and end apart: 8 -> 8, of which waited for: 4 -> 4; matrix products, arithmetic and copies ran while one was open for 0% -> 0% of each run, Pallas kernels for 5% -> 6%
where the time goes in v11:
time: 48.7 us; the launch traced here: 48.6 us
  blocking collectives  23.3 us (48%)
  waiting for transfers between devices  10.8 us (22%)
  starting transfers between devices  6.42 us (13%)
  Pallas kernels  5.41 us (11%)
  local copies, waits for them, and re-layouts  1.17 us (2%)
  between operations  0.8 us (2%)
  other arithmetic  0.67 us (1%)
    all_to_all x1, blocking collectives, timestep(): lax.all_to_all(half.reshape(chips, BLK_DEV, params), 'cells', 0, 0, tiled...  23.3 us
    ppermute x1, waiting for transfers between devices, timestep(): gradient = owned + lax.ppermute(owned, 'ens', [(0, 1), (1, 0)])  4.46 us
    ppermute x1, waiting for transfers between devices, timestep(): got_up = lax.ppermute(far, 'cells', up_pairs)  3.64 us
    ppermute x1, starting transfers between devices, timestep(): got_down2 = lax.ppermute(far_even, 'cells', down_pairs)  2.83 us
    pallas_call x1, Pallas kernels, timestep(): pl.pallas_call(select_kernel, out_shape=(jax.ShapeDtypeStruct((nblk, coun...  1.98 us
    pallas_call x1, Pallas kernels, timestep(): pl.pallas_call(make_end(ranks - 1, nblk), out_shape=(field, shaped(nblk /...  1.96 us
    ppermute x1, waiting for transfers between devices, timestep(): got_up2 = lax.ppermute(far_odd, 'cells', up_pairs)  1.83 us
    ppermute x1, starting transfers between devices, timestep(): got_down = lax.ppermute(far, 'cells', down_pairs)  1.61 us
  transfers between devices with their start and end apart: 8, of which 4 were waited for; matrix products, arithmetic and copies ran while one was open for 0% of the time, Pallas kernels for 6%

profile of v11, /device:TPU:16, one launch (start us, length us, event | category | flops | bytes accessed | tf_op | source)
XLA Modules:
  0.0 48.6 jit_solution(14416074024449669760)
XLA Ops:
  0.6 0.0 copy-start.2
  0.6 0.0 copy-start.1
  0.7 0.0 copy-start.4
  0.7 0.8 %copy-done.2 = bf16[2,4,4,2,8,128]{5,4,3,2,1,0:T(8,128)(2,1)S(1)} copy-done((bf16[2,4,4,2,8,128]{5,4,3,2,1,0:T(8,128)(2,1)S(1)}, bf16[2,4,4,2,8,128]{5,4,3,2,1,0:T(8,128)(2,1)}, u32[]{:S(2)}) %copy-start.2) | copy-done | bytes 131096
  1.5 0.3 copy-done.1
  1.8 0.0 copy-done.3
  1.9 0.5 %shard_map.87 = (f32[2,4,2,8,128]{4,3,2,1,0:T(8,128)S(1)}, f32[2,4,2,8,128]{4,3,2,1,0:T(8,128)S(1)}, f32[2,24,8,128]{3,2,1,0:T(8,128)S(1)}, f32[2,24,8,128]{3,2,1,0:T(8,128)S(1)}) custom-call(s32[1]{0:T(128)} %bitcast.pos.refs_0_, f32[8,128]{1,0:T(8,128)S(1)} %shard_map.86._, s32[1,256]{1,0:T(1,128)S(1)} %bitcast.3, f32[2,4,256]{2,1,0:T(4,128)S(1)} %copy-done.4, ...), custom_call_target="tpu_custom_call" | custom-call | tf_op jit(solution)/shard_map/pallas_call | solution.py:368
  2.4 0.1 collective-permute-start
  2.5 0.5 %collective-permute-start.2 = (f32[2,24,8,128]{3,2,1,0:T(8,128)S(1)}, f32[2,24,8,128]{3,2,1,0:T(8,128)S(1)}, u32[]{:S(2)}, u32[]{:S(2)}) collective-permute-start(f32[2,24,8,128]{3,2,1,0:T(8,128)S(1)} %get-tuple-element.20.refs_4_), channel_id=1, source_target_pairs={{0,2},{2,4},{4,0},{6,8},{8,6},{10,12},{12,14},{14,16},{16,10},{18,... | collective-permute-start | bytes 589832 | tf_op jit(solution)/shard_map/ppermute | solution.py:375
  3.0 1.6 %collective-permute-start.1 = (f32[2,24,8,128]{3,2,1,0:T(8,128)S(1)}, f32[2,24,8,128]{3,2,1,0:T(8,128)S(1)}, u32[]{:S(2)}, u32[]{:S(2)}) collective-permute-start(f32[2,24,8,128]{3,2,1,0:T(8,128)S(1)} %get-tuple-element.20.refs_4_), channel_id=1, source_target_pairs={{2,0},{4,2},{0,4},{8,6},{6,8},{12,10},{14,12},{16,14},{10,16},{20,... | collective-permute-start | bytes 589832 | tf_op jit(solution)/shard_map/ppermute | solution.py:376
  4.6 0.0 collective-permute-done.refs_5_.block_near
  4.6 3.6 %collective-permute-done.2.refs_6_.block_even = f32[2,24,8,128]{3,2,1,0:T(8,128)S(1)} collective-permute-done((f32[2,24,8,128]{3,2,1,0:T(8,128)S(1)}, f32[2,24,8,128]{3,2,1,0:T(8,128)S(1)}, u32[]{:S(2)}, u32[]{:S(2)}) %collective-permute-start.2) | collective-permute-done | bytes 196640 | tf_op jit(solution)/shard_map/ppermute | solution.py:375
  8.2 0.5 shard_map.88
  8.7 0.0 copy-start
  8.7 0.0 copy-start.5
  8.7 2.8 %collective-permute-start.5 = (f32[2,8,8,128]{3,2,1,0:T(8,128)S(1)}, f32[2,8,8,128]{3,2,1,0:T(8,128)S(1)}, u32[]{:S(2)}, u32[]{:S(2)}) collective-permute-start(f32[2,8,8,128]{3,2,1,0:T(8,128)S(1)} %get-tuple-element.25.sent_even), channel_id=1, source_target_pairs={{2,0},{4,2},{0,4},{8,6},{6,8},{12,10},{14,12},{16,14},{10,16},{20,... | collective-permute-start | bytes 196616 | tf_op jit(solution)/shard_map/ppermute | solution.py:397
  11.6 0.0 collective-permute-done.1.refs_6_.block_odd
  11.6 0.1 collective-permute-start.3
  11.7 0.5 %collective-permute-start.4 = (f32[2,8,8,128]{3,2,1,0:T(8,128)S(1)}, f32[2,8,8,128]{3,2,1,0:T(8,128)S(1)}, u32[]{:S(2)}, u32[]{:S(2)}) collective-permute-start(f32[2,8,8,128]{3,2,1,0:T(8,128)S(1)} %get-tuple-element.26.sent_odd), channel_id=1, source_target_pairs={{0,2},{2,4},{4,0},{6,8},{8,6},{10,12},{12,14},{14,16},{16,10},{18,... | collective-permute-start | bytes 196616 | tf_op jit(solution)/shard_map/ppermute | solution.py:406
  12.2 2.0 %shard_map.90 = (bf16[512,2048]{1,0:T(8,128)(2,1)S(1)}, f32[2,4,16,128,128]{4,3,2,1,0:T(8,128)S(1)}) custom-call(s32[1]{0:T(128)} %bitcast.pos.refs_0_, s32[2,8,128]{2,1,0:T(8,128)S(1)} %copy-done.5, bf16[2,4,2,8,128,128]{5,4,3,2,1,0:T(8,128)(2,1)S(1)} %copy-done), custom_call_target="tpu_custom_call" | custom-call | flops 16777216 | tf_op jit(solution)/shard_map/pallas_call | solution.py:378
  14.2 0.0 collective-permute-done.5.got_odd
  14.2 0.0 collective-permute-done.3.got_near
  14.2 1.8 %collective-permute-done.4.got_even = f32[2,8,8,128]{3,2,1,0:T(8,128)S(1)} collective-permute-done((f32[2,8,8,128]{3,2,1,0:T(8,128)S(1)}, f32[2,8,8,128]{3,2,1,0:T(8,128)S(1)}, u32[]{:S(2)}, u32[]{:S(2)}) %collective-permute-start.4) | collective-permute-done | bytes 65568 | tf_op jit(solution)/shard_map/ppermute | solution.py:406
  16.0 2.0 %shard_map.91 = (f32[2,4,2,8,128]{4,3,2,1,0:T(8,128)}, f32[256,128]{1,0:T(8,128)S(1)}, bf16[256,2048]{1,0:T(8,128)(2,1)S(1)}) custom-call(s32[1]{0:T(128)} %bitcast.pos.refs_0_, f32[2,4,2,8,128]{4,3,2,1,0:T(8,128)S(1)} %get-tuple-element.17.refs_1_.src, f32[2,4,2,8,128]{4,3,2,1,0:T(8,128)S(1)} %get-tuple-element.23.nxt, ...), custom_call_target="tpu_custom_call" | custom-call | tf_op jit(solution)/shard_map/pallas_call | solution.py:408
  18.0 0.1 collective-permute-start.6
  18.1 0.5 shard_map.92
  18.6 0.9 %collective-permute-done.6 = f32[256,128]{1,0:T(8,128)S(1)} collective-permute-done((f32[256,128]{1,0:T(8,128)S(1)}, f32[256,128]{1,0:T(8,128)S(1)}, u32[]{:S(2)}, u32[]{:S(2)}) %collective-permute-start.6) | collective-permute-done | bytes 131104 | tf_op jit(solution)/shard_map/ppermute | solution.py:422
  19.4 23.3 %all_to_all.5 = f32[64,4,128]{2,1,0:T(4,128)S(1)} all-to-all(f32[64,4,128]{2,1,0:T(4,128)S(1)} %bitcast.4), channel_id=1, replica_groups={{0,4,8,12,16,20,24,28,32,36,40,44,48,52,56,60,64,68,72,76,80,84,88,92,9..., dimensions={0} | all-to-all | bytes 262144 | tf_op jit(solution)/shard_map/all_to_all | solution.py:432
  42.7 0.1 reduce_sum.9
  42.8 0.7 %collective-permute-start.7 = (f32[4,128]{1,0:T(4,128)S(1)}, f32[4,128]{1,0:T(4,128)S(1)}, u32[]{:S(2)}, u32[]{:S(2)}) collective-permute-start(f32[4,128]{1,0:T(4,128)S(1)} %reduce_sum.9), channel_id=1, source_target_pairs={{0,1},{1,0},{2,3},{3,2},{4,5},{5,4},{6,7},{7,6},{8,9},{9,8},{10,11... | collective-permute-start | bytes 6152 | tf_op jit(solution)/shard_map/ppermute | solution.py:436
  43.5 4.5 %collective-permute-done.7 = f32[4,128]{1,0:T(4,128)S(1)} collective-permute-done((f32[4,128]{1,0:T(4,128)S(1)}, f32[4,128]{1,0:T(4,128)S(1)}, u32[]{:S(2)}, u32[]{:S(2)}) %collective-permute-start.7) | collective-permute-done | bytes 2080 | tf_op jit(solution)/shard_map/ppermute | solution.py:436
  48.0 0.6 %add.7 = f32[4,128]{1,0:T(4,128)} add(f32[4,128]{1,0:T(4,128)S(1)} %reduce_sum.9, f32[4,128]{1,0:T(4,128)S(1)} %collective-permute-done.7) | non-fusion elementwise | flops 512 | bytes 6144 | tf_op jit(solution)/shard_map/add | solution.py:436
  (9 shorter events, 0.0 us)
Async XLA Ops:
  0.6 0.9 %copy-start.2 = (bf16[2,4,4,2,8,128]{5,4,3,2,1,0:T(8,128)(2,1)S(1)}, bf16[2,4,4,2,8,128]{5,4,3,2,1,0:T(8,128)(2,1)}, u32[]{:S(2)}) copy-start(bf16[2,4,4,2,8,128]{5,4,3,2,1,0:T(8,128)(2,1)} %inv.3) | copy-start | bytes 393220
  0.6 1.2 %copy-start.1 = (bf16[2,6,4,4,2,8,128]{6,5,4,3,2,1,0:T(8,128)(2,1)S(1)}, bf16[2,6,4,4,2,8,128]{6,5,4,3,2,1,0:T(8,128)(2,1)}, u32[]{:S(2)}) copy-start(bf16[2,6,4,4,2,8,128]{6,5,4,3,2,1,0:T(8,128)(2,1)} %cpl.3) | copy-start | bytes 2359300
  0.7 1.2 %copy-start.4 = (f32[2,4,256]{2,1,0:T(4,128)S(1)}, f32[2,4,256]{2,1,0:T(4,128)}, u32[]{:S(2)}) copy-start(f32[2,4,256]{2,1,0:T(4,128)} %misfit.1) | copy-start | bytes 24580
  0.7 1.2 %copy-start.6 = (s32[256]{0:T(256)S(1)}, s32[256]{0:T(256)}, u32[]{:S(2)}) copy-start(s32[256]{0:T(256)} %param.11) | copy-start | bytes 3076
  0.7 1.2 %copy-start.3 = (f32[2,4,2,8,128]{4,3,2,1,0:T(8,128)S(1)}, f32[2,4,2,8,128]{4,3,2,1,0:T(8,128)}, u32[]{:S(2)}) copy-start(f32[2,4,2,8,128]{4,3,2,1,0:T(8,128)} %later.1) | copy-start | bytes 196612
  2.4 2.2 %collective-permute-start = (f32[2,24,8,128]{3,2,1,0:T(8,128)S(1)}, f32[2,24,8,128]{3,2,1,0:T(8,128)S(1)}, u32[]{:S(2)}, u32[]{:S(2)}) collective-permute-start(f32[2,24,8,128]{3,2,1,0:T(8,128)S(1)} %get-tuple-element.19.refs_3_), channel_id=1, source_target_pairs={{0,2},{2,0},{4,6},{6,4},{8,10},{10,8},{12,14},{14,12},{16,18},{18,... | collective-permute-start | bytes 589832 | tf_op jit(solution)/shard_map/ppermute | solution.py:377
  2.5 5.8 %collective-permute-start.2 = (f32[2,24,8,128]{3,2,1,0:T(8,128)S(1)}, f32[2,24,8,128]{3,2,1,0:T(8,128)S(1)}, u32[]{:S(2)}, u32[]{:S(2)}) collective-permute-start(f32[2,24,8,128]{3,2,1,0:T(8,128)S(1)} %get-tuple-element.20.refs_4_), channel_id=1, source_target_pairs={{0,2},{2,4},{4,0},{6,8},{8,6},{10,12},{12,14},{14,16},{16,10},{18,... | collective-permute-start | bytes 589832 | tf_op jit(solution)/shard_map/ppermute | solution.py:375
  3.0 8.6 %collective-permute-start.1 = (f32[2,24,8,128]{3,2,1,0:T(8,128)S(1)}, f32[2,24,8,128]{3,2,1,0:T(8,128)S(1)}, u32[]{:S(2)}, u32[]{:S(2)}) collective-permute-start(f32[2,24,8,128]{3,2,1,0:T(8,128)S(1)} %get-tuple-element.20.refs_4_), channel_id=1, source_target_pairs={{2,0},{4,2},{0,4},{8,6},{6,8},{12,10},{14,12},{16,14},{10,16},{20,... | collective-permute-start | bytes 589832 | tf_op jit(solution)/shard_map/ppermute | solution.py:376
  8.7 3.5 %copy-start = (bf16[2,4,2,8,128,128]{5,4,3,2,1,0:T(8,128)(2,1)S(1)}, bf16[2,4,2,8,128,128]{5,4,3,2,1,0:T(8,128)(2,1)}, u32[]{:S(2)}) copy-start(bf16[2,4,2,8,128,128]{5,4,3,2,1,0:T(8,128)(2,1)} %sens.1) | copy-start | bytes 12582916
  8.7 3.5 %copy-start.5 = (s32[2,8,128]{2,1,0:T(8,128)S(1)}, s32[2,8,128]{2,1,0:T(8,128)}, u32[]{:S(2)}) copy-start(s32[2,8,128]{2,1,0:T(8,128)} %bmap.1) | copy-start | bytes 24580
  8.7 5.5 %collective-permute-start.5 = (f32[2,8,8,128]{3,2,1,0:T(8,128)S(1)}, f32[2,8,8,128]{3,2,1,0:T(8,128)S(1)}, u32[]{:S(2)}, u32[]{:S(2)}) collective-permute-start(f32[2,8,8,128]{3,2,1,0:T(8,128)S(1)} %get-tuple-element.25.sent_even), channel_id=1, source_target_pairs={{2,0},{4,2},{0,4},{8,6},{6,8},{12,10},{14,12},{16,14},{10,16},{20,... | collective-permute-start | bytes 196616 | tf_op jit(solution)/shard_map/ppermute | solution.py:397
  11.6 2.6 %collective-permute-start.3 = (f32[2,8,8,128]{3,2,1,0:T(8,128)S(1)}, f32[2,8,8,128]{3,2,1,0:T(8,128)S(1)}, u32[]{:S(2)}, u32[]{:S(2)}) collective-permute-start(f32[2,8,8,128]{3,2,1,0:T(8,128)S(1)} %get-tuple-element.24.sent_near), channel_id=1, source_target_pairs={{0,2},{2,0},{4,6},{6,4},{8,10},{10,8},{12,14},{14,12},{16,18},{18,... | collective-permute-start | bytes 196616 | tf_op jit(solution)/shard_map/ppermute | solution.py:407
  11.7 4.3 %collective-permute-start.4 = (f32[2,8,8,128]{3,2,1,0:T(8,128)S(1)}, f32[2,8,8,128]{3,2,1,0:T(8,128)S(1)}, u32[]{:S(2)}, u32[]{:S(2)}) collective-permute-start(f32[2,8,8,128]{3,2,1,0:T(8,128)S(1)} %get-tuple-element.26.sent_odd), channel_id=1, source_target_pairs={{0,2},{2,4},{4,0},{6,8},{8,6},{10,12},{12,14},{14,16},{16,10},{18,... | collective-permute-start | bytes 196616 | tf_op jit(solution)/shard_map/ppermute | solution.py:406
  18.0 1.4 %collective-permute-start.6 = (f32[256,128]{1,0:T(8,128)S(1)}, f32[256,128]{1,0:T(8,128)S(1)}, u32[]{:S(2)}, u32[]{:S(2)}) collective-permute-start(f32[256,128]{1,0:T(8,128)S(1)} %get-tuple-element.31), channel_id=1, source_target_pairs={{0,2},{2,0},{4,6},{6,4},{8,10},{10,8},{12,14},{14,12},{16,18},{18,... | collective-permute-start | bytes 393224 | tf_op jit(solution)/shard_map/ppermute | solution.py:422
  42.8 5.2 %collective-permute-start.7 = (f32[4,128]{1,0:T(4,128)S(1)}, f32[4,128]{1,0:T(4,128)S(1)}, u32[]{:S(2)}, u32[]{:S(2)}) collective-permute-start(f32[4,128]{1,0:T(4,128)S(1)} %reduce_sum.9), channel_id=1, source_target_pairs={{0,1},{1,0},{2,3},{3,2},{4,5},{5,4},{6,7},{7,6},{8,9},{9,8},{10,11... | collective-permute-start | bytes 6152 | tf_op jit(solution)/shard_map/ppermute | solution.py:436

commit v12 on v9

--- a/solution.py
+++ b/solution.py
@@ -256,10 +256,22 @@
                 turned[m, u, g] = sens[m, u, g // rows, g % rows].astype(F32).T
 
 
+def block_sums(rows, grads, params):
+    both = lax.dot_general(rows, grads, (((1,), (1,)), ((), ())), preferred_element_type=F32)
+    return both[:, :params] + both[:, params:]
+
+
+def own_kernel(onehot, grads, adj, out, adj_out, sems):
+    store = pltpu.make_async_copy(adj, adj_out, sems.at[0])
+    store.start()
+    out[...] = block_sums(onehot[: out.shape[0]], grads[...], out.shape[1])
+    store.wait()
+
+
 def make_end(last, nblk):
     def end_kernel(
         pos, src, nxt, block_near, block_even, block_odd, sent_near, sent_even, sent_odd, got_near, got_even, got_odd,
-        cpl, inv, onehot, turned, adj_out, mine_out, other_out, adj, grads, sems,
+        cpl, inv, onehot, turned, adj, other_out, grads,
     ):
         members, unk, planes, rows, lanes = src.shape
         params = turned.shape[-2]
@@ -276,8 +288,6 @@
             )
             for u in range(unk):
                 adj[m, u] = a[u]
-        store = pltpu.make_async_copy(adj, adj_out, sems.at[0])
-        store.start()
         step = 32
         for g in range(groups):
             x, y = g // rows, g % rows
@@ -291,20 +301,13 @@
                 lo = (total - hi.astype(F32)).astype(BF16)
                 grads[p : p + step, g * lanes : (g + 1) * lanes] = hi
                 grads[params + p : params + p + step, g * lanes : (g + 1) * lanes] = lo
-        both = lax.dot_general(
-            onehot[...], grads[...], (((1,), (1,)), ((), ())), preferred_element_type=F32
-        )
-        out = both[:, :params] + both[:, params:]
-        mine_out[...] = out[:half_rows]
-        other_out[...] = out[half_rows:]
-        store.wait()
+        other_out[...] = block_sums(onehot[half_rows:], grads[...], params)
 
     return end_kernel
 
 
 VM = pl.BlockSpec(memory_space=pltpu.VMEM)
 SM = pl.BlockSpec(memory_space=pltpu.SMEM)
-HB = pl.BlockSpec(memory_space=pltpu.HBM)
 MIB = 1 << 20
 
 
@@ -335,7 +338,6 @@
     first_size = 2 * unk + unk * unk
     wells = well_cells.reshape(1, -1)
     cpl, inv = coupling, diag_inverse
-    dma = pltpu.SemaphoreType.DMA
     token = pl.pallas_call(
         first_kernel,
         out_shape=shaped(8, 128),
@@ -383,19 +385,29 @@
     )(pos, src, nxt, near, far, got_near, got_down, cpl, inv, nxt_even, near_even)
     got_up2 = lax.ppermute(far_odd, "cells", up_pairs)
     got_near2 = lax.ppermute(near2, "cells", intra_pairs)
-    adjoint, mine, other = pl.pallas_call(
+    adj, other, grads = pl.pallas_call(
         make_end(ranks - 1, nblk),
-        out_shape=(field, shaped(nblk // 2, params), shaped(nblk // 2, params)),
+        out_shape=(
+            field, shaped(nblk // 2, params), jax.ShapeDtypeStruct((2 * params, count), BF16)
+        ),
         in_specs=[SM] + [VM] * 15,
-        out_specs=(HB, VM, VM),
-        scratch_shapes=[pltpu.VMEM(field.shape, F32), pltpu.VMEM((2 * params, count), BF16), dma((1,))],
+        out_specs=(VM, VM, VM),
         compiler_params=room(16),
     )(
         pos, src, nxt2, got_near, got_up, got_down, near2, far_even, far_odd, got_near2, got_up2, got_down2,
         cpl, inv, onehot, turned,
     )
     chips = ranks // 2
-    half = mine + lax.ppermute(other, "cells", intra_pairs)
+    got_half = lax.ppermute(other, "cells", intra_pairs)
+    mine, adjoint = pl.pallas_call(
+        own_kernel,
+        out_shape=(shaped(nblk // 2, params), field),
+        in_specs=[VM, VM, VM],
+        out_specs=(VM, pl.BlockSpec(memory_space=pltpu.HBM)),
+        scratch_shapes=[pltpu.SemaphoreType.DMA((1,))],
+        compiler_params=room(6),
+    )(onehot, grads, adj)
+    half = mine + got_half
     same_core = [[core + 2 * chip for chip in range(chips)] for core in range(2)]
     parts = lax.all_to_all(
         half.reshape(chips, BLK_DEV, params), "cells", 0, 0, tiled=True, axis_index_groups=same_core

time: 49.1 us -> 48.6 us (0.990)
  waiting for transfers between devices: 14 us -> 13.4 us
    ppermute x1, waiting for transfers between devices: 1.33 us -> 0.69 us  [timestep(): got_half = lax.ppermute(other, 'cells', intra_pairs)]
    pallas_call x0 -> x1, Pallas kernels: none -> 0.64 us  [timestep(): pl.pallas_call(own_kernel, out_shape=(shaped(nblk // 2, params), field),...]
    pallas_call x1, Pallas kernels: 1.9 us -> 1.4 us  [timestep(): pl.pallas_call(make_end(ranks - 1, nblk), out_shape=(field, shaped(nblk /...]
  transfers between devices with their start and end apart: 8 -> 8, of which waited for: 4 -> 4; matrix products, arithmetic and copies ran while one was open for 0% -> 0% of each run, Pallas kernels for 5% -> 6%
where the time goes in v12:
time: 48.6 us; the launch traced here: 48.4 us
  blocking collectives  15.5 us (32%)
  waiting for transfers between devices  13.4 us (28%)
  starting transfers between devices  10.9 us (22%)
  Pallas kernels  5.05 us (10%)
  local copies, waits for them, and re-layouts  2.1 us (4%)
  between operations  0.81 us (2%)
  other arithmetic  0.67 us (1%)
    all_to_all x1, blocking collectives, timestep(): lax.all_to_all(half.reshape(chips, BLK_DEV, params), 'cells', 0, 0, tiled...  15.5 us
    ppermute x1, starting transfers between devices, timestep(): got_down = lax.ppermute(far, 'cells', down_pairs)  8.38 us
    ppermute x1, waiting for transfers between devices, timestep(): got_up2 = lax.ppermute(far_odd, 'cells', up_pairs)  4.87 us
    ppermute x1, waiting for transfers between devices, timestep(): gradient = owned + lax.ppermute(owned, 'ens', [(0, 1), (1, 0)])  4.46 us
    ppermute x1, waiting for transfers between devices, timestep(): got_up = lax.ppermute(far, 'cells', up_pairs)  3.35 us
    unnamed x14, local copies, waits for them, and re-layouts  2.1 us
    pallas_call x1, Pallas kernels, timestep(): pl.pallas_call(select_kernel, out_shape=(jax.ShapeDtypeStruct((nblk, coun...  1.98 us
    pallas_call x1, Pallas kernels, timestep(): pl.pallas_call(make_end(ranks - 1, nblk), out_shape=(field, shaped(nblk /...  1.4 us
  transfers between devices with their start and end apart: 8, of which 4 were waited for; matrix products, arithmetic and copies ran while one was open for 0% of the time, Pallas kernels for 6%

profile of v12, /device:TPU:16, one launch (start us, length us, event | category | flops | bytes accessed | tf_op | source)
XLA Modules:
  0.0 48.4 jit_solution(11995920066126385399)
XLA Ops:
  0.6 0.0 copy-start.2
  0.6 0.0 copy-start.1
  0.7 0.8 %copy-done.2 = bf16[2,4,4,2,8,128]{5,4,3,2,1,0:T(8,128)(2,1)S(1)} copy-done((bf16[2,4,4,2,8,128]{5,4,3,2,1,0:T(8,128)(2,1)S(1)}, bf16[2,4,4,2,8,128]{5,4,3,2,1,0:T(8,128)(2,1)}, u32[]{:S(2)}) %copy-start.2) | copy-done | bytes 131096
  1.5 0.3 copy-done.1
  1.8 0.0 copy-done.3
  1.9 0.5 %shard_map.88 = (f32[2,4,2,8,128]{4,3,2,1,0:T(8,128)S(1)}, f32[2,4,2,8,128]{4,3,2,1,0:T(8,128)S(1)}, f32[2,24,8,128]{3,2,1,0:T(8,128)S(1)}, f32[2,24,8,128]{3,2,1,0:T(8,128)S(1)}) custom-call(s32[1]{0:T(128)} %bitcast.pos.refs_0_, f32[8,128]{1,0:T(8,128)S(1)} %shard_map.87._, s32[1,256]{1,0:T(1,128)S(1)} %bitcast.3, f32[2,4,256]{2,1,0:T(4,128)S(1)} %copy-done.4, ...), custom_call_target="tpu_custom_call" | custom-call | tf_op jit(solution)/shard_map/pallas_call | solution.py:348
  2.4 0.1 collective-permute-start
  2.5 0.5 %collective-permute-start.2 = (f32[2,24,8,128]{3,2,1,0:T(8,128)S(1)}, f32[2,24,8,128]{3,2,1,0:T(8,128)S(1)}, u32[]{:S(2)}, u32[]{:S(2)}) collective-permute-start(f32[2,24,8,128]{3,2,1,0:T(8,128)S(1)} %get-tuple-element.23.refs_4_), channel_id=1, source_target_pairs={{0,2},{2,4},{4,6},{6,8},{8,10},{10,12},{12,14},{14,16},{16,18},{18... | collective-permute-start | bytes 589832 | tf_op jit(solution)/shard_map/ppermute | solution.py:355
  3.0 8.4 %collective-permute-start.1 = (f32[2,24,8,128]{3,2,1,0:T(8,128)S(1)}, f32[2,24,8,128]{3,2,1,0:T(8,128)S(1)}, u32[]{:S(2)}, u32[]{:S(2)}) collective-permute-start(f32[2,24,8,128]{3,2,1,0:T(8,128)S(1)} %get-tuple-element.23.refs_4_), channel_id=1, source_target_pairs={{2,0},{4,2},{6,4},{8,6},{10,8},{12,10},{14,12},{16,14},{18,16},{20... | collective-permute-start | bytes 589832 | tf_op jit(solution)/shard_map/ppermute | solution.py:356
  11.4 0.0 collective-permute-done.refs_5_.block_near
  11.4 3.3 %collective-permute-done.2.refs_6_.block_even = f32[2,24,8,128]{3,2,1,0:T(8,128)S(1)} collective-permute-done((f32[2,24,8,128]{3,2,1,0:T(8,128)S(1)}, f32[2,24,8,128]{3,2,1,0:T(8,128)S(1)}, u32[]{:S(2)}, u32[]{:S(2)}) %collective-permute-start.2) | collective-permute-done | bytes 196640 | tf_op jit(solution)/shard_map/ppermute | solution.py:355
  14.7 0.5 shard_map.89
  15.2 0.0 copy-start
  15.2 0.0 copy-start.5
  15.2 0.1 collective-permute-start.5
  15.3 0.0 collective-permute-done.1.refs_6_.block_odd
  15.3 1.0 %collective-permute-start.3 = (f32[2,8,8,128]{3,2,1,0:T(8,128)S(1)}, f32[2,8,8,128]{3,2,1,0:T(8,128)S(1)}, u32[]{:S(2)}, u32[]{:S(2)}) collective-permute-start(f32[2,8,8,128]{3,2,1,0:T(8,128)S(1)} %get-tuple-element.27.sent_near), channel_id=1, source_target_pairs={{0,2},{2,0},{4,6},{6,4},{8,10},{10,8},{12,14},{14,12},{16,18},{18,... | collective-permute-start | bytes 196616 | tf_op jit(solution)/shard_map/ppermute | solution.py:387
  16.3 0.1 collective-permute-start.4
  16.4 0.9 %copy-done = bf16[2,4,2,8,128,128]{5,4,3,2,1,0:T(8,128)(2,1)S(1)} copy-done((bf16[2,4,2,8,128,128]{5,4,3,2,1,0:T(8,128)(2,1)S(1)}, bf16[2,4,2,8,128,128]{5,4,3,2,1,0:T(8,128)(2,1)}, u32[]{:S(2)}) %copy-start) | copy-done | bytes 4194328
  17.4 2.0 %shard_map.86 = (bf16[512,2048]{1,0:T(8,128)(2,1)S(1)}, f32[2,4,16,128,128]{4,3,2,1,0:T(8,128)S(1)}) custom-call(s32[1]{0:T(128)} %bitcast.pos.refs_0_, s32[2,8,128]{2,1,0:T(8,128)S(1)} %copy-done.5, bf16[2,4,2,8,128,128]{5,4,3,2,1,0:T(8,128)(2,1)S(1)} %copy-done), custom_call_target="tpu_custom_call" | custom-call | flops 16777216 | tf_op jit(solution)/shard_map/pallas_call | solution.py:358
  19.4 0.0 collective-permute-done.5.got_odd
  19.4 0.0 collective-permute-done.3.got_near
  19.4 4.9 %collective-permute-done.4.got_even = f32[2,8,8,128]{3,2,1,0:T(8,128)S(1)} collective-permute-done((f32[2,8,8,128]{3,2,1,0:T(8,128)S(1)}, f32[2,8,8,128]{3,2,1,0:T(8,128)S(1)}, u32[]{:S(2)}, u32[]{:S(2)}) %collective-permute-start.4) | collective-permute-done | bytes 65568 | tf_op jit(solution)/shard_map/ppermute | solution.py:386
  24.3 1.4 %shard_map.91 = (f32[2,4,2,8,128]{4,3,2,1,0:T(8,128)S(1)}, f32[256,128]{1,0:T(8,128)S(1)}, bf16[256,2048]{1,0:T(8,128)(2,1)S(1)}) custom-call(s32[1]{0:T(128)} %bitcast.pos.refs_0_, f32[2,4,2,8,128]{4,3,2,1,0:T(8,128)S(1)} %get-tuple-element.20.refs_1_.src, f32[2,4,2,8,128]{4,3,2,1,0:T(8,128)S(1)} %get-tuple-element.26.nxt, ...), custom_call_target="tpu_custom_call" | custom-call | tf_op jit(solution)/shard_map/pallas_call | solution.py:388
  25.7 0.1 collective-permute-start.6
  25.8 0.6 %shard_map.92 = (f32[256,128]{1,0:T(8,128)S(1)}, f32[2,4,2,8,128]{4,3,2,1,0:T(8,128)}) custom-call(bf16[512,2048]{1,0:T(8,128)(2,1)S(1)} %get-tuple-element.19.onehot, bf16[256,2048]{1,0:T(8,128)(2,1)S(1)} %get-tuple-element.31.grads, f32[2,4,2,8,128]{4,3,2,1,0:T(8,128)S(1)} %get-tuple-element.32.adj), custom_call_target="tpu_custom_call" | custom-call | tf_op jit(solution)/shard_map/pallas_call | solution.py:402
  26.4 0.7 %collective-permute-done.6 = f32[256,128]{1,0:T(8,128)S(1)} collective-permute-done((f32[256,128]{1,0:T(8,128)S(1)}, f32[256,128]{1,0:T(8,128)S(1)}, u32[]{:S(2)}, u32[]{:S(2)}) %collective-permute-start.6) | collective-permute-done | bytes 131104 | tf_op jit(solution)/shard_map/ppermute | solution.py:401
  27.1 15.5 %all_to_all.5 = f32[64,4,128]{2,1,0:T(4,128)S(1)} all-to-all(f32[64,4,128]{2,1,0:T(4,128)S(1)} %bitcast.4), channel_id=1, replica_groups={{0,4,8,12,16,20,24,28,32,36,40,44,48,52,56,60,64,68,72,76,80,84,88,92,9..., dimensions={0} | all-to-all | bytes 262144 | tf_op jit(solution)/shard_map/all_to_all | solution.py:412
  42.6 0.1 reduce_sum.9
  42.7 0.7 %collective-permute-start.7 = (f32[4,128]{1,0:T(4,128)S(1)}, f32[4,128]{1,0:T(4,128)S(1)}, u32[]{:S(2)}, u32[]{:S(2)}) collective-permute-start(f32[4,128]{1,0:T(4,128)S(1)} %reduce_sum.9), channel_id=1, source_target_pairs={{0,1},{1,0},{2,3},{3,2},{4,5},{5,4},{6,7},{7,6},{8,9},{9,8},{10,11... | collective-permute-start | bytes 6152 | tf_op jit(solution)/shard_map/ppermute | solution.py:416
  43.4 4.5 %collective-permute-done.7 = f32[4,128]{1,0:T(4,128)S(1)} collective-permute-done((f32[4,128]{1,0:T(4,128)S(1)}, f32[4,128]{1,0:T(4,128)S(1)}, u32[]{:S(2)}, u32[]{:S(2)}) %collective-permute-start.7) | collective-permute-done | bytes 2080 | tf_op jit(solution)/shard_map/ppermute | solution.py:416
  47.9 0.6 %add.7 = f32[4,128]{1,0:T(4,128)} add(f32[4,128]{1,0:T(4,128)S(1)} %reduce_sum.9, f32[4,128]{1,0:T(4,128)S(1)} %collective-permute-done.7) | non-fusion elementwise | flops 512 | bytes 6144 | tf_op jit(solution)/shard_map/add | solution.py:416
  (9 shorter events, 0.1 us)
Async XLA Ops:
  0.6 0.9 %copy-start.2 = (bf16[2,4,4,2,8,128]{5,4,3,2,1,0:T(8,128)(2,1)S(1)}, bf16[2,4,4,2,8,128]{5,4,3,2,1,0:T(8,128)(2,1)}, u32[]{:S(2)}) copy-start(bf16[2,4,4,2,8,128]{5,4,3,2,1,0:T(8,128)(2,1)} %inv.3) | copy-start | bytes 393220
  0.6 1.2 %copy-start.1 = (bf16[2,6,4,4,2,8,128]{6,5,4,3,2,1,0:T(8,128)(2,1)S(1)}, bf16[2,6,4,4,2,8,128]{6,5,4,3,2,1,0:T(8,128)(2,1)}, u32[]{:S(2)}) copy-start(bf16[2,6,4,4,2,8,128]{6,5,4,3,2,1,0:T(8,128)(2,1)} %cpl.3) | copy-start | bytes 2359300
  0.7 1.2 %copy-start.4 = (f32[2,4,256]{2,1,0:T(4,128)S(1)}, f32[2,4,256]{2,1,0:T(4,128)}, u32[]{:S(2)}) copy-start(f32[2,4,256]{2,1,0:T(4,128)} %misfit.1) | copy-start | bytes 24580
  0.7 1.2 %copy-start.6 = (s32[256]{0:T(256)S(1)}, s32[256]{0:T(256)}, u32[]{:S(2)}) copy-start(s32[256]{0:T(256)} %param.11) | copy-start | bytes 3076
  0.7 1.2 %copy-start.3 = (f32[2,4,2,8,128]{4,3,2,1,0:T(8,128)S(1)}, f32[2,4,2,8,128]{4,3,2,1,0:T(8,128)}, u32[]{:S(2)}) copy-start(f32[2,4,2,8,128]{4,3,2,1,0:T(8,128)} %later.1) | copy-start | bytes 196612
  2.4 9.0 %collective-permute-start = (f32[2,24,8,128]{3,2,1,0:T(8,128)S(1)}, f32[2,24,8,128]{3,2,1,0:T(8,128)S(1)}, u32[]{:S(2)}, u32[]{:S(2)}) collective-permute-start(f32[2,24,8,128]{3,2,1,0:T(8,128)S(1)} %get-tuple-element.22.refs_3_), channel_id=1, source_target_pairs={{0,2},{2,0},{4,6},{6,4},{8,10},{10,8},{12,14},{14,12},{16,18},{18,... | collective-permute-start | bytes 589832 | tf_op jit(solution)/shard_map/ppermute | solution.py:357
  2.5 12.2 %collective-permute-start.2 = (f32[2,24,8,128]{3,2,1,0:T(8,128)S(1)}, f32[2,24,8,128]{3,2,1,0:T(8,128)S(1)}, u32[]{:S(2)}, u32[]{:S(2)}) collective-permute-start(f32[2,24,8,128]{3,2,1,0:T(8,128)S(1)} %get-tuple-element.23.refs_4_), channel_id=1, source_target_pairs={{0,2},{2,4},{4,6},{6,8},{8,10},{10,12},{12,14},{14,16},{16,18},{18... | collective-permute-start | bytes 589832 | tf_op jit(solution)/shard_map/ppermute | solution.py:355
  3.0 12.3 %collective-permute-start.1 = (f32[2,24,8,128]{3,2,1,0:T(8,128)S(1)}, f32[2,24,8,128]{3,2,1,0:T(8,128)S(1)}, u32[]{:S(2)}, u32[]{:S(2)}) collective-permute-start(f32[2,24,8,128]{3,2,1,0:T(8,128)S(1)} %get-tuple-element.23.refs_4_), channel_id=1, source_target_pairs={{2,0},{4,2},{6,4},{8,6},{10,8},{12,10},{14,12},{16,14},{18,16},{20... | collective-permute-start | bytes 589832 | tf_op jit(solution)/shard_map/ppermute | solution.py:356
  15.2 2.2 %copy-start = (bf16[2,4,2,8,128,128]{5,4,3,2,1,0:T(8,128)(2,1)S(1)}, bf16[2,4,2,8,128,128]{5,4,3,2,1,0:T(8,128)(2,1)}, u32[]{:S(2)}) copy-start(bf16[2,4,2,8,128,128]{5,4,3,2,1,0:T(8,128)(2,1)} %sens.1) | copy-start | bytes 12582916
  15.2 2.2 %copy-start.5 = (s32[2,8,128]{2,1,0:T(8,128)S(1)}, s32[2,8,128]{2,1,0:T(8,128)}, u32[]{:S(2)}) copy-start(s32[2,8,128]{2,1,0:T(8,128)} %bmap.1) | copy-start | bytes 24580
  15.2 4.2 %collective-permute-start.5 = (f32[2,8,8,128]{3,2,1,0:T(8,128)S(1)}, f32[2,8,8,128]{3,2,1,0:T(8,128)S(1)}, u32[]{:S(2)}, u32[]{:S(2)}) collective-permute-start(f32[2,8,8,128]{3,2,1,0:T(8,128)S(1)} %get-tuple-element.28.sent_even), channel_id=1, source_target_pairs={{2,0},{4,2},{6,4},{8,6},{10,8},{12,10},{14,12},{16,14},{18,16},{20... | collective-permute-start | bytes 196616 | tf_op jit(solution)/shard_map/ppermute | solution.py:377
  15.3 4.0 %collective-permute-start.3 = (f32[2,8,8,128]{3,2,1,0:T(8,128)S(1)}, f32[2,8,8,128]{3,2,1,0:T(8,128)S(1)}, u32[]{:S(2)}, u32[]{:S(2)}) collective-permute-start(f32[2,8,8,128]{3,2,1,0:T(8,128)S(1)} %get-tuple-element.27.sent_near), channel_id=1, source_target_pairs={{0,2},{2,0},{4,6},{6,4},{8,10},{10,8},{12,14},{14,12},{16,18},{18,... | collective-permute-start | bytes 196616 | tf_op jit(solution)/shard_map/ppermute | solution.py:387
  16.3 7.9 %collective-permute-start.4 = (f32[2,8,8,128]{3,2,1,0:T(8,128)S(1)}, f32[2,8,8,128]{3,2,1,0:T(8,128)S(1)}, u32[]{:S(2)}, u32[]{:S(2)}) collective-permute-start(f32[2,8,8,128]{3,2,1,0:T(8,128)S(1)} %get-tuple-element.29.sent_odd), channel_id=1, source_target_pairs={{0,2},{2,4},{4,6},{6,8},{8,10},{10,12},{12,14},{14,16},{16,18},{18... | collective-permute-start | bytes 196616 | tf_op jit(solution)/shard_map/ppermute | solution.py:386
  25.7 1.4 %collective-permute-start.6 = (f32[256,128]{1,0:T(8,128)S(1)}, f32[256,128]{1,0:T(8,128)S(1)}, u32[]{:S(2)}, u32[]{:S(2)}) collective-permute-start(f32[256,128]{1,0:T(8,128)S(1)} %get-tuple-element.35), channel_id=1, source_target_pairs={{0,2},{2,0},{4,6},{6,4},{8,10},{10,8},{12,14},{14,12},{16,18},{18,... | collective-permute-start | bytes 393224 | tf_op jit(solution)/shard_map/ppermute | solution.py:401
  42.7 5.2 %collective-permute-start.7 = (f32[4,128]{1,0:T(4,128)S(1)}, f32[4,128]{1,0:T(4,128)S(1)}, u32[]{:S(2)}, u32[]{:S(2)}) collective-permute-start(f32[4,128]{1,0:T(4,128)S(1)} %reduce_sum.9), channel_id=1, source_target_pairs={{0,1},{1,0},{2,3},{3,2},{4,5},{5,4},{6,7},{7,6},{8,9},{9,8},{10,11... | collective-permute-start | bytes 6152 | tf_op jit(solution)/shard_map/ppermute | solution.py:416
